TPU v7x, 128 devices: a whole 4x4x4 slice. The times are simulated.
128 devices in a mesh: dp: 4 (over x_hi, core), seq: 32 (over y, z, x_lo).
Axes of the slice: x: 4 (x_hi: 2, x_lo: 2; x = x_hi * 2 + x_lo), y: 4, z: 4, core: 2. Of those that a mesh axis runs over, the one named last changes fastest.
Arguments:
- queries: bfloat16 [4, 8192, 1024], P('dp', 'seq'), may hold values from -6 to 6
- keys: bfloat16 [4, 8192, 1024], P('dp', 'seq'), may hold values from -6 to 6
- values: bfloat16 [4, 8192, 1024], P('dp', 'seq'), may hold values from -6 to 6
- out_weight: bfloat16 [1024, 1024], replicated, may hold values from -0.1875 to 0.1875
- cotangent: bfloat16 [4, 8192, 1024], P('dp', 'seq'), may hold values from -6 to 6
Outputs:
- mixed: bfloat16 [4, 8192, 1024], P('dp', 'seq')
- grad_out_weight: float32 [1024, 1024], P(('dp', 'seq'))
- grad_queries: bfloat16 [4, 8192, 1024], P('dp', 'seq')
- grad_keys: bfloat16 [4, 8192, 1024], P('dp', 'seq')
- grad_values: bfloat16 [4, 8192, 1024], P('dp', 'seq')
All inputs are finite; a program needn't handle non-finite values.
Results may differ from a plain program's by a relative error of at most 0.02.
Values may be sent and summed in bfloat16 or wider, within the bound.
No kernel may reach another device: no remote copies, remote signals or barrier semaphores. Data moves between devices by JAX's collectives and lax.ppermute only.
A program may use at most 128 MiB of HBM per device.

v0:
```python
import math

import jax
import jax.numpy as jnp
from jax import lax
from jax.experimental import pallas as pl
from jax.experimental.pallas import tpu as pltpu
from jax.sharding import PartitionSpec as P

HEADS = 16
HEAD_DIM = 64
BLOCK = 64
TOKENS = 256
HIDDEN = 1024
PAIRS = HIDDEN // 128
LEVEL_ROWS = 8
MASKED = -1e30
F32 = jnp.float32
BF16 = jnp.bfloat16
SCALE = 1.0 / math.sqrt(HEAD_DIM)
ROOTS = (math.sqrt(64.0), math.sqrt(128.0), math.sqrt(256.0))


def mm(a, b, dims):
    return lax.dot_general(a, b, (dims, ((), ())), preferred_element_type=F32)


def iota(shape, dim):
    return lax.broadcasted_iota(jnp.int32, shape, dim)


def full(shape):
    return pl.BlockSpec(shape, lambda *_: (0,) * len(shape))


def pooled_levels(ref):
    one = [
        jnp.sum(ref[BLOCK * b : BLOCK * (b + 1), :].astype(F32), axis=0, keepdims=True)
        for b in range(4)
    ]
    two = [one[0] + one[1], one[2] + one[3]]
    three = [two[0] + two[1]]
    return [[x / root for x in rows] for rows, root in zip((one, two, three), ROOTS)]


def pool_kernel(q_ref, k_ref, v_ref, send_ref, cq_ref, first_ref, last_ref):
    me = lax.axis_index("seq")
    zero = jnp.zeros((1, HIDDEN), F32)
    q1, q2, q3 = pooled_levels(q_ref)
    cq_ref[...] = jnp.concatenate(q1 + q2 + q3 + [zero], axis=0).astype(BF16)
    k1, k2, k3 = pooled_levels(k_ref)
    v1, v2, v3 = pooled_levels(v_ref)
    slot1 = jnp.concatenate(k1 + v1, axis=0)
    slot2 = jnp.concatenate(k2 + [zero] * 2 + v2 + [zero] * 2, axis=0)
    slot3 = jnp.concatenate(k3 + [zero] * 3 + v3 + [zero] * 3, axis=0)
    for g in range(8):
        slot = jnp.where(me // 4 == g, slot1, jnp.where(me // 16 == g // 4, slot2, slot3))
        send_ref[32 * g : 32 * (g + 1), :] = jnp.concatenate([slot] * 4, axis=0).astype(BF16)
    first_ref[:BLOCK, :] = k_ref[:BLOCK, :]
    first_ref[BLOCK:, :] = v_ref[:BLOCK, :]
    last_ref[:BLOCK, :] = k_ref[TOKENS - BLOCK :, :]
    last_ref[BLOCK:, :] = v_ref[TOKENS - BLOCK :, :]


def pool(q, k, v):
    return pl.pallas_call(
        pool_kernel,
        out_shape=(
            jax.ShapeDtypeStruct((256, HIDDEN), BF16),
            jax.ShapeDtypeStruct((LEVEL_ROWS, HIDDEN), BF16),
            jax.ShapeDtypeStruct((2 * BLOCK, HIDDEN), BF16),
            jax.ShapeDtypeStruct((2 * BLOCK, HIDDEN), BF16),
        ),
        name="pool",
    )(q, k, v)


def window(own, left, right, half, row):
    if half == 0:
        return jnp.concatenate([left[row : row + BLOCK, :], own[: 3 * BLOCK, :]], axis=0)
    return jnp.concatenate([own[BLOCK:, :], right[row : row + BLOCK, :]], axis=0)


def band_bias(half, key_dim):
    me = lax.axis_index("seq")
    key_block = iota((256, 256), key_dim) // BLOCK
    query_block = iota((256, 256), 1 - key_dim) // BLOCK % 2
    gap = key_block - query_block
    keep = jnp.logical_and(gap >= 0, gap <= 2)
    if half == 0:
        keep = jnp.logical_and(keep, key_block >= jnp.where(me > 0, 0, 1))
    else:
        last = lax.axis_size("seq") - 1
        keep = jnp.logical_and(keep, key_block <= jnp.where(me < last, 3, 2))
    return jnp.where(keep, 0.0, MASKED).astype(F32)


def head_masks():
    lane = iota((1, 128), 1)
    low = jnp.where(lane < HEAD_DIM, 1.0, 0.0).astype(BF16)
    high = jnp.where(lane < HEAD_DIM, 0.0, 1.0).astype(BF16)
    return low, high


def two_heads(rows, masks):
    return jnp.concatenate([rows * masks[0], rows * masks[1]], axis=0)


def pick(stacked, low_lane):
    return jnp.where(low_lane, stacked[:128, :], stacked[128:, :])


def fine_forward_kernel(q_ref, k_ref, v_ref, left_ref, right_ref, n_ref, m_ref, l_ref, bias_ref):
    @pl.when(pl.program_id(0) == 0)
    def _():
        bias_ref[0] = band_bias(0, 1)
        bias_ref[1] = band_bias(1, 1)

    masks = head_masks()
    low_lane = iota((128, 128), 1) < HEAD_DIM
    ones = jnp.ones((256, 128), BF16)
    own_k, own_v = k_ref[...], v_ref[...]
    left, right = left_ref[...], right_ref[...]
    for half in range(2):
        rows = slice(128 * half, 128 * (half + 1))
        keys = window(own_k, left, right, half, 0)
        vals = window(own_v, left, right, half, BLOCK)
        query = two_heads(q_ref[rows, :], masks)
        scores = mm(query, keys, ((1,), (1,))) * SCALE + bias_ref[half]
        top = jnp.max(scores, axis=1, keepdims=True)
        weights = jnp.exp(scores - top).astype(BF16)
        both = mm(weights, jnp.concatenate([vals, ones], axis=1), ((1,), (0,)))
        n_ref[rows, :] = pick(both[:, :128], low_lane)
        l_ref[rows, :] = pick(both[:, 128:], low_lane)
        m_ref[rows, :] = pick(jnp.broadcast_to(top, (256, 128)), low_lane)


def pair_spec(rows):
    return pl.BlockSpec((rows, 128), lambda p: (0, p))


def fine_forward(q, k, v, left, right):
    tok = pair_spec(TOKENS)
    edge = pair_spec(2 * BLOCK)
    out = jax.ShapeDtypeStruct((TOKENS, HIDDEN), F32)
    return pl.pallas_call(
        fine_forward_kernel,
        grid=(PAIRS,),
        in_specs=[tok, tok, tok, edge, edge],
        out_specs=[tok, tok, tok],
        out_shape=(out, out, out),
        scratch_shapes=[pltpu.VMEM((2, 256, 256), F32)],
        cost_estimate=pl.CostEstimate(
            flops=3 * 16 * 2 * 256 * 256 * 128, transcendentals=16 * 256 * 256, bytes_accessed=6 << 20
        ),
        name="fine_forward",
    )(q, k, v, left, right)


def coarse_keep():
    me = lax.axis_index("seq")
    row = iota((128, 256), 0) % LEVEL_ROWS
    col = iota((128, 256), 1)
    dev = col // 8
    term = col % 8
    near = dev // 4 == me // 4
    mid = jnp.logical_and(dev // 16 == me // 16, jnp.logical_not(near))
    far = dev // 16 != me // 16
    apart = jnp.abs(4 * me + row - (4 * dev + term)) > 1
    one = jnp.logical_and(jnp.logical_and(row < 4, term < 4), jnp.logical_and(near, apart))
    two = jnp.logical_and(jnp.logical_and(row // 2 == 2, term < 2), mid)
    three = jnp.logical_and(jnp.logical_and(row == 6, term == 0), far)
    return jnp.logical_or(one, jnp.logical_or(two, three))


def by_head(rows, own):
    return jnp.concatenate([rows] * HEADS, axis=0) * own


def over_heads(stacked, own):
    return jnp.sum((stacked * own).reshape(HEADS, LEVEL_ROWS, HIDDEN), axis=0)


def join_kernel(
    cq_ref,
    kv_ref,
    n_ref,
    m_ref,
    l_ref,
    da_ref,
    att_ref,
    lse_ref,
    delta_ref,
    dq_ref,
    dkv_ref,
    mc_ref,
    lc_ref,
    nc_ref,
    g_ref,
    h_ref,
):
    own = jnp.where(
        iota((128, HIDDEN), 0) // LEVEL_ROWS == iota((128, HIDDEN), 1) // HEAD_DIM, 1.0, 0.0
    ).astype(F32)
    keep = coarse_keep()
    kv = kv_ref[...]
    query = by_head(cq_ref[...].astype(F32), own).astype(BF16)
    scores = jnp.where(keep, mm(query, kv, ((1,), (1,))) * SCALE, MASKED)
    top = jnp.max(scores, axis=1, keepdims=True)
    weights = jnp.where(keep, jnp.exp(scores - top), 0.0)
    total = jnp.sum(weights, axis=1, keepdims=True)
    on_values = pltpu.roll(weights, 4, 1).astype(BF16)
    nc_ref[...] = over_heads(mm(on_values, kv, ((1,), (0,))), own)
    mc_ref[...] = over_heads(jnp.broadcast_to(top, (128, HIDDEN)), own)
    lc_ref[...] = over_heads(jnp.broadcast_to(total, (128, HIDDEN)), own)
    same_head = jnp.where(
        iota((128, 128), 0) // HEAD_DIM == iota((128, 128), 1) // HEAD_DIM, 1.0, 0.0
    ).astype(BF16)
    for p in range(PAIRS):
        lanes = slice(128 * p, 128 * (p + 1))
        g_two, h_two, g_three, h_three = [], [], [], []
        g_one, h_one = [], []
        for b in range(4):
            rows = slice(BLOCK * b, BLOCK * (b + 1))
            level = (b, 4 + b // 2, 6)
            m0 = m_ref[rows, lanes]
            mc = [mc_ref[c : c + 1, lanes] for c in level]
            top_all = jnp.maximum(jnp.maximum(m0, mc[0]), jnp.maximum(mc[1], mc[2]))
            f0 = jnp.exp(m0 - top_all)
            fc = [jnp.exp(x - top_all) for x in mc]
            den = l_ref[rows, lanes] * f0
            num = n_ref[rows, lanes] * f0
            for c, f in zip(level, fc):
                den = den + lc_ref[c : c + 1, lanes] * f
                num = num + nc_ref[c : c + 1, lanes] * f
            inv = 1.0 / den
            att = (num * inv).astype(BF16)
            att_ref[rows, lanes] = att
            lse_ref[rows, lanes] = top_all + jnp.log(den)
            da = da_ref[rows, lanes].astype(F32)
            product = da * att.astype(F32)
            part = product.astype(BF16)
            rest = (product - part.astype(F32)).astype(BF16)
            delta = mm(part, same_head, ((1,), (0,))) + mm(rest, same_head, ((1,), (0,)))
            delta_ref[rows, lanes] = delta
            wc = [f * inv for f in fc]
            g = [jnp.sum(w * da, axis=0, keepdims=True) for w in wc]
            h = [jnp.sum(w * delta, axis=0, keepdims=True) for w in wc]
            g_one.append(g[0])
            h_one.append(h[0])
            g_two.append(g[1])
            h_two.append(h[1])
            g_three.append(g[2])
            h_three.append(h[2])
        zero = jnp.zeros((1, 128), F32)

        def rows_of(one, two, three):
            return jnp.concatenate(
                one
                + [two[0] + two[1], two[2] + two[3]]
                + [(three[0] + three[1]) + (three[2] + three[3]), zero],
                axis=0,
            )

        g_ref[:, lanes] = rows_of(g_one, g_two, g_three)
        h_ref[:, lanes] = rows_of(h_one, h_two, h_three)
    grads = by_head(g_ref[...], own).astype(BF16)
    sums = jnp.sum(by_head(h_ref[...], own), axis=1, keepdims=True) * (1.0 / HEAD_DIM)
    on_keys = pltpu.roll(mm(grads, kv, ((1,), (1,))), 252, 1)
    score_grad = weights * (on_keys - sums)
    row = iota((LEVEL_ROWS, 1), 0)
    share = jnp.where(row < 4, 1.0 / ROOTS[0], jnp.where(row < 6, 1.0 / ROOTS[1], 1.0 / ROOTS[2]))
    dq_ref[...] = over_heads(mm(score_grad.astype(BF16), kv, ((1,), (0,))), own) * (
        share.astype(F32) * SCALE
    )
    left = jnp.concatenate([(score_grad * SCALE).astype(BF16), on_values], axis=0)
    right = jnp.concatenate([query, grads], axis=0)
    dkv_ref[...] = mm(left, right, ((0,), (0,))).astype(BF16)


def join(cq, kv, n, m, l, da):
    f_out = jax.ShapeDtypeStruct((TOKENS, HIDDEN), F32)
    small = pltpu.VMEM((LEVEL_ROWS, HIDDEN), F32)
    return pl.pallas_call(
        join_kernel,
        out_shape=(
            jax.ShapeDtypeStruct((TOKENS, HIDDEN), BF16),
            f_out,
            f_out,
            jax.ShapeDtypeStruct((LEVEL_ROWS, HIDDEN), F32),
            jax.ShapeDtypeStruct((256, HIDDEN), BF16),
        ),
        scratch_shapes=[small] * 5,
        name="join",
    )(cq, kv, n, m, l, da)


def weight_kernel(att_ref, cot_ref, keep_ref, give_ref):
    core = lax.axis_index("dp") % 2
    cot = cot_ref[...]

    def half_rows(which):
        parts = []
        for hi in range(2):
            start = pl.multiple_of((2 * hi + which) * 256, 256)
            part = mm(att_ref[:, pl.ds(start, 256)], cot, ((0,), (0,)))
            parts.append(part.reshape(32, 8, HIDDEN))
        return jnp.concatenate(parts, axis=1).reshape(512, HIDDEN).astype(BF16)

    give_ref[...] = half_rows(1 - core)
    keep_ref[...] = half_rows(core)


def weight_terms(att, cot):
    out = jax.ShapeDtypeStruct((512, HIDDEN), BF16)
    return pl.pallas_call(
        weight_kernel,
        out_shape=(out, out),
        cost_estimate=pl.CostEstimate(
            flops=2 * 256 * 1024 * 1024, transcendentals=0, bytes_accessed=3 << 20
        ),
        name="weight_terms",
    )(att, cot)


def fine_backward_kernel(
    q_ref,
    k_ref,
    v_ref,
    left_ref,
    right_ref,
    da_ref,
    lse_ref,
    delta_ref,
    cdq_ref,
    gq_ref,
    dk_ref,
    dv_ref,
    to_left_ref,
    to_right_ref,
    bias_ref,
):
    @pl.when(pl.program_id(0) == 0)
    def _():
        bias_ref[0] = band_bias(0, 0)
        bias_ref[1] = band_bias(1, 0)

    masks = head_masks()
    low_lane = iota((128, 128), 1) < HEAD_DIM
    own_k, own_v = k_ref[...], v_ref[...]
    left, right = left_ref[...], right_ref[...]

    def stat_row(ref, rows):
        turned = ref[rows, :].T
        return jnp.concatenate([turned[:1, :], turned[HEAD_DIM : HEAD_DIM + 1, :]], axis=1)

    dks, dvs = [], []
    for half in range(2):
        rows = slice(128 * half, 128 * (half + 1))
        keys = window(own_k, left, right, half, 0)
        vals = window(own_v, left, right, half, BLOCK)
        query = two_heads(q_ref[rows, :], masks)
        grad = two_heads(da_ref[rows, :], masks)
        scores = mm(keys, query, ((1,), (1,))) * SCALE + bias_ref[half]
        prob = jnp.exp(scores - stat_row(lse_ref, rows))
        prob_grad = mm(vals, grad, ((1,), (1,)))
        score_grad = (prob * (prob_grad - stat_row(delta_ref, rows))).astype(BF16)
        dks.append(mm(score_grad, query, ((1,), (0,))) * SCALE)
        dvs.append(mm(prob.astype(BF16), grad, ((1,), (0,))))
        dq = pick(mm(score_grad, keys, ((0,), (0,))), low_lane) * SCALE
        for b in range(2):
            block = 2 * half + b
            coarse = (
                cdq_ref[block : block + 1, :]
                + cdq_ref[4 + half : 5 + half, :]
                + cdq_ref[6:7, :]
            )
            gq_ref[BLOCK * block : BLOCK * (block + 1), :] = (
                dq[BLOCK * b : BLOCK * (b + 1), :] + coarse
            ).astype(BF16)
    for first, ref, at in ((dks, dk_ref, 0), (dvs, dv_ref, BLOCK)):
        low, high = first
        to_left_ref[at : at + BLOCK, :] = low[:BLOCK, :].astype(BF16)
        ref[:BLOCK, :] = low[BLOCK : 2 * BLOCK, :]
        ref[BLOCK : 3 * BLOCK, :] = low[2 * BLOCK :, :] + high[: 2 * BLOCK, :]
        ref[3 * BLOCK :, :] = high[2 * BLOCK : 3 * BLOCK, :]
        to_right_ref[at : at + BLOCK, :] = high[3 * BLOCK :, :].astype(BF16)


def fine_backward(q, k, v, left, right, da, lse, delta, cdq):
    tok = pair_spec(TOKENS)
    edge = pair_spec(2 * BLOCK)
    f_out = jax.ShapeDtypeStruct((TOKENS, HIDDEN), F32)
    e_out = jax.ShapeDtypeStruct((2 * BLOCK, HIDDEN), BF16)
    return pl.pallas_call(
        fine_backward_kernel,
        grid=(PAIRS,),
        in_specs=[tok, tok, tok, edge, edge, tok, tok, tok, pair_spec(LEVEL_ROWS)],
        out_specs=[tok, tok, tok, edge, edge],
        out_shape=(jax.ShapeDtypeStruct((TOKENS, HIDDEN), BF16), f_out, f_out, e_out, e_out),
        scratch_shapes=[pltpu.VMEM((2, 256, 256), F32)],
        cost_estimate=pl.CostEstimate(
            flops=5 * 16 * 2 * 256 * 256 * 128, transcendentals=16 * 256 * 256, bytes_accessed=8 << 20
        ),
        name="fine_backward",
    )(q, k, v, left, right, da, lse, delta, cdq)


def finish_kernel(dk_ref, dv_ref, from_left_ref, from_right_ref, coarse_ref, gk_ref, gv_ref):
    me = lax.axis_index("seq")
    row = iota((16, 256), 0)
    col = iota((16, 256), 1)
    dev = col // 8
    level_row = row % 8
    term = col % 8 - 4 * (row // 8)
    near = dev // 4 == me // 4
    mid = jnp.logical_and(dev // 16 == me // 16, jnp.logical_not(near))
    far = dev // 16 != me // 16
    one = jnp.logical_and(jnp.logical_and(level_row < 4, term == level_row), near)
    two = jnp.logical_and(jnp.logical_and(level_row // 2 == 2, term == level_row - 4), mid)
    three = jnp.logical_and(jnp.logical_and(level_row == 6, term == 0), far)
    chosen = jnp.logical_or(one, jnp.logical_or(two, three))
    sums = mm(jnp.where(chosen, 1.0, 0.0).astype(BF16), coarse_ref[...], ((1,), (0,)))
    for at, own_ref, out_ref in ((0, dk_ref, gk_ref), (8, dv_ref, gv_ref)):
        side = BLOCK * (at // 8)
        for b in range(4):
            rows = slice(BLOCK * b, BLOCK * (b + 1))
            c1, c2, c3 = at + b, at + 4 + b // 2, at + 6
            coarse = (
                sums[c1 : c1 + 1, :] * (1.0 / ROOTS[0])
                + sums[c2 : c2 + 1, :] * (1.0 / ROOTS[1])
                + sums[c3 : c3 + 1, :] * (1.0 / ROOTS[2])
            )
            value = own_ref[rows, :] + coarse
            if b == 0:
                value = value + from_left_ref[side : side + BLOCK, :].astype(F32)
            if b == 3:
                value = value + from_right_ref[side : side + BLOCK, :].astype(F32)
            out_ref[rows, :] = value.astype(BF16)


def finish(dk, dv, from_left, from_right, coarse):
    out = jax.ShapeDtypeStruct((TOKENS, HIDDEN), BF16)
    return pl.pallas_call(finish_kernel, out_shape=(out, out), name="finish")(
        dk, dv, from_left, from_right, coarse
    )


def swap(x, axis, bit):
    return lax.ppermute(x, axis, [(i, i ^ bit) for i in range(lax.axis_size(axis))])


def to_next(x):
    n = lax.axis_size("seq")
    return lax.ppermute(x, "seq", [(i, i + 1) for i in range(n - 1)])


def to_previous(x):
    n = lax.axis_size("seq")
    return lax.ppermute(x, "seq", [(i + 1, i) for i in range(n - 1)])


def exchanged(x, rows):
    parts = x.reshape(32, rows, HIDDEN)
    return lax.all_to_all(parts, "seq", split_axis=0, concat_axis=0, tiled=True)


def on_device(queries, keys, values, out_weight, cotangent):
    q, k, v, cot = queries[0], keys[0], values[0], cotangent[0]
    send, cq, first, last = pool(q, k, v)
    coarse_kv = exchanged(send, 8).reshape(256, HIDDEN)
    left = to_next(last)
    right = to_previous(first)
    d_att = lax.dot_general(
        cot, out_weight, (((1,), (1,)), ((), ())), preferred_element_type=F32
    ).astype(BF16)
    n0, m0, l0 = fine_forward(q, k, v, left, right)
    att, lse, delta, cdq, dkv = join(cq, coarse_kv, n0, m0, l0, d_att)
    kept, given = weight_terms(att, cot)
    got = swap(given, "dp", 1)
    back = exchanged(dkv, 8).reshape(256, HIDDEN)
    gq, dk, dv, to_left, to_right = fine_backward(q, k, v, left, right, d_att, lse, delta, cdq)
    from_left = to_next(to_right)
    from_right = to_previous(to_left)
    mixed = jnp.dot(att, out_weight, preferred_element_type=F32).astype(BF16)
    chip = (kept.astype(F32) + got.astype(F32)).astype(BF16)
    rows = exchanged(chip, 16).astype(F32).sum(axis=0)
    high = lax.axis_index("dp") // 2 == 1
    mine = jnp.where(high, rows[8:], rows[:8])
    other = jnp.where(high, rows[:8], rows[8:]).astype(BF16)
    grad_weight = mine + swap(other, "dp", 2).astype(F32)
    gk, gv = finish(dk, dv, from_left, from_right, back)
    return (mixed[None], grad_weight, gq[None], gk[None], gv[None])


def solution(mesh):
    tokens = P("dp", "seq", None)
    return jax.shard_map(
        on_device,
        mesh=mesh,
        in_specs=(tokens, tokens, tokens, P(), tokens),
        out_specs=(tokens, P(("dp", "seq"), None), tokens, tokens, tokens),
        check_vma=False,
    )
```

profile of v0, /device:TPU:0, one launch (start us, length us, event | category | flops | bytes accessed | tf_op | source)
XLA Modules:
  0.0 103.4 jit_solution(11760002211693173363)
XLA Ops:
  0.6 0.0 copy-start
  0.6 0.0 copy-start.3
  0.7 2.8 %pool.1 = (bf16[256,1024]{1,0:T(8,128)(2,1)}, bf16[8,1024]{1,0:T(8,128)(2,1)}, bf16[128,1024]{1,0:T(8,128)(2,1)}, bf16[128,1024]{1,0:T(8,128)(2,1)}) custom-call(bf16[256,1024]{1,0:T(8,128)(2,1)} %bitcast.20, bf16[256,1024]{1,0:T(8,128)(2,1)} %bitcast.23, bf16[256,1024]{1,0:T(8,128)(2,1)} %bitcast.26), custom_call_target="tpu_custom_call" | custom-call | tf_op jit(solution)/shard_map/pool/pallas_call | solution.py:66
  3.4 9.4 %all-to-all-start = ((bf16[32,8,1024]{2,1,0:T(8,128)(2,1)}), bf16[32,8,1024]{2,1,0:T(8,128)(2,1)S(1)}, u32[]{:S(2)}, u32[]{:S(2)}) async-start(bf16[32,8,1024]{2,1,0:T(8,128)(2,1)} %bitcast.30), calls=%async_computation | async-start | bytes 1048576 | tf_op jit(solution)/shard_map/all_to_all | solution.py:465
  12.8 3.7 %collective-permute-start = (bf16[128,1024]{1,0:T(8,128)(2,1)}, bf16[128,1024]{1,0:T(8,128)(2,1)S(1)}, u32[]{:S(2)}, u32[]{:S(2)}) collective-permute-start(bf16[128,1024]{1,0:T(8,128)(2,1)} %get-tuple-element.28), channel_id=1, source_target_pairs={{0,1},{1,2},{2,3},{3,4},{4,5},{5,6},{6,7},{7,8},{8,9},{9,10},{10,1... | collective-permute-start | bytes 786440 | tf_op jit(solution)/shard_map/ppermute | solution.py:455
  16.5 1.3 %collective-permute-start.1 = (bf16[128,1024]{1,0:T(8,128)(2,1)}, bf16[128,1024]{1,0:T(8,128)(2,1)}, u32[]{:S(2)}, u32[]{:S(2)}) collective-permute-start(bf16[128,1024]{1,0:T(8,128)(2,1)} %get-tuple-element.29), channel_id=1, source_target_pairs={{1,0},{2,1},{3,2},{4,3},{5,4},{6,5},{7,6},{8,7},{9,8},{10,9},{11,1... | collective-permute-start | bytes 786440 | tf_op jit(solution)/shard_map/ppermute | solution.py:460
  17.8 0.0 copy-done
  17.8 0.0 copy-done.3
  17.9 1.5 %convolution_convert_fusion.1.da_ref = bf16[256,1024]{1,0:T(8,128)(2,1)} fusion(bf16[1024,1024]{1,0:T(8,128)(2,1)S(1)} %copy-done, bf16[1,256,1024]{2,1,0:T(8,128)(2,1)S(1)} %copy-done.3), kind=kOutput, calls=%fused_computation.3 | convolution fusion | flops 537133056 | bytes 3145728 | tf_op jit(solution)/shard_map/dot_general | solution.py:474
  19.4 4.7 %collective-permute-done.left_ref = bf16[128,1024]{1,0:T(8,128)(2,1)S(1)} collective-permute-done((bf16[128,1024]{1,0:T(8,128)(2,1)}, bf16[128,1024]{1,0:T(8,128)(2,1)S(1)}, u32[]{:S(2)}, u32[]{:S(2)}) %collective-permute-start) | collective-permute-done | bytes 262176 | tf_op jit(solution)/shard_map/ppermute | solution.py:455
  24.1 0.0 copy-start.4
  24.1 8.0 %collective-permute-done.1.right_ref = bf16[128,1024]{1,0:T(8,128)(2,1)} collective-permute-done((bf16[128,1024]{1,0:T(8,128)(2,1)}, bf16[128,1024]{1,0:T(8,128)(2,1)}, u32[]{:S(2)}, u32[]{:S(2)}) %collective-permute-start.1) | collective-permute-done | bytes 262176 | tf_op jit(solution)/shard_map/ppermute | solution.py:460
  32.1 0.0 copy-done.4
  32.1 7.5 %fine_forward.1 = (f32[256,1024]{1,0:T(8,128)}, f32[256,1024]{1,0:T(8,128)}, f32[256,1024]{1,0:T(8,128)}) custom-call(bf16[256,1024]{1,0:T(8,128)(2,1)} %bitcast.21, bf16[256,1024]{1,0:T(8,128)(2,1)} %bitcast.24, bf16[256,1024]{1,0:T(8,128)(2,1)} %bitcast.27, bf16[128,1024]{1,0:T(8,128)(2,1)} %copy-done.4, bf16[128,1024]{1,0:T(8,128)(2,1)} %collective-permute-done.1.right_ref), custom_call_target="tpu_custom_call" | custom-call | flops 805306368 | bytes 6291456 | tf_op jit(solution)/shard_map/fine_forward/pallas_call | solution.py:146
  39.6 0.0 all-to-all-done
  39.6 0.0 copy-start.1
  39.6 0.8 copy-done.1
  40.4 6.7 %join.1 = (bf16[256,1024]{1,0:T(8,128)(2,1)}, f32[256,1024]{1,0:T(8,128)}, f32[256,1024]{1,0:T(8,128)}, f32[8,1024]{1,0:T(8,128)}, bf16[256,1024]{1,0:T(8,128)(2,1)}) custom-call(bf16[8,1024]{1,0:T(8,128)(2,1)} %get-tuple-element.26.cq_ref, bf16[256,1024]{1,0:T(8,128)(2,1)} %bitcast.19, f32[256,1024]{1,0:T(8,128)} %get-tuple-element.30.n_ref, ...), custom_call_target="tpu_custom_call" | custom-call | tf_op jit(solution)/shard_map/join/pallas_call | solution.py:284
  47.1 3.0 %weight_terms.1 = (bf16[512,1024]{1,0:T(8,128)(2,1)}, bf16[512,1024]{1,0:T(8,128)(2,1)}) custom-call(bf16[256,1024]{1,0:T(8,128)(2,1)} %get-tuple-element.33.att_ref, bf16[256,1024]{1,0:T(8,128)(2,1)} %bitcast.31), custom_call_target="tpu_custom_call" | custom-call | flops 536870912 | bytes 3145728 | tf_op jit(solution)/shard_map/weight_terms/pallas_call | solution.py:316
  50.1 0.0 collective-permute-start.2
  50.1 2.9 %collective-permute-done.2 = bf16[512,1024]{1,0:T(8,128)(2,1)S(1)} collective-permute-done((bf16[512,1024]{1,0:T(8,128)(2,1)}, bf16[512,1024]{1,0:T(8,128)(2,1)S(1)}, u32[]{:S(2)}, u32[]{:S(2)}) %collective-permute-start.2) | collective-permute-done | bytes 1048608 | tf_op jit(solution)/shard_map/ppermute | solution.py:450
  53.0 2.6 %add_convert_fusion = bf16[512,1024]{1,0:T(8,128)(2,1)} fusion(bf16[512,1024]{1,0:T(8,128)(2,1)S(1)} %collective-permute-done.2, bf16[512,1024]{1,0:T(8,128)(2,1)} %get-tuple-element.34), kind=kLoop, calls=%fused_computation.1 | loop fusion | flops 2097152 | bytes 3145728 | tf_op jit(solution)/shard_map/convert_element_type | solution.py:486
  55.6 7.4 %all-to-all-start.1 = ((bf16[32,16,1024]{2,1,0:T(8,128)(2,1)}), bf16[32,16,1024]{2,1,0:T(8,128)(2,1)S(1)}, u32[]{:S(2)}, u32[]{:S(2)}) async-start(bf16[32,16,1024]{2,1,0:T(8,128)(2,1)} %bitcast.7), calls=%async_computation.1 | async-start | bytes 2097152 | tf_op jit(solution)/shard_map/all_to_all | solution.py:465
  63.0 9.5 %fine_backward.1 = (bf16[256,1024]{1,0:T(8,128)(2,1)}, f32[256,1024]{1,0:T(8,128)}, f32[256,1024]{1,0:T(8,128)}, bf16[128,1024]{1,0:T(8,128)(2,1)}, bf16[128,1024]{1,0:T(8,128)(2,1)}) custom-call(bf16[256,1024]{1,0:T(8,128)(2,1)} %bitcast.22, bf16[256,1024]{1,0:T(8,128)(2,1)} %bitcast.25, bf16[256,1024]{1,0:T(8,128)(2,1)} %bitcast.28, ...), custom_call_target="tpu_custom_call" | custom-call | flops 1342177280 | bytes 8388608 | tf_op jit(solution)/shard_map/fine_backward/pallas_call | solution.py:395
  72.5 3.7 %collective-permute-start.4 = (bf16[128,1024]{1,0:T(8,128)(2,1)}, bf16[128,1024]{1,0:T(8,128)(2,1)S(1)}, u32[]{:S(2)}, u32[]{:S(2)}) collective-permute-start(bf16[128,1024]{1,0:T(8,128)(2,1)} %get-tuple-element.42), channel_id=1, source_target_pairs={{0,1},{1,2},{2,3},{3,4},{4,5},{5,6},{6,7},{7,8},{8,9},{9,10},{10,1... | collective-permute-start | bytes 786440 | tf_op jit(solution)/shard_map/ppermute | solution.py:455
  76.3 1.3 %collective-permute-start.5 = (bf16[128,1024]{1,0:T(8,128)(2,1)}, bf16[128,1024]{1,0:T(8,128)(2,1)}, u32[]{:S(2)}, u32[]{:S(2)}) collective-permute-start(bf16[128,1024]{1,0:T(8,128)(2,1)} %get-tuple-element.43), channel_id=1, source_target_pairs={{1,0},{2,1},{3,2},{4,3},{5,4},{6,5},{7,6},{8,7},{9,8},{10,9},{11,1... | collective-permute-start | bytes 786440 | tf_op jit(solution)/shard_map/ppermute | solution.py:460
  77.6 4.0 %all-to-all-done.1 = bf16[32,16,1024]{2,1,0:T(8,128)(2,1)S(1)} async-done(((bf16[32,16,1024]{2,1,0:T(8,128)(2,1)}), bf16[32,16,1024]{2,1,0:T(8,128)(2,1)S(1)}, u32[]{:S(2)}, u32[]{:S(2)}) %all-to-all-start.1) | async-done | bytes 1048608 | tf_op jit(solution)/shard_map/all_to_all | solution.py:465
  81.5 5.5 %all-to-all-start.2 = ((bf16[32,8,1024]{2,1,0:T(8,128)(2,1)}), bf16[32,8,1024]{2,1,0:T(8,128)(2,1)}, u32[]{:S(2)}, u32[]{:S(2)}) async-start(bf16[32,8,1024]{2,1,0:T(8,128)(2,1)} %bitcast.29), calls=%async_computation.2 | async-start | bytes 1048576 | tf_op jit(solution)/shard_map/all_to_all | solution.py:465
  87.0 0.2 convert_reduce_fusion
  87.2 2.8 %collective-permute-start.3 = (bf16[8,1024]{1,0:T(8,128)(2,1)S(1)}, bf16[8,1024]{1,0:T(8,128)(2,1)S(1)}, u32[]{:S(2)}, u32[]{:S(2)}) collective-permute-start(bf16[8,1024]{1,0:T(8,128)(2,1)S(1)} %select_convert_fusion), channel_id=1, source_target_pairs={{0,64},{32,96},{64,0},{96,32},{1,65},{33,97},{65,1},{97,33},{2,66}... | collective-permute-start | bytes 49160 | tf_op jit(solution)/shard_map/ppermute | solution.py:450
  90.0 2.5 %fusion = bf16[1,256,1024]{2,1,0:T(8,128)(2,1)} fusion(bf16[256,1024]{1,0:T(8,128)(2,1)} %get-tuple-element.33.att_ref, bf16[1024,1024]{1,0:T(8,128)(2,1)S(1)} %copy-done), kind=kOutput, calls=%fused_computation.4 | convolution fusion | flops 537133056 | bytes 3145728 | tf_op jit(solution)/shard_map/dot_general | solution.py:485
  92.6 0.0 collective-permute-done.4.from_left_ref
  92.6 0.0 copy-start.2
  92.6 0.0 collective-permute-done.5.from_right_ref
  92.6 7.0 %all-to-all-done.2 = bf16[32,8,1024]{2,1,0:T(8,128)(2,1)} async-done(((bf16[32,8,1024]{2,1,0:T(8,128)(2,1)}), bf16[32,8,1024]{2,1,0:T(8,128)(2,1)}, u32[]{:S(2)}, u32[]{:S(2)}) %all-to-all-start.2) | async-done | bytes 524320 | tf_op jit(solution)/shard_map/all_to_all | solution.py:465
  99.6 0.0 copy-done.2
  99.6 3.2 %finish.1 = (bf16[256,1024]{1,0:T(8,128)(2,1)}, bf16[256,1024]{1,0:T(8,128)(2,1)}) custom-call(f32[256,1024]{1,0:T(8,128)} %get-tuple-element.40.dk_ref, f32[256,1024]{1,0:T(8,128)} %get-tuple-element.41.dv_ref, bf16[128,1024]{1,0:T(8,128)(2,1)} %copy-done.2, bf16[128,1024]{1,0:T(8,128)(2,1)} %collective-permute-done.5.from_right_ref, ...), custom_call_target="tpu_custom_call" | custom-call | tf_op jit(solution)/shard_map/finish/pallas_call | solution.py:444
  102.7 0.0 collective-permute-done.3
  102.7 0.6 convert_add_fusion
  (1 shorter events, 0.0 us)
Async XLA Ops:
  0.6 17.2 %copy-start = (bf16[1024,1024]{1,0:T(8,128)(2,1)S(1)}, bf16[1024,1024]{1,0:T(8,128)(2,1)}, u32[]{:S(2)}) copy-start(bf16[1024,1024]{1,0:T(8,128)(2,1)} %param.8) | copy-start | bytes 6291460
  0.6 17.2 %copy-start.3 = (bf16[1,256,1024]{2,1,0:T(8,128)(2,1)S(1)}, bf16[1,256,1024]{2,1,0:T(8,128)(2,1)}, u32[]{:S(2)}) copy-start(bf16[1,256,1024]{2,1,0:T(8,128)(2,1)} %param.9) | copy-start | bytes 1572868
  3.4 36.2 %all-to-all-start = ((bf16[32,8,1024]{2,1,0:T(8,128)(2,1)}), bf16[32,8,1024]{2,1,0:T(8,128)(2,1)S(1)}, u32[]{:S(2)}, u32[]{:S(2)}) async-start(bf16[32,8,1024]{2,1,0:T(8,128)(2,1)} %bitcast.30), calls=%async_computation | async-start | bytes 1048576 | tf_op jit(solution)/shard_map/all_to_all | solution.py:465
  12.8 11.3 %collective-permute-start = (bf16[128,1024]{1,0:T(8,128)(2,1)}, bf16[128,1024]{1,0:T(8,128)(2,1)S(1)}, u32[]{:S(2)}, u32[]{:S(2)}) collective-permute-start(bf16[128,1024]{1,0:T(8,128)(2,1)} %get-tuple-element.28), channel_id=1, source_target_pairs={{0,1},{1,2},{2,3},{3,4},{4,5},{5,6},{6,7},{7,8},{8,9},{9,10},{10,1... | collective-permute-start | bytes 786440 | tf_op jit(solution)/shard_map/ppermute | solution.py:455
  16.5 15.6 %collective-permute-start.1 = (bf16[128,1024]{1,0:T(8,128)(2,1)}, bf16[128,1024]{1,0:T(8,128)(2,1)}, u32[]{:S(2)}, u32[]{:S(2)}) collective-permute-start(bf16[128,1024]{1,0:T(8,128)(2,1)} %get-tuple-element.29), channel_id=1, source_target_pairs={{1,0},{2,1},{3,2},{4,3},{5,4},{6,5},{7,6},{8,7},{9,8},{10,9},{11,1... | collective-permute-start | bytes 786440 | tf_op jit(solution)/shard_map/ppermute | solution.py:460
  24.1 8.0 %copy-start.4 = (bf16[128,1024]{1,0:T(8,128)(2,1)}, bf16[128,1024]{1,0:T(8,128)(2,1)S(1)}, u32[]{:S(2)}) copy-start(bf16[128,1024]{1,0:T(8,128)(2,1)S(1)} %collective-permute-done.left_ref) | copy-start | bytes 786436
  39.6 0.8 copy-start.1
  50.1 2.9 %collective-permute-start.2 = (bf16[512,1024]{1,0:T(8,128)(2,1)}, bf16[512,1024]{1,0:T(8,128)(2,1)S(1)}, u32[]{:S(2)}, u32[]{:S(2)}) collective-permute-start(bf16[512,1024]{1,0:T(8,128)(2,1)} %get-tuple-element.35), channel_id=1, source_target_pairs={{0,32},{32,0},{64,96},{96,64},{1,33},{33,1},{65,97},{97,65},{2,34}... | collective-permute-start | bytes 3145736 | tf_op jit(solution)/shard_map/ppermute | solution.py:450
  55.6 25.9 %all-to-all-start.1 = ((bf16[32,16,1024]{2,1,0:T(8,128)(2,1)}), bf16[32,16,1024]{2,1,0:T(8,128)(2,1)S(1)}, u32[]{:S(2)}, u32[]{:S(2)}) async-start(bf16[32,16,1024]{2,1,0:T(8,128)(2,1)} %bitcast.7), calls=%async_computation.1 | async-start | bytes 2097152 | tf_op jit(solution)/shard_map/all_to_all | solution.py:465
  72.5 20.0 %collective-permute-start.4 = (bf16[128,1024]{1,0:T(8,128)(2,1)}, bf16[128,1024]{1,0:T(8,128)(2,1)S(1)}, u32[]{:S(2)}, u32[]{:S(2)}) collective-permute-start(bf16[128,1024]{1,0:T(8,128)(2,1)} %get-tuple-element.42), channel_id=1, source_target_pairs={{0,1},{1,2},{2,3},{3,4},{4,5},{5,6},{6,7},{7,8},{8,9},{9,10},{10,1... | collective-permute-start | bytes 786440 | tf_op jit(solution)/shard_map/ppermute | solution.py:455
  76.3 16.3 %collective-permute-start.5 = (bf16[128,1024]{1,0:T(8,128)(2,1)}, bf16[128,1024]{1,0:T(8,128)(2,1)}, u32[]{:S(2)}, u32[]{:S(2)}) collective-permute-start(bf16[128,1024]{1,0:T(8,128)(2,1)} %get-tuple-element.43), channel_id=1, source_target_pairs={{1,0},{2,1},{3,2},{4,3},{5,4},{6,5},{7,6},{8,7},{9,8},{10,9},{11,1... | collective-permute-start | bytes 786440 | tf_op jit(solution)/shard_map/ppermute | solution.py:460
  81.5 18.0 %all-to-all-start.2 = ((bf16[32,8,1024]{2,1,0:T(8,128)(2,1)}), bf16[32,8,1024]{2,1,0:T(8,128)(2,1)}, u32[]{:S(2)}, u32[]{:S(2)}) async-start(bf16[32,8,1024]{2,1,0:T(8,128)(2,1)} %bitcast.29), calls=%async_computation.2 | async-start | bytes 1048576 | tf_op jit(solution)/shard_map/all_to_all | solution.py:465
  87.2 15.5 %collective-permute-start.3 = (bf16[8,1024]{1,0:T(8,128)(2,1)S(1)}, bf16[8,1024]{1,0:T(8,128)(2,1)S(1)}, u32[]{:S(2)}, u32[]{:S(2)}) collective-permute-start(bf16[8,1024]{1,0:T(8,128)(2,1)S(1)} %select_convert_fusion), channel_id=1, source_target_pairs={{0,64},{32,96},{64,0},{96,32},{1,65},{33,97},{65,1},{97,33},{2,66}... | collective-permute-start | bytes 49160 | tf_op jit(solution)/shard_map/ppermute | solution.py:450
  92.6 7.0 %copy-start.2 = (bf16[128,1024]{1,0:T(8,128)(2,1)}, bf16[128,1024]{1,0:T(8,128)(2,1)S(1)}, u32[]{:S(2)}) copy-start(bf16[128,1024]{1,0:T(8,128)(2,1)S(1)} %collective-permute-done.4.from_left_ref) | copy-start | bytes 786436
where the time goes:
time: 105 us; the launch traced here: 103 us
  starting transfers between devices  35.1 us (33%)
  Pallas kernels  32.7 us (31%)
  waiting for transfers between devices  26.5 us (25%)
  matrix products  4.08 us (4%)
  other arithmetic  3.39 us (3%)
    all_to_all x3, starting transfers between devices, exchanged(): return lax.all_to_all(parts, 'seq', split_axis=0, concat_axis=0, tiled=True)  22.3 us
    all_to_all x3, waiting for transfers between devices, exchanged(): return lax.all_to_all(parts, 'seq', split_axis=0, concat_axis=0, tiled=True)  10.9 us
    pallas_call x1, Pallas kernels, fine_backward(): pl.pallas_call(fine_backward_kernel, grid=(PAIRS,), in_specs=[tok, tok, t...  9.54 us
    ppermute x2, waiting for transfers between devices, to_previous(): return lax.ppermute(x, 'seq', [(i + 1, i) for i in range(n - 1)])  8.02 us
    pallas_call x1, Pallas kernels, fine_forward(): pl.pallas_call(fine_forward_kernel, grid=(PAIRS,), in_specs=[tok, tok, to...  7.53 us
    ppermute x2, starting transfers between devices, to_next(): return lax.ppermute(x, 'seq', [(i, i + 1) for i in range(n - 1)])  7.42 us
    pallas_call x1, Pallas kernels, join(): pl.pallas_call(join_kernel, out_shape=(jax.ShapeDtypeStruct((TOKENS, HIDD...  6.7 us
    ppermute x2, waiting for transfers between devices, to_next(): return lax.ppermute(x, 'seq', [(i, i + 1) for i in range(n - 1)])  4.68 us
  transfers between devices with their start and end apart: 9, of which 5 were waited for; matrix products, arithmetic and copies ran while one was open for 4% of the time, Pallas kernels for 20%

commit v1 on v0

v1 whole, which is shorter than its diff:
```python
import math

import jax
import jax.numpy as jnp
from jax import lax
from jax.experimental import pallas as pl
from jax.experimental.pallas import tpu as pltpu
from jax.sharding import PartitionSpec as P


HEADS = 16
HEAD_DIM = 64
BLOCK = 64
TOKENS = 256
HIDDEN = 1024
PAIRS = HIDDEN // 128
LEVEL_ROWS = 8
MASKED = -1e30
F32 = jnp.float32
BF16 = jnp.bfloat16
SCALE = 1.0 / math.sqrt(HEAD_DIM)
ROOTS = (math.sqrt(64.0), math.sqrt(128.0), math.sqrt(256.0))


def mm(a, b, dims):
    return lax.dot_general(a, b, (dims, ((), ())), preferred_element_type=F32)


def iota(shape, dim):
    return lax.broadcasted_iota(jnp.int32, shape, dim)


def local_call(kernel, outs, args, flops, scratch=(), exps=0, far_in=(), far_out=()):
    near = pl.BlockSpec(memory_space=pltpu.VMEM)
    far = pl.BlockSpec(memory_space=pltpu.HBM)
    held = [
        pltpu.with_memory_space_constraint(x, pltpu.HBM if i in far_in else pltpu.VMEM)
        for i, x in enumerate(args)
    ]
    return pl.pallas_call(
        kernel,
        in_specs=[far if i in far_in else near for i in range(len(args))],
        out_specs=tuple(far if i in far_out else near for i in range(len(outs))),
        out_shape=tuple(
            (pltpu.HBM if i in far_out else pltpu.VMEM)(*out) for i, out in enumerate(outs)
        ),
        scratch_shapes=list(scratch),
        compiler_params=pltpu.CompilerParams(vmem_limit_bytes=24 << 20),
        cost_estimate=pl.CostEstimate(flops=flops, transcendentals=exps, bytes_accessed=1 << 20),
    )(*held)


def pooled_levels(one):
    two = [one[0] + one[1], one[2] + one[3]]
    three = [two[0] + two[1]]
    return [[x / root for x in rows] for rows, root in zip((one, two, three), ROOTS)]


def pool_kernel(
    q_ref, k_ref, v_ref, send_ref, cq_ref, first_ref, last_ref, held_ref, out_ref, sems, edge_sems, out_sem
):
    me = lax.axis_index("seq")
    copies = {}
    for i, ref in ((1, k_ref), (2, v_ref), (0, q_ref)):
        for b in range(4):
            rows = pl.ds(BLOCK * b, BLOCK)
            copies[i, b] = pltpu.make_async_copy(ref.at[rows], held_ref.at[i, rows], sems.at[i, b])
            copies[i, b].start()
    edges = []
    for i, ref in enumerate((k_ref, v_ref)):
        to = pl.ds(BLOCK * i, BLOCK)
        edges.append(
            pltpu.make_async_copy(ref.at[pl.ds(0, BLOCK)], first_ref.at[to], edge_sems.at[i, 0])
        )
        edges.append(
            pltpu.make_async_copy(
                ref.at[pl.ds(TOKENS - BLOCK, BLOCK)], last_ref.at[to], edge_sems.at[i, 1]
            )
        )
    for copy in edges:
        copy.start()

    def sums(i):
        parts = []
        for b in range(4):
            copies[i, b].wait()
            rows = held_ref[i, BLOCK * b : BLOCK * (b + 1), :].astype(F32)
            parts.append(jnp.sum(rows, axis=0, keepdims=True))
        return parts

    zero = jnp.zeros((1, HIDDEN), F32)
    k1, k2, k3 = pooled_levels(sums(1))
    v1, v2, v3 = pooled_levels(sums(2))
    slot1 = jnp.concatenate(k1 + v1, axis=0)
    slot2 = jnp.concatenate(k2 + [zero] * 2 + v2 + [zero] * 2, axis=0)
    slot3 = jnp.concatenate(k3 + [zero] * 3 + v3 + [zero] * 3, axis=0)
    for g in range(8):
        slot = jnp.where(me // 4 == g, slot1, jnp.where(me // 16 == g // 4, slot2, slot3))
        out_ref[32 * g : 32 * (g + 1), :] = jnp.concatenate([slot] * 4, axis=0).astype(BF16)
    out = pltpu.make_async_copy(out_ref, send_ref, out_sem)
    out.start()
    q1, q2, q3 = pooled_levels(sums(0))
    cq_ref[...] = jnp.concatenate(q1 + q2 + q3 + [zero], axis=0).astype(BF16)
    for copy in edges:
        copy.wait()
    out.wait()


def pool(q, k, v):
    slab = ((2 * BLOCK, HIDDEN), BF16)
    return local_call(
        pool_kernel,
        [((256, HIDDEN), BF16), ((LEVEL_ROWS, HIDDEN), BF16), slab, slab],
        (q, k, v),
        3 * 256 * 1024,
        scratch=[
            pltpu.VMEM((3, TOKENS, HIDDEN), BF16),
            pltpu.VMEM((256, HIDDEN), BF16),
            pltpu.SemaphoreType.DMA((3, 4)),
            pltpu.SemaphoreType.DMA((2, 2)),
            pltpu.SemaphoreType.DMA,
        ],
        far_in=(0, 1, 2),
        far_out=(0,),
    )


def window(own, left, right, half, row):
    if half == 0:
        return jnp.concatenate([left[row : row + BLOCK, :], own[: 3 * BLOCK, :]], axis=0)
    return jnp.concatenate([own[BLOCK:, :], right[row : row + BLOCK, :]], axis=0)


def band_bias(half, key_dim):
    me = lax.axis_index("seq")
    key_block = iota((256, 256), key_dim) // BLOCK
    query_block = iota((256, 256), 1 - key_dim) // BLOCK % 2
    gap = key_block - query_block
    keep = jnp.logical_and(gap >= 0, gap <= 2)
    if half == 0:
        keep = jnp.logical_and(keep, key_block >= jnp.where(me > 0, 0, 1))
    else:
        last = lax.axis_size("seq") - 1
        keep = jnp.logical_and(keep, key_block <= jnp.where(me < last, 3, 2))
    return jnp.where(keep, 0.0, MASKED).astype(F32)


def head_masks(scale):
    lane = iota((1, 128), 1)
    low = jnp.where(lane < HEAD_DIM, scale, 0.0).astype(BF16)
    high = jnp.where(lane < HEAD_DIM, 0.0, scale).astype(BF16)
    return low, high


def two_heads(rows, masks):
    return jnp.concatenate([rows * masks[0], rows * masks[1]], axis=0)


def pick(stacked, low_lane):
    return jnp.where(low_lane, stacked[:128, :], stacked[128:, :])


def over_groups(body, count):
    width = 128 * count

    def step(g, carry):
        start = g * width
        lanes = [pl.ds(pl.multiple_of(start + 128 * p, 128), 128) for p in range(count)]
        body(g, lanes, pl.ds(pl.multiple_of(start, 128), width))
        return carry

    if count == PAIRS:
        body(0, [slice(128 * p, 128 * (p + 1)) for p in range(PAIRS)], slice(0, HIDDEN))
    else:
        lax.fori_loop(0, PAIRS // count, step, 0)


FORWARD_GROUP = 2
BACKWARD_GROUP = 2


def fine_forward_kernel(
    q_ref, k_ref, v_ref, left_ref, right_ref, a_out, lse_out, bias_ref, a_ref, lse_ref, sems, lse_sem
):
    bias_ref[0] = band_bias(0, 1)
    bias_ref[1] = band_bias(1, 1)
    masks = head_masks(SCALE)
    lane = iota((128, 128), 1)
    low_lane = lane < HEAD_DIM
    ones = jnp.ones((256, 128), BF16)
    lse_ref[...] = jnp.zeros((TOKENS, 128), F32)

    def out_copy(g, span):
        return pltpu.make_async_copy(a_ref.at[:, span], a_out.at[:, span], sems.at[g])

    def body(g, groups, span):
        units = [(p, lanes, half) for p, lanes in enumerate(groups) for half in range(2)]
        scores = []
        for p, lanes, half in units:
            rows = slice(128 * half, 128 * (half + 1))
            keys = window(k_ref.at[:, lanes], left_ref.at[:, lanes], right_ref.at[:, lanes], half, 0)
            query = two_heads(q_ref[rows, lanes], masks)
            scores.append(mm(query, keys, ((1,), (1,))) + bias_ref[half])
        tops = [jnp.max(x, axis=1, keepdims=True) for x in scores]
        weights = [jnp.exp(x - top).astype(BF16) for x, top in zip(scores, tops)]
        for (p, lanes, half), top, weight in zip(units, tops, weights):
            rows = slice(128 * half, 128 * (half + 1))
            vals = window(
                v_ref.at[:, lanes], left_ref.at[:, lanes], right_ref.at[:, lanes], half, BLOCK
            )
            both = mm(weight, jnp.concatenate([vals, ones], axis=1), ((1,), (0,)))
            total = both[:, 128:]
            a_ref[rows, lanes] = (pick(both[:, :128], low_lane) / pick(total, low_lane)).astype(BF16)
            lse = top + jnp.log(total)
            head = 2 * (g * len(groups) + p)
            lse_ref[rows, :] = jnp.where(
                lane == head, lse[:128, :], jnp.where(lane == head + 1, lse[128:, :], lse_ref[rows, :])
            )
        out_copy(g, span).start()

    over_groups(body, FORWARD_GROUP)
    lse_copy = pltpu.make_async_copy(lse_ref, lse_out, lse_sem)
    lse_copy.start()
    for g in range(PAIRS // FORWARD_GROUP):
        width = 128 * FORWARD_GROUP
        out_copy(g, pl.ds(width * g, width)).wait()
    lse_copy.wait()


def fine_forward(q, k, v, left, right):
    return local_call(
        fine_forward_kernel,
        [((TOKENS, HIDDEN), BF16), ((TOKENS, 128), F32)],
        (q, k, v, left, right),
        3 * 16 * 2 * 256 * 256 * 128,
        scratch=[
            pltpu.VMEM((2, 256, 256), F32),
            pltpu.VMEM((TOKENS, HIDDEN), BF16),
            pltpu.VMEM((TOKENS, 128), F32),
            pltpu.SemaphoreType.DMA((PAIRS // FORWARD_GROUP,)),
            pltpu.SemaphoreType.DMA,
        ],
        exps=16 * 256 * 256,
        far_out=(0, 1),
    )


def coarse_keep():
    me = lax.axis_index("seq")
    row = iota((128, 256), 0) % LEVEL_ROWS
    col = iota((128, 256), 1)
    dev = col // 8
    term = col % 8
    near = dev // 4 == me // 4
    mid = jnp.logical_and(dev // 16 == me // 16, jnp.logical_not(near))
    far = dev // 16 != me // 16
    apart = jnp.abs(4 * me + row - (4 * dev + term)) > 1
    one = jnp.logical_and(jnp.logical_and(row < 4, term < 4), jnp.logical_and(near, apart))
    two = jnp.logical_and(jnp.logical_and(row // 2 == 2, term < 2), mid)
    three = jnp.logical_and(jnp.logical_and(row == 6, term == 0), far)
    return jnp.logical_or(one, jnp.logical_or(two, three))


def by_head(rows, own):
    return jnp.concatenate([rows] * HEADS, axis=0) * own


def over_heads(stacked, own):
    return jnp.sum((stacked * own).reshape(HEADS, LEVEL_ROWS, HIDDEN), axis=0)


def three_terms(x):
    first = x.astype(BF16)
    rest = x - first.astype(F32)
    second = rest.astype(BF16)
    third = (rest - second.astype(F32)).astype(BF16)
    return jnp.concatenate([first, second, third], axis=1)


def join_kernel(
    cq_ref,
    kv_ref,
    a_hbm,
    lse0_hbm,
    da_hbm,
    att_ref,
    lse_ref,
    delta_ref,
    dq_ref,
    dkv_ref,
    give_ref,
    a_ref,
    da_ref,
    lse0_ref,
    m0_ref,
    mc_ref,
    nc_ref,
    g_ref,
    h_ref,
    sems,
):
    loads = [
        pltpu.make_async_copy(lse0_hbm, lse0_ref, sems.at[2]),
        pltpu.make_async_copy(a_hbm, a_ref, sems.at[0]),
        pltpu.make_async_copy(da_hbm, da_ref, sems.at[1]),
    ]
    for load in loads:
        load.start()
    own = jnp.where(
        iota((128, HIDDEN), 0) // LEVEL_ROWS == iota((128, HIDDEN), 1) // HEAD_DIM, 1.0, 0.0
    ).astype(F32)
    keep = coarse_keep()
    kv = kv_ref[...]
    query = by_head(cq_ref[...].astype(F32), own * SCALE).astype(BF16)
    scores = jnp.where(keep, mm(query, kv, ((1,), (1,))), MASKED)
    top = jnp.max(scores, axis=1, keepdims=True)
    weights = jnp.where(keep, jnp.exp(scores - top), 0.0)
    total = jnp.maximum(jnp.sum(weights, axis=1, keepdims=True), 1.0)
    on_values = pltpu.roll(weights, 4, 1).astype(BF16)
    inverse = 1.0 / total
    nc_ref[...] = over_heads(mm(on_values, kv, ((1,), (0,))) * inverse, own)
    mc_ref[...] = over_heads(jnp.broadcast_to(top + jnp.log(total), (128, HIDDEN)), own)
    same_head = jnp.where(
        iota((128, 128), 0) // HEAD_DIM == iota((128, 128), 1) // HEAD_DIM, 1.0, 0.0
    ).astype(BF16)
    spread = jnp.where(
        iota((384, HIDDEN), 0) % 128 == iota((384, HIDDEN), 1) // HEAD_DIM, 1.0, 0.0
    ).astype(BF16)
    for load in loads:
        load.wait()
    m0_ref[...] = mm(three_terms(lse0_ref[...]), spread, ((1,), (0,)))
    zero = jnp.zeros((1, 128), F32)

    def rows_of(parts):
        one, two, three = zip(*parts)
        return jnp.concatenate(
            list(one)
            + [two[0] + two[1], two[2] + two[3]]
            + [(three[0] + three[1]) + (three[2] + three[3]), zero],
            axis=0,
        )

    for p in range(PAIRS):
        lanes = slice(128 * p, 128 * (p + 1))
        g_parts, h_parts, lses, deltas = [], [], [], []
        for b in range(4):
            rows = slice(BLOCK * b, BLOCK * (b + 1))
            level = (b, 4 + b // 2, 6)
            m0 = m0_ref[rows, lanes]
            mc = [mc_ref[c : c + 1, lanes] for c in level]
            top_all = jnp.maximum(m0, jnp.maximum(mc[0], jnp.maximum(mc[1], mc[2])))
            f0 = jnp.exp(m0 - top_all)
            fc = [jnp.exp(x - top_all) for x in mc]
            inv = 1.0 / (f0 + fc[0] + (fc[1] + fc[2]))
            num = a_ref[rows, lanes].astype(F32) * f0
            for c, f in zip(level, fc):
                num = num + nc_ref[c : c + 1, lanes] * f
            att = (num * inv).astype(BF16)
            att_ref[rows, lanes] = att
            lses.append(top_all - jnp.log(inv))
            da = da_ref[rows, lanes].astype(F32)
            product = da * att.astype(F32)
            part = product.astype(BF16)
            rest = (product - part.astype(F32)).astype(BF16)
            delta = mm(part, same_head, ((1,), (0,))) + mm(rest, same_head, ((1,), (0,)))
            deltas.append(delta)
            wc = [f * inv for f in fc]
            g_parts.append([jnp.sum(w * da, axis=0, keepdims=True) for w in wc])
            h_parts.append([jnp.sum(w * delta, axis=0, keepdims=True) for w in wc])
        for parts, ref in ((lses, lse_ref), (deltas, delta_ref)):
            turned = jnp.concatenate(parts, axis=0).T
            for half in range(2):
                span = slice(128 * half, 128 * (half + 1))
                ref[p, half : half + 1, :] = jnp.concatenate(
                    [turned[:1, span], turned[HEAD_DIM : HEAD_DIM + 1, span]], axis=1
                )
        g_ref[:, lanes] = rows_of(g_parts)
        h_ref[:, lanes] = rows_of(h_parts)
    core = lax.axis_index("dp") % 2
    for hi in range(2):
        start = pl.multiple_of((2 * hi + 1 - core) * 256, 256)
        give_ref[:, 256 * hi : 256 * (hi + 1)] = att_ref[:, pl.ds(start, 256)]
    grads = (by_head(g_ref[...], own) * inverse).astype(BF16)
    sums = jnp.sum(by_head(h_ref[...], own), axis=1, keepdims=True) * (inverse * (1.0 / HEAD_DIM))
    on_keys = pltpu.roll(mm(grads, kv, ((1,), (1,))), 252, 1)
    score_grad = (weights * (on_keys - sums)).astype(BF16)
    row = iota((LEVEL_ROWS, 1), 0)
    share = jnp.where(row < 4, 1.0 / ROOTS[0], jnp.where(row < 6, 1.0 / ROOTS[1], 1.0 / ROOTS[2]))
    dq_ref[...] = over_heads(mm(score_grad, kv, ((1,), (0,))), own) * (share.astype(F32) * SCALE)
    left = jnp.concatenate([score_grad, on_values], axis=0)
    right = jnp.concatenate([query, grads], axis=0)
    dkv_ref[...] = mm(left, right, ((0,), (0,))).astype(BF16)


def join(cq, kv, a, lse0, da):
    stat = ((PAIRS, 2, 256), F32)
    level = pltpu.VMEM((LEVEL_ROWS, HIDDEN), F32)
    return local_call(
        join_kernel,
        [
            ((TOKENS, HIDDEN), BF16),
            stat,
            stat,
            ((LEVEL_ROWS, HIDDEN), F32),
            ((256, HIDDEN), BF16),
            ((TOKENS, 512), BF16),
        ],
        (cq, kv, a, lse0, da),
        5 * 2 * 128 * 256 * 1024,
        scratch=[
            pltpu.VMEM((TOKENS, HIDDEN), BF16),
            pltpu.VMEM((TOKENS, HIDDEN), BF16),
            pltpu.VMEM((TOKENS, 128), F32),
            pltpu.VMEM((TOKENS, HIDDEN), F32),
            level,
            level,
            level,
            level,
            pltpu.SemaphoreType.DMA((3,)),
        ],
        exps=6 * 256 * 1024,
        far_in=(2, 3, 4),
    )


SLOT = 48


def weight_kernel(
    att_ref, got_ref, cot_ref, peer_cot_ref, dkv_ref, send_out, lhs_ref, send_ref, sems
):
    core = lax.axis_index("dp") % 2
    for hi in range(2):
        start = pl.multiple_of((2 * hi + core) * 256, 256)
        rows = slice(256 * hi, 256 * (hi + 1))
        lhs_ref[rows, :TOKENS] = att_ref[:, pl.ds(start, 256)].T
        lhs_ref[rows, TOKENS:] = got_ref[:, rows].T
    width = 256
    copies = []
    for j in range(HIDDEN // width):
        cols = slice(width * j, width * (j + 1))
        cot = jnp.concatenate([cot_ref[:, cols], peer_cot_ref[:, cols]], axis=0)
        terms = mm(lhs_ref[...], cot, ((1,), (0,))).reshape(2, 16, 16, width)
        coarse = dkv_ref[:, cols].astype(F32).reshape(16, 16, width)
        slots = jnp.concatenate([coarse, terms[0], terms[1]], axis=1)
        send_ref[:, cols] = slots.reshape(16 * SLOT, width).astype(BF16)
        span = pl.ds(width * j, width)
        copies.append(
            pltpu.make_async_copy(send_ref.at[:, span], send_out.at[:, span], sems.at[j])
        )
        copies[-1].start()
    for copy in copies:
        copy.wait()


def weight_terms(att, got, cot, peer_cot, dkv):
    return local_call(
        weight_kernel,
        [((16 * SLOT, HIDDEN), BF16)],
        (att, got, cot, peer_cot, dkv),
        2 * 512 * 512 * 1024,
        scratch=[
            pltpu.VMEM((512, 512), BF16),
            pltpu.VMEM((16 * SLOT, HIDDEN), BF16),
            pltpu.SemaphoreType.DMA((4,)),
        ],
        far_out=(0,),
    )[0]


def stat_row(ref, pair, start, count):
    half, at = start // 128, start % 128
    row = ref[pair, half : half + 1, :]
    if count == 128:
        return row
    return jnp.concatenate([row[:, at : at + count], row[:, 128 + at : 128 + at + count]], axis=1)


def edge_backward_kernel(
    q_hbm,
    da_hbm,
    k_hbm,
    v_hbm,
    left_hbm,
    right_hbm,
    lse_ref,
    delta_ref,
    to_left_ref,
    to_right_ref,
    q_ref,
    da_ref,
    k_ref,
    v_ref,
    left_ref,
    right_ref,
    part_sems,
    sems,
):
    me = lax.axis_index("seq")
    now, later = [], []
    for i, (far, near) in enumerate(((left_hbm, left_ref), (right_hbm, right_ref))):
        now.append(pltpu.make_async_copy(far, near, sems.at[i]))
    for i, (far, near) in enumerate(((q_hbm, q_ref), (da_hbm, da_ref))):
        for at, (start, size) in enumerate(
            ((0, BLOCK), (TOKENS - BLOCK, BLOCK), (BLOCK, TOKENS - 2 * BLOCK))
        ):
            rows = pl.ds(start, size)
            copy = pltpu.make_async_copy(far.at[rows], near.at[rows], part_sems.at[i, at])
            (now if at < 2 else later).append(copy)
    for i, (far, near) in enumerate(((k_hbm, k_ref), (v_hbm, v_ref))):
        later.append(pltpu.make_async_copy(far, near, sems.at[2 + i]))
    for copy in now + later:
        copy.start()
    for copy in now:
        copy.wait()
    masks = head_masks(1.0)
    scaled = head_masks(SCALE)
    last = lax.axis_size("seq") - 1
    left_bias = jnp.where(me > 0, 0.0, MASKED).astype(F32)
    right_bias = jnp.where(me < last, 0.0, MASKED).astype(F32)

    def body(g, groups, span):
        units = []
        for p, lanes in enumerate(groups):
            pair = g * len(groups) + p
            units.append((pair, lanes, 0, left_ref, to_left_ref, left_bias))
            units.append((pair, lanes, TOKENS - BLOCK, right_ref, to_right_ref, right_bias))
        held = []
        for pair, lanes, start, near_ref, out_ref, bias in units:
            rows = slice(start, start + BLOCK)
            query = two_heads(q_ref[rows, lanes], scaled)
            grad = two_heads(da_ref[rows, lanes], masks)
            scores = mm(near_ref[:BLOCK, lanes], query, ((1,), (1,))) + bias
            prob_grad = mm(near_ref[BLOCK:, lanes], grad, ((1,), (1,)))
            held.append((query, grad, scores, prob_grad))
        probs = [
            jnp.exp(h[2] - stat_row(lse_ref, u[0], u[2], BLOCK)) for u, h in zip(units, held)
        ]
        for (pair, lanes, start, near_ref, out_ref, bias), (query, grad, _, prob_grad), prob in zip(
            units, held, probs
        ):
            delta = stat_row(delta_ref, pair, start, BLOCK)
            score_grad = (prob * (prob_grad - delta)).astype(BF16)
            out_ref[:BLOCK, lanes] = mm(score_grad, query, ((1,), (0,))).astype(BF16)
            out_ref[BLOCK:, lanes] = mm(prob.astype(BF16), grad, ((1,), (0,))).astype(BF16)

    over_groups(body, PAIRS)
    for copy in later:
        copy.wait()


def edge_backward(q, da, k, v, left, right, lse, delta):
    slab = ((2 * BLOCK, HIDDEN), BF16)
    tokens = ((TOKENS, HIDDEN), BF16)
    return local_call(
        edge_backward_kernel,
        [slab, slab, tokens, tokens, tokens, tokens, slab, slab],
        (q, da, k, v, left, right, lse, delta),
        4 * 16 * 2 * 64 * 128 * 128,
        scratch=[pltpu.SemaphoreType.DMA((2, 3)), pltpu.SemaphoreType.DMA((4,))],
        far_in=(0, 1, 2, 3, 4, 5),
        exps=16 * 64 * 128,
    )


def fine_backward_kernel(
    q_ref,
    k_ref,
    v_ref,
    left_ref,
    right_ref,
    da_ref,
    lse_ref,
    delta_ref,
    cdq_ref,
    gq_out,
    dk_out,
    dv_out,
    bias_ref,
    gq_ref,
    dk_ref,
    dv_ref,
    sems,
):
    bias_ref[0] = band_bias(0, 0)
    bias_ref[1] = band_bias(1, 0)
    masks = head_masks(1.0)
    scaled = head_masks(SCALE)
    low_lane = iota((128, 128), 1) < HEAD_DIM

    def copies(g, span):
        held_refs = (gq_ref, dk_ref, dv_ref)
        return [
            pltpu.make_async_copy(ref.at[:, span], out.at[:, span], sems.at[i, g])
            for i, (ref, out) in enumerate(zip(held_refs, (gq_out, dk_out, dv_out)))
        ]

    def body(g, groups, span):
        units = [
            (g * len(groups) + p, lanes, half) for p, lanes in enumerate(groups) for half in range(2)
        ]
        held = []
        for pair, lanes, half in units:
            rows = slice(128 * half, 128 * (half + 1))
            near = (left_ref.at[:, lanes], right_ref.at[:, lanes], half)
            keys = window(k_ref.at[:, lanes], *near, 0)
            vals = window(v_ref.at[:, lanes], *near, BLOCK)
            query = two_heads(q_ref[rows, lanes], scaled)
            grad = two_heads(da_ref[rows, lanes], masks)
            scores = mm(keys, query, ((1,), (1,))) + bias_ref[half]
            prob_grad = mm(vals, grad, ((1,), (1,)))
            held.append((keys, query, grad, scores, prob_grad))
        probs = [
            jnp.exp(h[3] - stat_row(lse_ref, u[0], 128 * u[2], 128)) for u, h in zip(units, held)
        ]
        parts = []
        for (pair, lanes, half), (keys, query, grad, _, prob_grad), prob in zip(
            units, held, probs
        ):
            rows = slice(128 * half, 128 * (half + 1))
            delta = stat_row(delta_ref, pair, 128 * half, 128)
            score_grad = (prob * (prob_grad - delta)).astype(BF16)
            dk = mm(score_grad, query, ((1,), (0,)))
            dv = mm(prob.astype(BF16), grad, ((1,), (0,)))
            parts.append((dk, dv))
            dq = pick(mm(score_grad, keys, ((0,), (0,))), low_lane) * SCALE
            for b in range(2):
                block = 2 * half + b
                coarse = (
                    cdq_ref[block : block + 1, lanes]
                    + cdq_ref[4 + half : 5 + half, lanes]
                    + cdq_ref[6:7, lanes]
                )
                gq_ref[BLOCK * block : BLOCK * (block + 1), lanes] = (
                    dq[BLOCK * b : BLOCK * (b + 1), :] + coarse
                ).astype(BF16)
        for p, lanes in enumerate(groups):
            for ref, low, high in zip((dk_ref, dv_ref), parts[2 * p], parts[2 * p + 1]):
                ref[:BLOCK, lanes] = low[BLOCK : 2 * BLOCK, :].astype(BF16)
                middle = low[2 * BLOCK :, :] + high[: 2 * BLOCK, :]
                ref[BLOCK : 3 * BLOCK, lanes] = middle.astype(BF16)
                ref[3 * BLOCK :, lanes] = high[2 * BLOCK : 3 * BLOCK, :].astype(BF16)
        for copy in copies(g, span):
            copy.start()

    over_groups(body, BACKWARD_GROUP)
    width = 128 * BACKWARD_GROUP
    for g in range(PAIRS // BACKWARD_GROUP):
        for copy in copies(g, pl.ds(width * g, width)):
            copy.wait()


def fine_backward(q, k, v, left, right, da, lse, delta, cdq):
    out = ((TOKENS, HIDDEN), BF16)
    return local_call(
        fine_backward_kernel,
        [out, out, out],
        (q, k, v, left, right, da, lse, delta, cdq),
        5 * 16 * 2 * 256 * 256 * 128,
        scratch=[pltpu.VMEM((2, 256, 256), F32)]
        + [pltpu.VMEM((TOKENS, HIDDEN), BF16)] * 3
        + [pltpu.SemaphoreType.DMA((3, PAIRS // BACKWARD_GROUP))],
        exps=16 * 256 * 256,
        far_out=(0, 1, 2),
    )


def sums_kernel(
    got_ref,
    dk_hbm,
    dv_hbm,
    coarse_ref,
    mine_ref,
    to_low_ref,
    to_high_ref,
    to_both_ref,
    dk_ref,
    dv_ref,
    sems,
):
    copies = [
        pltpu.make_async_copy(dk_hbm, dk_ref, sems.at[0]),
        pltpu.make_async_copy(dv_hbm, dv_ref, sems.at[1]),
    ]
    for copy in copies:
        copy.start()
    me = lax.axis_index("seq")
    low, column = me % 2, me // 2
    high = lax.axis_index("dp") // 2
    row = iota((64, 16 * SLOT), 0)
    col = iota((64, 16 * SLOT), 1)
    source = col // SLOT
    at = col % SLOT
    near = source // 2 == column // 2
    mid = jnp.logical_and(source // 8 == column // 8, jnp.logical_not(near))
    far = source // 8 != column // 8
    level_row = row % 8
    side = jnp.where(row < 16, low, 1 - low)
    term = at - 8 * side - 4 * (row // 8 % 2)
    one = jnp.logical_and(jnp.logical_and(level_row < 4, term == level_row), near)
    two = jnp.logical_and(jnp.logical_and(level_row // 2 == 2, term == level_row - 4), mid)
    three = jnp.logical_and(jnp.logical_and(level_row == 6, term == 0), far)
    coarse = jnp.logical_and(jnp.logical_or(one, jnp.logical_or(two, three)), row < 32)
    block = row // 8 - 4
    block_high = jnp.where(block < 2, high, 1 - high)
    block_low = jnp.where(block % 2 == 0, low, 1 - low)
    weight = jnp.logical_and(row >= 32, at == 16 + 16 * block_high + 8 * block_low + level_row)
    chosen = jnp.where(jnp.logical_or(coarse, weight), 1.0, 0.0).astype(BF16)
    sums = mm(chosen, got_ref[...], ((1,), (0,)))
    coarse_ref[...] = sums[:16, :]
    mine_ref[...] = sums[32:40, :]
    to_low_ref[:16, :] = sums[16:32, :].astype(BF16)
    to_low_ref[16:, :] = sums[40:48, :].astype(BF16)
    to_high_ref[...] = sums[48:56, :].astype(BF16)
    to_both_ref[...] = sums[56:, :].astype(BF16)
    for copy in copies:
        copy.wait()


def all_sums(got, dk, dv):
    return local_call(
        sums_kernel,
        [
            ((16, HIDDEN), F32),
            ((8, HIDDEN), F32),
            ((24, HIDDEN), BF16),
            ((8, HIDDEN), BF16),
            ((8, HIDDEN), BF16),
            ((TOKENS, HIDDEN), BF16),
            ((TOKENS, HIDDEN), BF16),
        ],
        (got, dk, dv),
        2 * 64 * 768 * 1024,
        scratch=[pltpu.SemaphoreType.DMA((2,))],
        far_in=(1, 2),
    )


def finish_kernel(
    dk_ref,
    dv_ref,
    from_left_ref,
    from_right_ref,
    sums_ref,
    low_ref,
    gk_out,
    gv_out,
    gk_ref,
    gv_ref,
    sems,
):
    copies = []
    sums = sums_ref[...] + low_ref[:16, :].astype(F32)
    for at, own_ref, out_ref, out in ((0, dk_ref, gk_ref, gk_out), (8, dv_ref, gv_ref, gv_out)):
        side = BLOCK * (at // 8)
        for b in range(4):
            rows = slice(BLOCK * b, BLOCK * (b + 1))
            c1, c2, c3 = at + b, at + 4 + b // 2, at + 6
            coarse = (
                sums[c1 : c1 + 1, :] * (1.0 / ROOTS[0])
                + sums[c2 : c2 + 1, :] * (1.0 / ROOTS[1])
                + sums[c3 : c3 + 1, :] * (1.0 / ROOTS[2])
            )
            value = own_ref[rows, :].astype(F32) + coarse
            if b == 0:
                value = value + from_left_ref[side : side + BLOCK, :].astype(F32)
            if b == 3:
                value = value + from_right_ref[side : side + BLOCK, :].astype(F32)
            out_ref[rows, :] = value.astype(BF16)
            span = pl.ds(BLOCK * b, BLOCK)
            copies.append(
                pltpu.make_async_copy(out_ref.at[span], out.at[span], sems.at[at // 8, b])
            )
            copies[-1].start()
    for copy in copies:
        copy.wait()


def finish(dk, dv, from_left, from_right, sums, low):
    out = ((TOKENS, HIDDEN), BF16)
    return local_call(
        finish_kernel,
        [out, out],
        (dk, dv, from_left, from_right, sums, low),
        16 * 256 * 1024,
        scratch=[pltpu.VMEM((TOKENS, HIDDEN), BF16)] * 2 + [pltpu.SemaphoreType.DMA((2, 4))],
        far_out=(0, 1),
    )


def swap(x, axis, bit):
    return lax.ppermute(x, axis, [(i, i ^ bit) for i in range(lax.axis_size(axis))])


def to_next(x):
    n = lax.axis_size("seq")
    return lax.ppermute(x, "seq", [(i, i + 1) for i in range(n - 1)])


def to_previous(x):
    n = lax.axis_size("seq")
    return lax.ppermute(x, "seq", [(i + 1, i) for i in range(n - 1)])


def swap_both(x):
    n = lax.axis_size("seq")
    total = n * lax.axis_size("dp")
    return lax.ppermute(x, ("dp", "seq"), [(i, i ^ (2 * n + 1)) for i in range(total)])


def exchanged(x):
    parts = x.reshape(32, 8, HIDDEN)
    got = lax.all_to_all(parts, "seq", split_axis=0, concat_axis=0, tiled=True)
    return got.reshape(256, HIDDEN)


def exchanged_back(x):
    parts = x.reshape(16, SLOT, HIDDEN)
    groups = [[2 * j + low for j in range(16)] for low in range(2)]
    got = lax.all_to_all(
        parts, "seq", split_axis=0, concat_axis=0, tiled=True, axis_index_groups=groups
    )
    return got.reshape(16 * SLOT, HIDDEN)


def body(q, k, v, out_weight, cot):
    send, cq, first, last = pool(q, k, v)
    left = to_next(last)
    right = to_previous(first)
    coarse_kv = exchanged(send)
    peer_cot = swap(cot, "dp", 1)
    d_att = lax.dot_general(
        cot, out_weight, (((1,), (1,)), ((), ())), preferred_element_type=F32
    ).astype(BF16)
    a0, lse0 = fine_forward(q, k, v, left, right)
    att, lse, delta, cdq, dkv, give = join(cq, coarse_kv, a0, lse0, d_att)
    got = swap(give, "dp", 1)
    mixed = jnp.dot(att, out_weight, preferred_element_type=F32).astype(BF16)
    send_back = weight_terms(att, got, cot, peer_cot, dkv)
    back = exchanged_back(send_back)
    to_left, to_right, *near = edge_backward(q, d_att, k, v, left, right, lse, delta)
    from_left = to_next(to_right)
    from_right = to_previous(to_left)
    near_q, near_da, near_k, near_v, near_left, near_right = near
    gq, dk, dv = fine_backward(
        near_q, near_k, near_v, near_left, near_right, near_da, lse, delta, cdq
    )
    sums, mine, to_low, to_high, to_both, dk, dv = all_sums(back, dk, dv)
    low = swap(to_low, "seq", 1)
    high = swap(to_high, "dp", 2)
    both = swap_both(to_both)
    gk, gv = finish(dk, dv, from_left, from_right, sums, low)
    grad_weight = (mine + low[16:].astype(F32)) + (high.astype(F32) + both.astype(F32))
    return (mixed[None], grad_weight, gq[None], gk[None], gv[None])


def on_device(queries, keys, values, out_weight, cotangent):
    return body(queries[0], keys[0], values[0], out_weight, cotangent[0])


def solution(mesh):
    tokens = P("dp", "seq", None)
    return jax.shard_map(
        on_device,
        mesh=mesh,
        in_specs=(tokens, tokens, tokens, P(), tokens),
        out_specs=(tokens, P(("dp", "seq"), None), tokens, tokens, tokens),
        check_vma=False,
    )
```

time: 105 us -> 96.7 us (0.921)
  Pallas kernels: 32.7 us -> 25.5 us
  waiting for transfers between devices: 26.5 us -> 32 us
  starting transfers between devices: 35.1 us -> 30.6 us
  other arithmetic: 3.39 us -> 0.63 us
  local copies, waits for them, and re-layouts: 0.81 us -> 2.13 us
    pallas_call x6 -> x8, Pallas kernels: 32.7 us -> 25.5 us  [local_call(): pl.pallas_call(kernel, in_specs=[far if i in far_in else near for i in ra...]
    all_to_all x3 -> x2, waiting for transfers between devices: 10.9 us -> 17.7 us  [the longest x1 17.7 us: exchanged_back(): lax.all_to_all(parts, 'seq', split_axis=0, concat_axis=0, tiled=True, axi...]
    all_to_all x3 -> x2, starting transfers between devices: 22.3 us -> 16.2 us  [the longest x1 9.63 us: exchanged(): got = lax.all_to_all(parts, 'seq', split_axis=0, concat_axis=0, tiled=True)]
    convert_element_type x2 -> x0, other arithmetic: 2.61 us -> none  [the longest x1 2.6 us: on_device(): chip = (kept.astype(F32) + got.astype(F32)).astype(BF16)]
    ppermute x0 -> x1, starting transfers between devices: none -> 1.89 us  [swap_both(): lax.ppermute(x, ('dp', 'seq'), [(i, i ^ 2 * n + 1) for i in range(total)])]
    ppermute x0 -> x1, waiting for transfers between devices: none -> 1.55 us  [swap_both(): lax.ppermute(x, ('dp', 'seq'), [(i, i ^ 2 * n + 1) for i in range(total)])]
    ppermute x2 -> x4, waiting for transfers between devices: 2.87 us -> 1.52 us  [swap(): lax.ppermute(x, axis, [(i, i ^ bit) for i in range(lax.axis_size(axis))])]
    ppermute x2, waiting for transfers between devices: 4.68 us -> 3.36 us  [to_next(): return lax.ppermute(x, 'seq', [(i, i + 1) for i in range(n - 1)])]
  transfers between devices with their start and end apart: 9 -> 11, of which waited for: 5 -> 5; matrix products, arithmetic and copies ran while one was open for 4% -> 5% of each run, Pallas kernels for 20% -> 20%
where the time goes in v1:
time: 96.7 us; the launch traced here: 95.8 us
  waiting for transfers between devices  32 us (33%)
  starting transfers between devices  30.6 us (32%)
  Pallas kernels  25.5 us (26%)
  matrix products  4.08 us (4%)
  local copies, waits for them, and re-layouts  2.13 us (2%)
    pallas_call x8, Pallas kernels, local_call(): pl.pallas_call(kernel, in_specs=[far if i in far_in else near for i in ra...  25.5 us
    all_to_all x1, waiting for transfers between devices, exchanged_back(): lax.all_to_all(parts, 'seq', split_axis=0, concat_axis=0, tiled=True, axi...  17.7 us
    all_to_all x1, starting transfers between devices, exchanged(): got = lax.all_to_all(parts, 'seq', split_axis=0, concat_axis=0, tiled=True)  9.63 us
    ppermute x2, waiting for transfers between devices, to_previous(): return lax.ppermute(x, 'seq', [(i + 1, i) for i in range(n - 1)])  7.91 us
    ppermute x2, starting transfers between devices, to_next(): return lax.ppermute(x, 'seq', [(i, i + 1) for i in range(n - 1)])  6.86 us
    all_to_all x1, starting transfers between devices, exchanged_back(): lax.all_to_all(parts, 'seq', split_axis=0, concat_axis=0, tiled=True, axi...  6.54 us
    ppermute x2, waiting for transfers between devices, to_next(): return lax.ppermute(x, 'seq', [(i, i + 1) for i in range(n - 1)])  3.36 us
    ppermute x4, starting transfers between devices, swap(): lax.ppermute(x, axis, [(i, i ^ bit) for i in range(lax.axis_size(axis))])  3.06 us
  transfers between devices with their start and end apart: 11, of which 5 were waited for; matrix products, arithmetic and copies ran while one was open for 5% of the time, Pallas kernels for 20%

profile of v1, /device:TPU:0, one launch (start us, length us, event | category | flops | bytes accessed | tf_op | source)
XLA Modules:
  0.0 95.8 jit_solution(7340803728474925022)
XLA Ops:
  0.6 0.0 copy-start
  0.6 2.5 %shard_map.92 = (bf16[256,1024]{1,0:T(8,128)(2,1)}, bf16[8,1024]{1,0:T(8,128)(2,1)S(1)}, bf16[128,1024]{1,0:T(8,128)(2,1)S(1)}, bf16[128,1024]{1,0:T(8,128)(2,1)S(1)}) custom-call(bf16[256,1024]{1,0:T(8,128)(2,1)} %bitcast.18, bf16[256,1024]{1,0:T(8,128)(2,1)} %bitcast.21, bf16[256,1024]{1,0:T(8,128)(2,1)} %bitcast.24), custom_call_target="tpu_custom_call" | custom-call | flops 786432 | bytes 1048576 | tf_op jit(solution)/shard_map/pallas_call | solution.py:40
  3.1 0.0 copy-start.7
  3.1 0.7 copy-done.7
  3.8 0.0 copy-start.8
  3.8 0.7 copy-done.8
  4.5 0.0 copy-start.1
  4.5 0.0 copy-start.2
  4.5 9.6 %all-to-all-start = ((bf16[32,8,1024]{2,1,0:T(8,128)(2,1)}), bf16[32,8,1024]{2,1,0:T(8,128)(2,1)}, u32[]{:S(2)}, u32[]{:S(2)}) async-start(bf16[32,8,1024]{2,1,0:T(8,128)(2,1)} %bitcast.30), calls=%async_computation | async-start | bytes 1048576 | tf_op jit(solution)/shard_map/all_to_all | solution.py:813
  14.2 0.0 copy-start.3
  14.2 3.8 %collective-permute-start = (bf16[128,1024]{1,0:T(8,128)(2,1)}, bf16[128,1024]{1,0:T(8,128)(2,1)S(1)}, u32[]{:S(2)}, u32[]{:S(2)}) collective-permute-start(bf16[128,1024]{1,0:T(8,128)(2,1)} %copy-done.8), channel_id=1, source_target_pairs={{0,1},{1,2},{2,3},{3,4},{4,5},{5,6},{6,7},{7,8},{8,9},{9,10},{10,1... | collective-permute-start | bytes 786440 | tf_op jit(solution)/shard_map/ppermute | solution.py:797
  18.0 1.3 %collective-permute-start.1 = (bf16[128,1024]{1,0:T(8,128)(2,1)}, bf16[128,1024]{1,0:T(8,128)(2,1)S(1)}, u32[]{:S(2)}, u32[]{:S(2)}) collective-permute-start(bf16[128,1024]{1,0:T(8,128)(2,1)} %copy-done.7), channel_id=1, source_target_pairs={{1,0},{2,1},{3,2},{4,3},{5,4},{6,5},{7,6},{8,7},{9,8},{10,9},{11,1... | collective-permute-start | bytes 786440 | tf_op jit(solution)/shard_map/ppermute | solution.py:802
  19.3 0.1 collective-permute-start.3
  19.4 0.0 copy-done
  19.4 2.6 %convolution_convert_fusion.1.da_hbm = bf16[256,1024]{1,0:T(8,128)(2,1)} fusion(bf16[1024,1024]{1,0:T(8,128)(2,1)S(1)} %copy-done, bf16[1,256,1024]{2,1,0:T(8,128)(2,1)} %param.9), kind=kOutput, calls=%fused_computation.1 | convolution fusion | flops 537133056 | bytes 3145728 | tf_op jit(solution)/shard_map/dot_general | solution.py:832
  21.9 3.4 %collective-permute-done.left_ref.left_hbm = bf16[128,1024]{1,0:T(8,128)(2,1)S(1)} collective-permute-done((bf16[128,1024]{1,0:T(8,128)(2,1)}, bf16[128,1024]{1,0:T(8,128)(2,1)S(1)}, u32[]{:S(2)}, u32[]{:S(2)}) %collective-permute-start) | collective-permute-done | bytes 262176 | tf_op jit(solution)/shard_map/ppermute | solution.py:797
  25.3 0.0 copy-start.5
  25.3 7.9 %collective-permute-done.1.right_ref.right_hbm = bf16[128,1024]{1,0:T(8,128)(2,1)S(1)} collective-permute-done((bf16[128,1024]{1,0:T(8,128)(2,1)}, bf16[128,1024]{1,0:T(8,128)(2,1)S(1)}, u32[]{:S(2)}, u32[]{:S(2)}) %collective-permute-start.1) | collective-permute-done | bytes 262176 | tf_op jit(solution)/shard_map/ppermute | solution.py:802
  33.2 0.0 copy-done.1
  33.2 0.0 copy-done.2
  33.2 0.0 copy-done.3
  33.2 3.1 %shard_map.93 = (bf16[256,1024]{1,0:T(8,128)(2,1)}, f32[256,128]{1,0:T(8,128)}) custom-call(bf16[256,1024]{1,0:T(8,128)(2,1)S(1)} %bitcast.20, bf16[256,1024]{1,0:T(8,128)(2,1)S(1)} %bitcast.23, bf16[256,1024]{1,0:T(8,128)(2,1)S(1)} %bitcast.26, bf16[128,1024]{1,0:T(8,128)(2,1)S(1)} %collective-permute-done.left_ref.left_hbm, ...), custom_call_target="tpu_custom_call" | custom-call | flops 805306368 | bytes 1048576 | tf_op jit(solution)/shard_map/pallas_call | solution.py:40
  36.4 0.0 copy-start.6
  36.4 0.7 copy-done.6
  37.1 0.0 copy-start.4
  37.1 0.0 all-to-all-done
  37.1 5.7 %shard_map.94 = (bf16[256,1024]{1,0:T(8,128)(2,1)S(1)}, f32[8,2,256]{2,1,0:T(2,128)S(1)}, f32[8,2,256]{2,1,0:T(2,128)S(1)}, f32[8,1024]{1,0:T(8,128)S(1)}, bf16[...) custom-call(bf16[8,1024]{1,0:T(8,128)(2,1)S(1)} %get-tuple-element.37.cq_ref, bf16[256,1024]{1,0:T(8,128)(2,1)} %bitcast.4.kv_ref, ...), custom_call_target="tpu_custom_call" | custom-call | flops 335544320 | bytes 1048576 | tf_op jit(solution)/shard_map/pallas_call | solution.py:40
  42.8 0.0 copy-done.5
  42.8 0.1 collective-permute-start.2
  42.9 0.0 collective-permute-done.3.peer_cot_ref
  42.9 1.5 %collective-permute-done.2.got_ref = bf16[256,512]{1,0:T(8,128)(2,1)S(1)} collective-permute-done((bf16[256,512]{1,0:T(8,128)(2,1)S(1)}, bf16[256,512]{1,0:T(8,128)(2,1)S(1)}, u32[]{:S(2)}, u32[]{:S(2)}) %collective-permute-start.2) | collective-permute-done | bytes 262176 | tf_op jit(solution)/shard_map/ppermute | solution.py:792
  44.4 0.0 copy-done.4
  44.4 2.8 %shard_map.95 = bf16[768,1024]{1,0:T(8,128)(2,1)} custom-call(bf16[256,1024]{1,0:T(8,128)(2,1)S(1)} %get-tuple-element.43.att_ref, bf16[256,512]{1,0:T(8,128)(2,1)S(1)} %collective-permute-done.2.got_ref, bf16[256,1024]{1,0:T(8,128)(2,1)S(1)} %bitcast.28, bf16[256,1024]{1,0:T(8,128)(2,1)} %collective-permute-done.3.peer_cot_ref, ...), custom_call_target="tpu_custom_call" | custom-call | flops 536870912 | bytes 1048576 | tf_op jit(solution)/shard_map/pallas_call | solution.py:40
  47.2 6.5 %all-to-all-start.1 = ((bf16[16,48,1024]{2,1,0:T(8,128)(2,1)}), bf16[16,48,1024]{2,1,0:T(8,128)(2,1)}, u32[]{:S(2)}, u32[]{:S(2)}) async-start(bf16[16,48,1024]{2,1,0:T(8,128)(2,1)} %bitcast.29), calls=%async_computation.1 | async-start | bytes 3145728 | tf_op jit(solution)/shard_map/all_to_all | solution.py:820
  53.8 3.2 %shard_map.96 = (bf16[128,1024]{1,0:T(8,128)(2,1)S(1)}, bf16[128,1024]{1,0:T(8,128)(2,1)}, bf16[256,1024]{1,0:T(8,128)(2,1)S(1)}, bf16[256,1024]{1,0:T(8,128)(2,...) custom-call(bf16[256,1024]{1,0:T(8,128)(2,1)} %bitcast.19, ...), custom_call_target="tpu_custom_call" | custom-call | flops 134217728 | bytes 1048576 | tf_op jit(solution)/shard_map/pallas_call | solution.py:40
  57.0 3.1 %collective-permute-start.7 = (bf16[128,1024]{1,0:T(8,128)(2,1)}, bf16[128,1024]{1,0:T(8,128)(2,1)S(1)}, u32[]{:S(2)}, u32[]{:S(2)}) collective-permute-start(bf16[128,1024]{1,0:T(8,128)(2,1)} %get-tuple-element.64), channel_id=1, source_target_pairs={{0,1},{1,2},{2,3},{3,4},{4,5},{5,6},{6,7},{7,8},{8,9},{9,10},{10,1... | collective-permute-start | bytes 786440 | tf_op jit(solution)/shard_map/ppermute | solution.py:797
  60.1 1.3 %collective-permute-start.8 = (bf16[128,1024]{1,0:T(8,128)(2,1)S(1)}, bf16[128,1024]{1,0:T(8,128)(2,1)S(1)}, u32[]{:S(2)}, u32[]{:S(2)}) collective-permute-start(bf16[128,1024]{1,0:T(8,128)(2,1)S(1)} %get-tuple-element.65), channel_id=1, source_target_pairs={{1,0},{2,1},{3,2},{4,3},{5,4},{6,5},{7,6},{8,7},{9,8},{10,9},{11,1... | collective-permute-start | bytes 786440 | tf_op jit(solution)/shard_map/ppermute | solution.py:802
  61.4 4.5 %shard_map.97 = (bf16[256,1024]{1,0:T(8,128)(2,1)}, bf16[256,1024]{1,0:T(8,128)(2,1)}, bf16[256,1024]{1,0:T(8,128)(2,1)}) custom-call(bf16[256,1024]{1,0:T(8,128)(2,1)S(1)} %get-tuple-element.48.q_ref, bf16[256,1024]{1,0:T(8,128)(2,1)S(1)} %get-tuple-element.49.k_ref, bf16[256,1024]{1,0:T(8,128)(2,1)S(1)} %get-tuple-element.50.v_ref, ...), custom_call_target="tpu_custom_call" | custom-call | flops 1342177280 | bytes 1048576 | tf_op jit(solution)/shard_map/pallas_call | solution.py:40
  65.9 17.7 %all-to-all-done.1 = bf16[16,48,1024]{2,1,0:T(8,128)(2,1)} async-done(((bf16[16,48,1024]{2,1,0:T(8,128)(2,1)}), bf16[16,48,1024]{2,1,0:T(8,128)(2,1)}, u32[]{:S(2)}, u32[]{:S(2)}) %all-to-all-start.1) | async-done | bytes 1572896 | tf_op jit(solution)/shard_map/all_to_all | solution.py:820
  83.6 2.6 %shard_map.98 = (f32[16,1024]{1,0:T(8,128)S(1)}, f32[8,1024]{1,0:T(8,128)S(1)}, bf16[24,1024]{1,0:T(8,128)(2,1)S(1)}, bf16[8,1024]{1,0:T(8,128)(2,1)S(1)}, bf16[...) custom-call(bf16[768,1024]{1,0:T(8,128)(2,1)} %bitcast.8.got_ref, ...), custom_call_target="tpu_custom_call" | custom-call | flops 100663296 | bytes 1048576 | tf_op jit(solution)/shard_map/pallas_call | solution.py:40
  86.2 0.1 collective-permute-start.4
  86.3 2.8 %collective-permute-start.5 = (bf16[8,1024]{1,0:T(8,128)(2,1)S(1)}, bf16[8,1024]{1,0:T(8,128)(2,1)S(1)}, u32[]{:S(2)}, u32[]{:S(2)}) collective-permute-start(bf16[8,1024]{1,0:T(8,128)(2,1)S(1)} %get-tuple-element.59), channel_id=1, source_target_pairs={{0,64},{32,96},{64,0},{96,32},{1,65},{33,97},{65,1},{97,33},{2,66}... | collective-permute-start | bytes 49160 | tf_op jit(solution)/shard_map/ppermute | solution.py:792
  89.1 1.9 %collective-permute-start.6 = (bf16[8,1024]{1,0:T(8,128)(2,1)S(1)}, bf16[8,1024]{1,0:T(8,128)(2,1)S(1)}, u32[]{:S(2)}, u32[]{:S(2)}) collective-permute-start(bf16[8,1024]{1,0:T(8,128)(2,1)S(1)} %get-tuple-element.60), channel_id=1, source_target_pairs={{0,65},{1,64},{2,67},{3,66},{4,69},{5,68},{6,71},{7,70},{8,73},{9,... | collective-permute-start | bytes 49160 | tf_op jit(solution)/shard_map/ppermute | solution.py:808
  91.0 1.5 %fusion = bf16[1,256,1024]{2,1,0:T(8,128)(2,1)} fusion(bf16[256,1024]{1,0:T(8,128)(2,1)S(1)} %get-tuple-element.43.att_ref, bf16[1024,1024]{1,0:T(8,128)(2,1)S(1)} %copy-done), kind=kOutput, calls=%fused_computation.2 | convolution fusion | flops 537133056 | bytes 3145728 | tf_op jit(solution)/shard_map/dot_general | solution.py:838
  92.5 0.0 collective-permute-done.5
  92.5 1.6 %collective-permute-done.6 = bf16[8,1024]{1,0:T(8,128)(2,1)S(1)} collective-permute-done((bf16[8,1024]{1,0:T(8,128)(2,1)S(1)}, bf16[8,1024]{1,0:T(8,128)(2,1)S(1)}, u32[]{:S(2)}, u32[]{:S(2)}) %collective-permute-start.6) | collective-permute-done | bytes 16416 | tf_op jit(solution)/shard_map/ppermute | solution.py:808
  94.1 0.0 collective-permute-done.4.low_ref
  94.1 0.6 add_add_fusion
  94.7 0.0 collective-permute-done.7.from_left_ref
  94.7 0.0 collective-permute-done.8.from_right_ref
  94.7 1.1 %shard_map.99 = (bf16[256,1024]{1,0:T(8,128)(2,1)}, bf16[256,1024]{1,0:T(8,128)(2,1)}) custom-call(bf16[256,1024]{1,0:T(8,128)(2,1)S(1)} %get-tuple-element.62.dk_ref, bf16[256,1024]{1,0:T(8,128)(2,1)S(1)} %get-tuple-element.63.dv_ref, bf16[128,1024]{1,0:T(8,128)(2,1)S(1)} %collective-permute-done.7.from_left_ref, ...), custom_call_target="tpu_custom_call" | custom-call | flops 4194304 | bytes 1048576 | tf_op jit(solution)/shard_map/pallas_call | solution.py:40
Async XLA Ops:
  0.6 18.7 %copy-start = (bf16[1024,1024]{1,0:T(8,128)(2,1)S(1)}, bf16[1024,1024]{1,0:T(8,128)(2,1)}, u32[]{:S(2)}) copy-start(bf16[1024,1024]{1,0:T(8,128)(2,1)} %param.8) | copy-start | bytes 6291460
  3.1 0.7 copy-start.7
  3.8 0.7 copy-start.8
  4.5 28.7 %copy-start.1 = (bf16[1,256,1024]{2,1,0:T(8,128)(2,1)S(1)}, bf16[1,256,1024]{2,1,0:T(8,128)(2,1)}, u32[]{:S(2)}) copy-start(bf16[1,256,1024]{2,1,0:T(8,128)(2,1)} %param.5) | copy-start | bytes 1572868
  4.5 28.7 %copy-start.2 = (bf16[1,256,1024]{2,1,0:T(8,128)(2,1)S(1)}, bf16[1,256,1024]{2,1,0:T(8,128)(2,1)}, u32[]{:S(2)}) copy-start(bf16[1,256,1024]{2,1,0:T(8,128)(2,1)} %param.6) | copy-start | bytes 1572868
  4.5 32.5 %all-to-all-start = ((bf16[32,8,1024]{2,1,0:T(8,128)(2,1)}), bf16[32,8,1024]{2,1,0:T(8,128)(2,1)}, u32[]{:S(2)}, u32[]{:S(2)}) async-start(bf16[32,8,1024]{2,1,0:T(8,128)(2,1)} %bitcast.30), calls=%async_computation | async-start | bytes 1048576 | tf_op jit(solution)/shard_map/all_to_all | solution.py:813
  14.2 19.0 %copy-start.3 = (bf16[1,256,1024]{2,1,0:T(8,128)(2,1)S(1)}, bf16[1,256,1024]{2,1,0:T(8,128)(2,1)}, u32[]{:S(2)}) copy-start(bf16[1,256,1024]{2,1,0:T(8,128)(2,1)} %param.7) | copy-start | bytes 1572868
  14.2 11.1 %collective-permute-start = (bf16[128,1024]{1,0:T(8,128)(2,1)}, bf16[128,1024]{1,0:T(8,128)(2,1)S(1)}, u32[]{:S(2)}, u32[]{:S(2)}) collective-permute-start(bf16[128,1024]{1,0:T(8,128)(2,1)} %copy-done.8), channel_id=1, source_target_pairs={{0,1},{1,2},{2,3},{3,4},{4,5},{5,6},{6,7},{7,8},{8,9},{9,10},{10,1... | collective-permute-start | bytes 786440 | tf_op jit(solution)/shard_map/ppermute | solution.py:797
  18.0 15.2 %collective-permute-start.1 = (bf16[128,1024]{1,0:T(8,128)(2,1)}, bf16[128,1024]{1,0:T(8,128)(2,1)S(1)}, u32[]{:S(2)}, u32[]{:S(2)}) collective-permute-start(bf16[128,1024]{1,0:T(8,128)(2,1)} %copy-done.7), channel_id=1, source_target_pairs={{1,0},{2,1},{3,2},{4,3},{5,4},{6,5},{7,6},{8,7},{9,8},{10,9},{11,1... | collective-permute-start | bytes 786440 | tf_op jit(solution)/shard_map/ppermute | solution.py:802
  19.3 23.6 %collective-permute-start.3 = (bf16[256,1024]{1,0:T(8,128)(2,1)}, bf16[256,1024]{1,0:T(8,128)(2,1)}, u32[]{:S(2)}, u32[]{:S(2)}) collective-permute-start(bf16[256,1024]{1,0:T(8,128)(2,1)} %bitcast.27), channel_id=1, source_target_pairs={{0,32},{32,0},{64,96},{96,64},{1,33},{33,1},{65,97},{97,65},{2,34}... | collective-permute-start | bytes 1572872 | tf_op jit(solution)/shard_map/ppermute | solution.py:792
  25.3 17.5 %copy-start.5 = (bf16[128,1024]{1,0:T(8,128)(2,1)}, bf16[128,1024]{1,0:T(8,128)(2,1)S(1)}, u32[]{:S(2)}) copy-start(bf16[128,1024]{1,0:T(8,128)(2,1)S(1)} %collective-permute-done.left_ref.left_hbm) | copy-start | bytes 786436
  36.4 0.7 copy-start.6
  37.1 7.3 %copy-start.4 = (bf16[1,256,1024]{2,1,0:T(8,128)(2,1)S(1)}, bf16[1,256,1024]{2,1,0:T(8,128)(2,1)}, u32[]{:S(2)}) copy-start(bf16[1,256,1024]{2,1,0:T(8,128)(2,1)} %param.9) | copy-start | bytes 1572868
  42.8 1.6 %collective-permute-start.2 = (bf16[256,512]{1,0:T(8,128)(2,1)S(1)}, bf16[256,512]{1,0:T(8,128)(2,1)S(1)}, u32[]{:S(2)}, u32[]{:S(2)}) collective-permute-start(bf16[256,512]{1,0:T(8,128)(2,1)S(1)} %get-tuple-element.44), channel_id=1, source_target_pairs={{0,32},{32,0},{64,96},{96,64},{1,33},{33,1},{65,97},{97,65},{2,34}... | collective-permute-start | bytes 786440 | tf_op jit(solution)/shard_map/ppermute | solution.py:792
  47.2 36.4 %all-to-all-start.1 = ((bf16[16,48,1024]{2,1,0:T(8,128)(2,1)}), bf16[16,48,1024]{2,1,0:T(8,128)(2,1)}, u32[]{:S(2)}, u32[]{:S(2)}) async-start(bf16[16,48,1024]{2,1,0:T(8,128)(2,1)} %bitcast.29), calls=%async_computation.1 | async-start | bytes 3145728 | tf_op jit(solution)/shard_map/all_to_all | solution.py:820
  57.0 37.7 %collective-permute-start.7 = (bf16[128,1024]{1,0:T(8,128)(2,1)}, bf16[128,1024]{1,0:T(8,128)(2,1)S(1)}, u32[]{:S(2)}, u32[]{:S(2)}) collective-permute-start(bf16[128,1024]{1,0:T(8,128)(2,1)} %get-tuple-element.64), channel_id=1, source_target_pairs={{0,1},{1,2},{2,3},{3,4},{4,5},{5,6},{6,7},{7,8},{8,9},{9,10},{10,1... | collective-permute-start | bytes 786440 | tf_op jit(solution)/shard_map/ppermute | solution.py:797
  60.1 34.6 %collective-permute-start.8 = (bf16[128,1024]{1,0:T(8,128)(2,1)S(1)}, bf16[128,1024]{1,0:T(8,128)(2,1)S(1)}, u32[]{:S(2)}, u32[]{:S(2)}) collective-permute-start(bf16[128,1024]{1,0:T(8,128)(2,1)S(1)} %get-tuple-element.65), channel_id=1, source_target_pairs={{1,0},{2,1},{3,2},{4,3},{5,4},{6,5},{7,6},{8,7},{9,8},{10,9},{11,1... | collective-permute-start | bytes 786440 | tf_op jit(solution)/shard_map/ppermute | solution.py:802
  86.2 7.8 %collective-permute-start.4 = (bf16[24,1024]{1,0:T(8,128)(2,1)S(1)}, bf16[24,1024]{1,0:T(8,128)(2,1)S(1)}, u32[]{:S(2)}, u32[]{:S(2)}) collective-permute-start(bf16[24,1024]{1,0:T(8,128)(2,1)S(1)} %get-tuple-element.58), channel_id=1, source_target_pairs={{0,1},{1,0},{2,3},{3,2},{4,5},{5,4},{6,7},{7,6},{8,9},{9,8},{10,11... | collective-permute-start | bytes 147464 | tf_op jit(solution)/shard_map/ppermute | solution.py:792
  86.3 6.2 %collective-permute-start.5 = (bf16[8,1024]{1,0:T(8,128)(2,1)S(1)}, bf16[8,1024]{1,0:T(8,128)(2,1)S(1)}, u32[]{:S(2)}, u32[]{:S(2)}) collective-permute-start(bf16[8,1024]{1,0:T(8,128)(2,1)S(1)} %get-tuple-element.59), channel_id=1, source_target_pairs={{0,64},{32,96},{64,0},{96,32},{1,65},{33,97},{65,1},{97,33},{2,66}... | collective-permute-start | bytes 49160 | tf_op jit(solution)/shard_map/ppermute | solution.py:792
  89.1 4.9 %collective-permute-start.6 = (bf16[8,1024]{1,0:T(8,128)(2,1)S(1)}, bf16[8,1024]{1,0:T(8,128)(2,1)S(1)}, u32[]{:S(2)}, u32[]{:S(2)}) collective-permute-start(bf16[8,1024]{1,0:T(8,128)(2,1)S(1)} %get-tuple-element.60), channel_id=1, source_target_pairs={{0,65},{1,64},{2,67},{3,66},{4,69},{5,68},{6,71},{7,70},{8,73},{9,... | collective-permute-start | bytes 49160 | tf_op jit(solution)/shard_map/ppermute | solution.py:808

commit v2 on v1

--- a/solution.py
+++ b/solution.py
@@ -57,7 +57,7 @@
 
 
 def pool_kernel(
-    q_ref, k_ref, v_ref, send_ref, cq_ref, first_ref, last_ref, held_ref, out_ref, sems, edge_sems, out_sem
+    q_ref, k_ref, v_ref, levels_ref, cq_ref, inner_ref, outer_ref, held_ref, sems, edge_sems
 ):
     me = lax.axis_index("seq")
     copies = {}
@@ -66,17 +66,15 @@
             rows = pl.ds(BLOCK * b, BLOCK)
             copies[i, b] = pltpu.make_async_copy(ref.at[rows], held_ref.at[i, rows], sems.at[i, b])
             copies[i, b].start()
+    inner = pl.multiple_of((1 - me % 2) * (TOKENS - BLOCK), BLOCK)
+    outer = pl.multiple_of((me % 2) * (TOKENS - BLOCK), BLOCK)
     edges = []
     for i, ref in enumerate((k_ref, v_ref)):
         to = pl.ds(BLOCK * i, BLOCK)
-        edges.append(
-            pltpu.make_async_copy(ref.at[pl.ds(0, BLOCK)], first_ref.at[to], edge_sems.at[i, 0])
-        )
-        edges.append(
-            pltpu.make_async_copy(
-                ref.at[pl.ds(TOKENS - BLOCK, BLOCK)], last_ref.at[to], edge_sems.at[i, 1]
+        for j, (start, out) in enumerate(((inner, inner_ref), (outer, outer_ref))):
+            edges.append(
+                pltpu.make_async_copy(ref.at[pl.ds(start, BLOCK)], out.at[to], edge_sems.at[i, j])
             )
-        )
     for copy in edges:
         copy.start()
 
@@ -94,35 +92,53 @@
     slot1 = jnp.concatenate(k1 + v1, axis=0)
     slot2 = jnp.concatenate(k2 + [zero] * 2 + v2 + [zero] * 2, axis=0)
     slot3 = jnp.concatenate(k3 + [zero] * 3 + v3 + [zero] * 3, axis=0)
-    for g in range(8):
-        slot = jnp.where(me // 4 == g, slot1, jnp.where(me // 16 == g // 4, slot2, slot3))
-        out_ref[32 * g : 32 * (g + 1), :] = jnp.concatenate([slot] * 4, axis=0).astype(BF16)
-    out = pltpu.make_async_copy(out_ref, send_ref, out_sem)
-    out.start()
+    levels_ref[...] = jnp.concatenate([slot1, slot2, slot3], axis=0).astype(BF16)
     q1, q2, q3 = pooled_levels(sums(0))
     cq_ref[...] = jnp.concatenate(q1 + q2 + q3 + [zero], axis=0).astype(BF16)
     for copy in edges:
         copy.wait()
-    out.wait()
 
 
 def pool(q, k, v):
     slab = ((2 * BLOCK, HIDDEN), BF16)
     return local_call(
         pool_kernel,
-        [((256, HIDDEN), BF16), ((LEVEL_ROWS, HIDDEN), BF16), slab, slab],
+        [((24, HIDDEN), BF16), ((LEVEL_ROWS, HIDDEN), BF16), slab, slab],
         (q, k, v),
         3 * 256 * 1024,
         scratch=[
             pltpu.VMEM((3, TOKENS, HIDDEN), BF16),
-            pltpu.VMEM((256, HIDDEN), BF16),
             pltpu.SemaphoreType.DMA((3, 4)),
             pltpu.SemaphoreType.DMA((2, 2)),
-            pltpu.SemaphoreType.DMA,
         ],
         far_in=(0, 1, 2),
+    )
+
+
+def slots_kernel(own_ref, peer_ref, send_out, send_ref, sem):
+    column = lax.axis_index("seq") // 2
+    own, peer = own_ref[...].astype(F32), peer_ref[...].astype(F32)
+    one, two, three = [
+        jnp.concatenate([own[8 * i : 8 * (i + 1)], peer[8 * i : 8 * (i + 1)]], axis=0).astype(BF16)
+        for i in range(3)
+    ]
+    for j in range(16):
+        slot = jnp.where(column // 2 == j // 2, one, jnp.where(column // 8 == j // 8, two, three))
+        send_ref[16 * j : 16 * (j + 1), :] = slot
+    copy = pltpu.make_async_copy(send_ref, send_out, sem)
+    copy.start()
+    copy.wait()
+
+
+def slots(own, peer):
+    return local_call(
+        slots_kernel,
+        [((256, HIDDEN), BF16)],
+        (own, peer),
+        256 * 1024,
+        scratch=[pltpu.VMEM((256, HIDDEN), BF16), pltpu.SemaphoreType.DMA],
         far_out=(0,),
-    )
+    )[0]
 
 
 def window(own, left, right, half, row):
@@ -175,72 +191,180 @@
         lax.fori_loop(0, PAIRS // count, step, 0)
 
 
+def by_parity(inner, outer):
+    odd = lax.axis_index("seq") % 2 == 1
+    return jnp.where(odd, inner, outer), jnp.where(odd, outer, inner)
+
+
 FORWARD_GROUP = 2
 BACKWARD_GROUP = 2
-
-
-def fine_forward_kernel(
-    q_ref, k_ref, v_ref, left_ref, right_ref, a_out, lse_out, bias_ref, a_ref, lse_ref, sems, lse_sem
+RIM_GROUP = 4
+
+
+def soft_rows(scores, vals, low_lane, rows):
+    top = jnp.max(scores, axis=1, keepdims=True)
+    weight = jnp.exp(scores - top).astype(BF16)
+    ones = jnp.ones((vals.shape[0], 128), BF16)
+    both = mm(weight, jnp.concatenate([vals, ones], axis=1), ((1,), (0,)))
+    total = both[:, 128:]
+    part = jnp.where(low_lane, both[:rows, :128], both[rows:, :128])
+    share = jnp.where(low_lane, total[:rows], total[rows:])
+    return (part / share).astype(BF16), top + jnp.log(total)
+
+
+def place(ref, span, lse, lane, head, rows):
+    ref[span, :] = jnp.where(
+        lane == head, lse[:rows, :], jnp.where(lane == head + 1, lse[rows:, :], ref[span, :])
+    )
+
+
+def inside_kernel(
+    q_ref,
+    k_ref,
+    v_ref,
+    cot_ref,
+    w_hbm,
+    a_out,
+    lse_out,
+    da_out,
+    a_ref,
+    lse_ref,
+    w_ref,
+    da_ref,
+    sems,
+    lse_sem,
+    w_sems,
+    da_sems,
 ):
-    bias_ref[0] = band_bias(0, 1)
-    bias_ref[1] = band_bias(1, 1)
+    steps = PAIRS // FORWARD_GROUP
+    width = 128 * FORWARD_GROUP
+
+    def w_copy(g):
+        rows = pl.ds(pl.multiple_of(width * g, width), width)
+        return pltpu.make_async_copy(w_hbm.at[rows], w_ref.at[rows], w_sems.at[g])
+
+    def da_copy(g, span):
+        return pltpu.make_async_copy(da_ref.at[:, span], da_out.at[:, span], da_sems.at[g])
+
+    def a_copy(g, span):
+        return pltpu.make_async_copy(a_ref.at[:, span], a_out.at[:, span], sems.at[g])
+
+    for g in range(steps):
+        w_copy(g).start()
+    gap = iota((256, 256), 1) // BLOCK - iota((256, 256), 0) // BLOCK % 2
+    bias = jnp.where(jnp.logical_and(gap >= 0, gap <= 2), 0.0, MASKED).astype(F32)
     masks = head_masks(SCALE)
     lane = iota((128, 128), 1)
     low_lane = lane < HEAD_DIM
-    ones = jnp.ones((256, 128), BF16)
-    lse_ref[...] = jnp.zeros((TOKENS, 128), F32)
-
-    def out_copy(g, span):
-        return pltpu.make_async_copy(a_ref.at[:, span], a_out.at[:, span], sems.at[g])
+    lse_ref[...] = jnp.zeros((128, 128), F32)
 
     def body(g, groups, span):
-        units = [(p, lanes, half) for p, lanes in enumerate(groups) for half in range(2)]
         scores = []
-        for p, lanes, half in units:
-            rows = slice(128 * half, 128 * (half + 1))
-            keys = window(k_ref.at[:, lanes], left_ref.at[:, lanes], right_ref.at[:, lanes], half, 0)
-            query = two_heads(q_ref[rows, lanes], masks)
-            scores.append(mm(query, keys, ((1,), (1,))) + bias_ref[half])
-        tops = [jnp.max(x, axis=1, keepdims=True) for x in scores]
-        weights = [jnp.exp(x - top).astype(BF16) for x, top in zip(scores, tops)]
-        for (p, lanes, half), top, weight in zip(units, tops, weights):
-            rows = slice(128 * half, 128 * (half + 1))
-            vals = window(
-                v_ref.at[:, lanes], left_ref.at[:, lanes], right_ref.at[:, lanes], half, BLOCK
-            )
-            both = mm(weight, jnp.concatenate([vals, ones], axis=1), ((1,), (0,)))
-            total = both[:, 128:]
-            a_ref[rows, lanes] = (pick(both[:, :128], low_lane) / pick(total, low_lane)).astype(BF16)
-            lse = top + jnp.log(total)
-            head = 2 * (g * len(groups) + p)
-            lse_ref[rows, :] = jnp.where(
-                lane == head, lse[:128, :], jnp.where(lane == head + 1, lse[128:, :], lse_ref[rows, :])
-            )
-        out_copy(g, span).start()
+        for lanes in groups:
+            query = two_heads(q_ref[BLOCK : 3 * BLOCK, lanes], masks)
+            scores.append(mm(query, k_ref[:, lanes], ((1,), (1,))) + bias)
+        for p, (lanes, score) in enumerate(zip(groups, scores)):
+            a_ref[:, lanes], lse = soft_rows(score, v_ref[:, lanes], low_lane, 128)
+            place(lse_ref, slice(0, 128), lse, lane, 2 * (g * len(groups) + p), 128)
+        a_copy(g, span).start()
+        w_copy(g).wait()
+        rows = pl.ds(pl.multiple_of(width * g, width), width)
+        da_ref[:, span] = mm(cot_ref[...], w_ref[rows, :], ((1,), (1,))).astype(BF16)
+        da_copy(g, span).start()
 
     over_groups(body, FORWARD_GROUP)
     lse_copy = pltpu.make_async_copy(lse_ref, lse_out, lse_sem)
     lse_copy.start()
-    for g in range(PAIRS // FORWARD_GROUP):
-        width = 128 * FORWARD_GROUP
-        out_copy(g, pl.ds(width * g, width)).wait()
+    for g in range(steps):
+        a_copy(g, pl.ds(width * g, width)).wait()
+        da_copy(g, pl.ds(width * g, width)).wait()
     lse_copy.wait()
 
 
-def fine_forward(q, k, v, left, right):
+def inside_forward(q, k, v, cot, w):
+    steps = PAIRS // FORWARD_GROUP
     return local_call(
-        fine_forward_kernel,
-        [((TOKENS, HIDDEN), BF16), ((TOKENS, 128), F32)],
-        (q, k, v, left, right),
-        3 * 16 * 2 * 256 * 256 * 128,
+        inside_kernel,
+        [((128, HIDDEN), BF16), ((128, 128), F32), ((TOKENS, HIDDEN), BF16)],
+        (q, k, v, cot, w),
+        3 * 16 * 2 * 128 * 256 * 128 + 2 * 256 * 1024 * 1024,
         scratch=[
-            pltpu.VMEM((2, 256, 256), F32),
+            pltpu.VMEM((128, HIDDEN), BF16),
+            pltpu.VMEM((128, 128), F32),
+            pltpu.VMEM((HIDDEN, HIDDEN), BF16),
             pltpu.VMEM((TOKENS, HIDDEN), BF16),
-            pltpu.VMEM((TOKENS, 128), F32),
-            pltpu.SemaphoreType.DMA((PAIRS // FORWARD_GROUP,)),
+            pltpu.SemaphoreType.DMA((steps,)),
             pltpu.SemaphoreType.DMA,
+            pltpu.SemaphoreType.DMA((steps,)),
+            pltpu.SemaphoreType.DMA((steps,)),
         ],
-        exps=16 * 256 * 256,
+        exps=8 * 256 * 256,
+        far_in=(4,),
+        far_out=(0, 1, 2),
+    )
+
+
+def rim_kernel(
+    q_ref, k_ref, v_ref, inner_ref, outer_ref, a_out, lse_out, left_ref, right_ref, a_ref, lse_ref, sems
+):
+    left_ref[...], right_ref[...] = by_parity(inner_ref[...], outer_ref[...])
+    me = lax.axis_index("seq")
+    last = lax.axis_size("seq") - 1
+    key_lane = iota((128, 192), 1)
+    starts = (
+        jnp.where(jnp.logical_and(key_lane < BLOCK, me == 0), MASKED, 0.0).astype(F32),
+        jnp.where(jnp.logical_and(key_lane >= 2 * BLOCK, me == last), MASKED, 0.0).astype(F32),
+    )
+    masks = head_masks(SCALE)
+    lane = iota((BLOCK, 128), 1)
+    low_lane = lane < HEAD_DIM
+    lse_ref[...] = jnp.zeros((128, 128), F32)
+
+    def body(g, groups, span):
+        units = [(p, lanes, side) for p, lanes in enumerate(groups) for side in range(2)]
+        scores = []
+        for p, lanes, side in units:
+            at = side * (TOKENS - BLOCK)
+            query = two_heads(q_ref[at : at + BLOCK, lanes], masks)
+            if side == 0:
+                keys = jnp.concatenate([left_ref[:BLOCK, lanes], k_ref[: 2 * BLOCK, lanes]], axis=0)
+            else:
+                keys = jnp.concatenate([k_ref[2 * BLOCK :, lanes], right_ref[:BLOCK, lanes]], axis=0)
+            scores.append(mm(query, keys, ((1,), (1,))) + starts[side])
+        for (p, lanes, side), score in zip(units, scores):
+            if side == 0:
+                vals = jnp.concatenate([left_ref[BLOCK:, lanes], v_ref[: 2 * BLOCK, lanes]], axis=0)
+            else:
+                vals = jnp.concatenate([v_ref[2 * BLOCK :, lanes], right_ref[BLOCK:, lanes]], axis=0)
+            rows = slice(BLOCK * side, BLOCK * (side + 1))
+            a_ref[rows, lanes], lse = soft_rows(score, vals, low_lane, BLOCK)
+            place(lse_ref, rows, lse, lane, 2 * (g * len(groups) + p), BLOCK)
+
+    over_groups(body, RIM_GROUP)
+    copies = [
+        pltpu.make_async_copy(a_ref, a_out, sems.at[0]),
+        pltpu.make_async_copy(lse_ref, lse_out, sems.at[1]),
+    ]
+    for copy in copies:
+        copy.start()
+    for copy in copies:
+        copy.wait()
+
+
+def rim_forward(q, k, v, inner, outer):
+    return local_call(
+        rim_kernel,
+        [((128, HIDDEN), BF16), ((128, 128), F32)],
+        (q, k, v, inner, outer),
+        3 * 16 * 2 * 128 * 192 * 128,
+        scratch=[
+            pltpu.VMEM((2 * BLOCK, HIDDEN), BF16),
+            pltpu.VMEM((2 * BLOCK, HIDDEN), BF16),
+            pltpu.VMEM((128, HIDDEN), BF16),
+            pltpu.VMEM((128, 128), F32),
+            pltpu.SemaphoreType.DMA((2,)),
+        ],
+        exps=16 * 128 * 192,
         far_out=(0, 1),
     )
 
@@ -249,7 +373,8 @@
     me = lax.axis_index("seq")
     row = iota((128, 256), 0) % LEVEL_ROWS
     col = iota((128, 256), 1)
-    dev = col // 8
+    same = me % 2
+    dev = 2 * (col // 16) + same + (1 - 2 * same) * (col % 16 // 8)
     term = col % 8
     near = dev // 4 == me // 4
     mid = jnp.logical_and(dev // 16 == me // 16, jnp.logical_not(near))
@@ -280,15 +405,21 @@
 def join_kernel(
     cq_ref,
     kv_ref,
-    a_hbm,
-    lse0_hbm,
+    a_mid_hbm,
+    lse_mid_hbm,
+    a_rim_hbm,
+    lse_rim_hbm,
     da_hbm,
+    w_hbm,
     att_ref,
     lse_ref,
     delta_ref,
     dq_ref,
-    dkv_ref,
+    packed_ref,
+    own_ref,
+    near_ref,
     give_ref,
+    w_ref,
     a_ref,
     da_ref,
     lse0_ref,
@@ -297,15 +428,26 @@
     nc_ref,
     g_ref,
     h_ref,
+    dkv_ref,
     sems,
 ):
     loads = [
-        pltpu.make_async_copy(lse0_hbm, lse0_ref, sems.at[2]),
-        pltpu.make_async_copy(a_hbm, a_ref, sems.at[0]),
-        pltpu.make_async_copy(da_hbm, da_ref, sems.at[1]),
+        pltpu.make_async_copy(da_hbm, da_ref, sems.at[0]),
     ]
+    mid = pl.ds(BLOCK, 2 * BLOCK)
+    for i, (mid_hbm, rim_hbm, ref) in enumerate(
+        ((lse_mid_hbm, lse_rim_hbm, lse0_ref), (a_mid_hbm, a_rim_hbm, a_ref))
+    ):
+        loads.append(pltpu.make_async_copy(mid_hbm, ref.at[mid], sems.at[2 + 3 * i]))
+        for side in range(2):
+            to = pl.ds(side * (TOKENS - BLOCK), BLOCK)
+            rows = pl.ds(side * BLOCK, BLOCK)
+            sem = sems.at[3 + 3 * i + side]
+            loads.append(pltpu.make_async_copy(rim_hbm.at[rows], ref.at[to], sem))
+    w_copy = pltpu.make_async_copy(w_hbm, w_ref, sems.at[1])
     for load in loads:
         load.start()
+    w_copy.start()
     own = jnp.where(
         iota((128, HIDDEN), 0) // LEVEL_ROWS == iota((128, HIDDEN), 1) // HEAD_DIM, 1.0, 0.0
     ).astype(F32)
@@ -389,10 +531,20 @@
     dq_ref[...] = over_heads(mm(score_grad, kv, ((1,), (0,))), own) * (share.astype(F32) * SCALE)
     left = jnp.concatenate([score_grad, on_values], axis=0)
     right = jnp.concatenate([query, grads], axis=0)
-    dkv_ref[...] = mm(left, right, ((0,), (0,))).astype(BF16)
-
-
-def join(cq, kv, a, lse0, da):
+    dkv = mm(left, right, ((0,), (0,))).astype(BF16)
+    dkv_ref[...] = dkv
+    row, col = iota((128, 256), 0), iota((128, 256), 1)
+    taken = 16 * (row // 8) + 8 * (row % 8 // 4) + 4 * (row % 4 // 2) + row % 2
+    pick_rows = jnp.where(col == taken, 1.0, 0.0).astype(BF16)
+    packed_ref[...] = mm(pick_rows, dkv, ((1,), (0,))).astype(BF16)
+    column = lax.axis_index("seq") // 2
+    other = column + 1 - 2 * (column % 2)
+    own_ref[...] = dkv_ref[pl.ds(pl.multiple_of(16 * column, 16), 16), :]
+    near_ref[...] = dkv_ref[pl.ds(pl.multiple_of(16 * other, 16), 16), :]
+    w_copy.wait()
+
+
+def join(cq, kv, inside, rim, da, w):
     stat = ((PAIRS, 2, 256), F32)
     level = pltpu.VMEM((LEVEL_ROWS, HIDDEN), F32)
     return local_call(
@@ -402,10 +554,13 @@
             stat,
             stat,
             ((LEVEL_ROWS, HIDDEN), F32),
-            ((256, HIDDEN), BF16),
+            ((128, HIDDEN), BF16),
+            ((16, HIDDEN), BF16),
+            ((16, HIDDEN), BF16),
             ((TOKENS, 512), BF16),
+            ((HIDDEN, HIDDEN), BF16),
         ],
-        (cq, kv, a, lse0, da),
+        (cq, kv, *inside, *rim, da, w),
         5 * 2 * 128 * 256 * 1024,
         scratch=[
             pltpu.VMEM((TOKENS, HIDDEN), BF16),
@@ -416,18 +571,19 @@
             level,
             level,
             level,
-            pltpu.SemaphoreType.DMA((3,)),
+            pltpu.VMEM((256, HIDDEN), BF16),
+            pltpu.SemaphoreType.DMA((8,)),
         ],
         exps=6 * 256 * 1024,
-        far_in=(2, 3, 4),
-    )
-
-
-SLOT = 48
+        far_in=(2, 3, 4, 5, 6, 7),
+    )
+
+
+SLOT = 40
 
 
 def weight_kernel(
-    att_ref, got_ref, cot_ref, peer_cot_ref, dkv_ref, send_out, lhs_ref, send_ref, sems
+    att_ref, got_ref, cot_ref, peer_cot_ref, packed_ref, send_ref, lhs_ref
 ):
     core = lax.axis_index("dp") % 2
     for hi in range(2):
@@ -436,35 +592,22 @@
         lhs_ref[rows, :TOKENS] = att_ref[:, pl.ds(start, 256)].T
         lhs_ref[rows, TOKENS:] = got_ref[:, rows].T
     width = 256
-    copies = []
     for j in range(HIDDEN // width):
         cols = slice(width * j, width * (j + 1))
         cot = jnp.concatenate([cot_ref[:, cols], peer_cot_ref[:, cols]], axis=0)
         terms = mm(lhs_ref[...], cot, ((1,), (0,))).reshape(2, 16, 16, width)
-        coarse = dkv_ref[:, cols].astype(F32).reshape(16, 16, width)
+        coarse = packed_ref[:, cols].astype(F32).reshape(16, 8, width)
         slots = jnp.concatenate([coarse, terms[0], terms[1]], axis=1)
         send_ref[:, cols] = slots.reshape(16 * SLOT, width).astype(BF16)
-        span = pl.ds(width * j, width)
-        copies.append(
-            pltpu.make_async_copy(send_ref.at[:, span], send_out.at[:, span], sems.at[j])
-        )
-        copies[-1].start()
-    for copy in copies:
-        copy.wait()
-
-
-def weight_terms(att, got, cot, peer_cot, dkv):
+
+
+def weight_terms(att, got, cot, peer_cot, packed):
     return local_call(
         weight_kernel,
         [((16 * SLOT, HIDDEN), BF16)],
-        (att, got, cot, peer_cot, dkv),
+        (att, got, cot, peer_cot, packed),
         2 * 512 * 512 * 1024,
-        scratch=[
-            pltpu.VMEM((512, 512), BF16),
-            pltpu.VMEM((16 * SLOT, HIDDEN), BF16),
-            pltpu.SemaphoreType.DMA((4,)),
-        ],
-        far_out=(0,),
+        scratch=[pltpu.VMEM((512, 512), BF16)],
     )[0]
 
 
@@ -481,24 +624,28 @@
     da_hbm,
     k_hbm,
     v_hbm,
-    left_hbm,
-    right_hbm,
+    inner_hbm,
+    outer_hbm,
     lse_ref,
     delta_ref,
-    to_left_ref,
-    to_right_ref,
+    to_inner_ref,
+    to_outer_ref,
     q_ref,
     da_ref,
     k_ref,
     v_ref,
     left_ref,
     right_ref,
+    to_left_ref,
+    to_right_ref,
+    inner_ref,
+    outer_ref,
     part_sems,
     sems,
 ):
     me = lax.axis_index("seq")
     now, later = [], []
-    for i, (far, near) in enumerate(((left_hbm, left_ref), (right_hbm, right_ref))):
+    for i, (far, near) in enumerate(((inner_hbm, inner_ref), (outer_hbm, outer_ref))):
         now.append(pltpu.make_async_copy(far, near, sems.at[i]))
     for i, (far, near) in enumerate(((q_hbm, q_ref), (da_hbm, da_ref))):
         for at, (start, size) in enumerate(
@@ -513,6 +660,7 @@
         copy.start()
     for copy in now:
         copy.wait()
+    left_ref[...], right_ref[...] = by_parity(inner_ref[...], outer_ref[...])
     masks = head_masks(1.0)
     scaled = head_masks(SCALE)
     last = lax.axis_size("seq") - 1
@@ -545,19 +693,21 @@
             out_ref[BLOCK:, lanes] = mm(prob.astype(BF16), grad, ((1,), (0,))).astype(BF16)
 
     over_groups(body, PAIRS)
+    to_inner_ref[...], to_outer_ref[...] = by_parity(to_left_ref[...], to_right_ref[...])
     for copy in later:
         copy.wait()
 
 
-def edge_backward(q, da, k, v, left, right, lse, delta):
+def edge_backward(q, da, k, v, inner, outer, lse, delta):
     slab = ((2 * BLOCK, HIDDEN), BF16)
     tokens = ((TOKENS, HIDDEN), BF16)
     return local_call(
         edge_backward_kernel,
         [slab, slab, tokens, tokens, tokens, tokens, slab, slab],
-        (q, da, k, v, left, right, lse, delta),
+        (q, da, k, v, inner, outer, lse, delta),
         4 * 16 * 2 * 64 * 128 * 128,
-        scratch=[pltpu.SemaphoreType.DMA((2, 3)), pltpu.SemaphoreType.DMA((4,))],
+        scratch=[pltpu.VMEM((2 * BLOCK, HIDDEN), BF16)] * 4
+        + [pltpu.SemaphoreType.DMA((2, 3)), pltpu.SemaphoreType.DMA((4,))],
         far_in=(0, 1, 2, 3, 4, 5),
         exps=16 * 64 * 128,
     )
@@ -667,6 +817,8 @@
 
 def sums_kernel(
     got_ref,
+    near_ref,
+    own_ref,
     dk_hbm,
     dv_hbm,
     coarse_ref,
@@ -695,21 +847,26 @@
     mid = jnp.logical_and(source // 8 == column // 8, jnp.logical_not(near))
     far = source // 8 != column // 8
     level_row = row % 8
-    side = jnp.where(row < 16, low, 1 - low)
-    term = at - 8 * side - 4 * (row // 8 % 2)
-    one = jnp.logical_and(jnp.logical_and(level_row < 4, term == level_row), near)
+    side = jnp.where(row < 16, 0, 1)
+    term = at - 4 * side - 2 * (row // 8 % 2)
     two = jnp.logical_and(jnp.logical_and(level_row // 2 == 2, term == level_row - 4), mid)
     three = jnp.logical_and(jnp.logical_and(level_row == 6, term == 0), far)
-    coarse = jnp.logical_and(jnp.logical_or(one, jnp.logical_or(two, three)), row < 32)
+    coarse = jnp.logical_and(jnp.logical_or(two, three), row < 32)
     block = row // 8 - 4
     block_high = jnp.where(block < 2, high, 1 - high)
     block_low = jnp.where(block % 2 == 0, low, 1 - low)
-    weight = jnp.logical_and(row >= 32, at == 16 + 16 * block_high + 8 * block_low + level_row)
+    weight = jnp.logical_and(row >= 32, at == 8 + 16 * block_high + 8 * block_low + level_row)
     chosen = jnp.where(jnp.logical_or(coarse, weight), 1.0, 0.0).astype(BF16)
     sums = mm(chosen, got_ref[...], ((1,), (0,)))
-    coarse_ref[...] = sums[:16, :]
+    row = iota((32, 32), 0)
+    col = iota((32, 32), 1) % 16
+    side = jnp.where(row < 16, 0, 1)
+    first = jnp.logical_and(row % 8 < 4, col == 8 * side + 4 * (row // 8 % 2) + row % 8)
+    close = jnp.concatenate([near_ref[...], own_ref[...]], axis=0)
+    coarse_sums = sums[:32, :] + mm(jnp.where(first, 1.0, 0.0).astype(BF16), close, ((1,), (0,)))
+    coarse_ref[...] = coarse_sums[:16, :]
     mine_ref[...] = sums[32:40, :]
-    to_low_ref[:16, :] = sums[16:32, :].astype(BF16)
+    to_low_ref[:16, :] = coarse_sums[16:, :].astype(BF16)
     to_low_ref[16:, :] = sums[40:48, :].astype(BF16)
     to_high_ref[...] = sums[48:56, :].astype(BF16)
     to_both_ref[...] = sums[56:, :].astype(BF16)
@@ -717,7 +874,7 @@
         copy.wait()
 
 
-def all_sums(got, dk, dv):
+def all_sums(got, near, own, dk, dv):
     return local_call(
         sums_kernel,
         [
@@ -729,18 +886,18 @@
             ((TOKENS, HIDDEN), BF16),
             ((TOKENS, HIDDEN), BF16),
         ],
-        (got, dk, dv),
-        2 * 64 * 768 * 1024,
+        (got, near, own, dk, dv),
+        2 * 64 * 640 * 1024,
         scratch=[pltpu.SemaphoreType.DMA((2,))],
-        far_in=(1, 2),
+        far_in=(3, 4),
     )
 
 
 def finish_kernel(
     dk_ref,
     dv_ref,
-    from_left_ref,
-    from_right_ref,
+    inner_ref,
+    outer_ref,
     sums_ref,
     low_ref,
     gk_out,
@@ -751,6 +908,7 @@
 ):
     copies = []
     sums = sums_ref[...] + low_ref[:16, :].astype(F32)
+    from_left, from_right = by_parity(inner_ref[...], outer_ref[...])
     for at, own_ref, out_ref, out in ((0, dk_ref, gk_ref, gk_out), (8, dv_ref, gv_ref, gv_out)):
         side = BLOCK * (at // 8)
         for b in range(4):
@@ -763,9 +921,9 @@
             )
             value = own_ref[rows, :].astype(F32) + coarse
             if b == 0:
-                value = value + from_left_ref[side : side + BLOCK, :].astype(F32)
+                value = value + from_left[side : side + BLOCK, :].astype(F32)
             if b == 3:
-                value = value + from_right_ref[side : side + BLOCK, :].astype(F32)
+                value = value + from_right[side : side + BLOCK, :].astype(F32)
             out_ref[rows, :] = value.astype(BF16)
             span = pl.ds(BLOCK * b, BLOCK)
             copies.append(
@@ -776,12 +934,12 @@
         copy.wait()
 
 
-def finish(dk, dv, from_left, from_right, sums, low):
+def finish(dk, dv, inner, outer, sums, low):
     out = ((TOKENS, HIDDEN), BF16)
     return local_call(
         finish_kernel,
         [out, out],
-        (dk, dv, from_left, from_right, sums, low),
+        (dk, dv, inner, outer, sums, low),
         16 * 256 * 1024,
         scratch=[pltpu.VMEM((TOKENS, HIDDEN), BF16)] * 2 + [pltpu.SemaphoreType.DMA((2, 4))],
         far_out=(0, 1),
@@ -792,14 +950,13 @@
     return lax.ppermute(x, axis, [(i, i ^ bit) for i in range(lax.axis_size(axis))])
 
 
-def to_next(x):
+def swap_inner(x):
+    return swap(x, "seq", 1)
+
+
+def swap_outer(x):
     n = lax.axis_size("seq")
-    return lax.ppermute(x, "seq", [(i, i + 1) for i in range(n - 1)])
-
-
-def to_previous(x):
-    n = lax.axis_size("seq")
-    return lax.ppermute(x, "seq", [(i + 1, i) for i in range(n - 1)])
+    return lax.ppermute(x, "seq", [(i, i + 1 if i % 2 else i - 1) for i in range(1, n - 1)])
 
 
 def swap_both(x):
@@ -808,48 +965,51 @@
     return lax.ppermute(x, ("dp", "seq"), [(i, i ^ (2 * n + 1)) for i in range(total)])
 
 
-def exchanged(x):
-    parts = x.reshape(32, 8, HIDDEN)
-    got = lax.all_to_all(parts, "seq", split_axis=0, concat_axis=0, tiled=True)
-    return got.reshape(256, HIDDEN)
-
-
-def exchanged_back(x):
-    parts = x.reshape(16, SLOT, HIDDEN)
+def exchanged(x, rows):
     groups = [[2 * j + low for j in range(16)] for low in range(2)]
     got = lax.all_to_all(
-        parts, "seq", split_axis=0, concat_axis=0, tiled=True, axis_index_groups=groups
-    )
-    return got.reshape(16 * SLOT, HIDDEN)
+        x.reshape(16, rows, HIDDEN),
+        "seq",
+        split_axis=0,
+        concat_axis=0,
+        tiled=True,
+        axis_index_groups=groups,
+    )
+    return got.reshape(16 * rows, HIDDEN)
 
 
 def body(q, k, v, out_weight, cot):
-    send, cq, first, last = pool(q, k, v)
-    left = to_next(last)
-    right = to_previous(first)
-    coarse_kv = exchanged(send)
+    levels, cq, inner, outer = pool(q, k, v)
+    peer_levels = swap(levels, "seq", 1)
+    outer = swap_outer(outer)
+    inner = swap_inner(inner)
+    send = slots(levels, peer_levels)
+    coarse_kv = exchanged(send, 16)
     peer_cot = swap(cot, "dp", 1)
-    d_att = lax.dot_general(
-        cot, out_weight, (((1,), (1,)), ((), ())), preferred_element_type=F32
-    ).astype(BF16)
-    a0, lse0 = fine_forward(q, k, v, left, right)
-    att, lse, delta, cdq, dkv, give = join(cq, coarse_kv, a0, lse0, d_att)
+    *inside, d_att = inside_forward(q, k, v, cot, out_weight)
+    rim = rim_forward(q, k, v, inner, outer)
+    att, lse, delta, cdq, packed, own_rows, near_rows, give, near_w = join(
+        cq, coarse_kv, inside, rim, d_att, out_weight
+    )
     got = swap(give, "dp", 1)
-    mixed = jnp.dot(att, out_weight, preferred_element_type=F32).astype(BF16)
-    send_back = weight_terms(att, got, cot, peer_cot, dkv)
-    back = exchanged_back(send_back)
-    to_left, to_right, *near = edge_backward(q, d_att, k, v, left, right, lse, delta)
-    from_left = to_next(to_right)
-    from_right = to_previous(to_left)
+    mixed = jnp.dot(att, near_w, preferred_element_type=F32).astype(BF16)
+    send_back = weight_terms(att, got, cot, peer_cot, packed)
+    back = exchanged(send_back, SLOT)
+    near_rows = swap(near_rows, "seq", 2)
+    to_inner, to_outer, *near = edge_backward(q, d_att, k, v, inner, outer, lse, delta)
+    from_outer = swap_outer(to_outer)
+    from_inner = swap_inner(to_inner)
     near_q, near_da, near_k, near_v, near_left, near_right = near
     gq, dk, dv = fine_backward(
         near_q, near_k, near_v, near_left, near_right, near_da, lse, delta, cdq
     )
-    sums, mine, to_low, to_high, to_both, dk, dv = all_sums(back, dk, dv)
+    sums, mine, to_low, to_high, to_both, dk, dv = all_sums(
+        back, near_rows, own_rows, dk, dv
+    )
     low = swap(to_low, "seq", 1)
     high = swap(to_high, "dp", 2)
     both = swap_both(to_both)
-    gk, gv = finish(dk, dv, from_left, from_right, sums, low)
+    gk, gv = finish(dk, dv, from_inner, from_outer, sums, low)
     grad_weight = (mine + low[16:].astype(F32)) + (high.astype(F32) + both.astype(F32))
     return (mixed[None], grad_weight, gq[None], gk[None], gv[None])
 

time: 96.7 us -> 84 us (0.87)
  waiting for transfers between devices: 32 us -> 17.5 us
  Pallas kernels: 25.5 us -> 28.3 us
  starting transfers between devices: 30.6 us -> 31.7 us
  matrix products: 4.08 us -> 3.1 us
    ppermute x4 -> x2, waiting for transfers between devices: 11.3 us -> 0.01 us  [swap_outer(): lax.ppermute(x, 'seq', [(i, i + 1 if i % 2 else i - 1) for i in range(1,...]
    ppermute x4 -> x2, starting transfers between devices: 9.45 us -> 1.33 us  [swap_outer(): lax.ppermute(x, 'seq', [(i, i + 1 if i % 2 else i - 1) for i in range(1,...]
    ppermute x4 -> x8, starting transfers between devices: 3.06 us -> 10.5 us  [swap(): lax.ppermute(x, axis, [(i, i ^ bit) for i in range(lax.axis_size(axis))])]
    all_to_all x2, waiting for transfers between devices: 17.7 us -> 10.9 us  [exchanged(): lax.all_to_all(x.reshape(16, rows, HIDDEN), 'seq', split_axis=0, concat_a...]
    ppermute x4 -> x8, waiting for transfers between devices: 1.52 us -> 5.83 us  [swap(): lax.ppermute(x, axis, [(i, i ^ bit) for i in range(lax.axis_size(axis))])]
    pallas_call x8 -> x10, Pallas kernels: 25.5 us -> 28.3 us  [local_call(): pl.pallas_call(kernel, in_specs=[far if i in far_in else near for i in ra...]
    all_to_all x2, starting transfers between devices: 16.2 us -> 18.8 us  [exchanged(): lax.all_to_all(x.reshape(16, rows, HIDDEN), 'seq', split_axis=0, concat_a...]
    dot_general x2 -> x1, matrix products: 4.08 us -> 3.1 us  [body(): mixed = jnp.dot(att, near_w, preferred_element_type=F32).astype(BF16)]
  transfers between devices with their start and end apart: 11 -> 13, of which waited for: 5 -> 8; matrix products, arithmetic and copies ran while one was open for 5% -> 4% of each run, Pallas kernels for 20% -> 25%
where the time goes in v2:
time: 84 us; the launch traced here: 83.5 us
  starting transfers between devices  31.7 us (38%)
  Pallas kernels  28.3 us (34%)
  waiting for transfers between devices  17.5 us (21%)
  matrix products  3.1 us (4%)
  local copies, waits for them, and re-layouts  1.38 us (2%)
  between operations  0.85 us (1%)
    pallas_call x10, Pallas kernels, local_call(): pl.pallas_call(kernel, in_specs=[far if i in far_in else near for i in ra...  28.3 us
    all_to_all x2, starting transfers between devices, exchanged(): lax.all_to_all(x.reshape(16, rows, HIDDEN), 'seq', split_axis=0, concat_a...  18.8 us
    all_to_all x2, waiting for transfers between devices, exchanged(): lax.all_to_all(x.reshape(16, rows, HIDDEN), 'seq', split_axis=0, concat_a...  10.9 us
    ppermute x8, starting transfers between devices, swap(): lax.ppermute(x, axis, [(i, i ^ bit) for i in range(lax.axis_size(axis))])  10.5 us
    ppermute x8, waiting for transfers between devices, swap(): lax.ppermute(x, axis, [(i, i ^ bit) for i in range(lax.axis_size(axis))])  5.83 us
    dot_general x1, matrix products, body(): mixed = jnp.dot(att, near_w, preferred_element_type=F32).astype(BF16)  3.1 us
  transfers between devices with their start and end apart: 13, of which 8 were waited for; matrix products, arithmetic and copies ran while one was open for 4% of the time, Pallas kernels for 25%

profile of v2, /device:TPU:0, one launch (start us, length us, event | category | flops | bytes accessed | tf_op | source)
XLA Modules:
  0.0 83.5 jit_solution(10466887591899552439)
XLA Ops:
  0.6 0.0 copy-start.2
  0.6 0.0 copy-start.1
  0.7 0.0 copy-start
  0.7 0.0 copy-start.3
  0.7 2.6 %shard_map.92 = (bf16[24,1024]{1,0:T(8,128)(2,1)S(1)}, bf16[8,1024]{1,0:T(8,128)(2,1)S(1)}, bf16[128,1024]{1,0:T(8,128)(2,1)}, bf16[128,1024]{1,0:T(8,128)(2,1)S(1)}) custom-call(bf16[256,1024]{1,0:T(8,128)(2,1)} %bitcast.15, bf16[256,1024]{1,0:T(8,128)(2,1)} %bitcast.19, bf16[256,1024]{1,0:T(8,128)(2,1)} %bitcast.23), custom_call_target="tpu_custom_call" | custom-call | flops 786432 | bytes 1048576 | tf_op jit(solution)/shard_map/pallas_call | solution.py:40
  3.3 1.7 %collective-permute-start = (bf16[24,1024]{1,0:T(8,128)(2,1)S(1)}, bf16[24,1024]{1,0:T(8,128)(2,1)S(1)}, u32[]{:S(2)}, u32[]{:S(2)}) collective-permute-start(bf16[24,1024]{1,0:T(8,128)(2,1)S(1)} %get-tuple-element.44.own_ref), channel_id=1, source_target_pairs={{0,1},{1,0},{2,3},{3,2},{4,5},{5,4},{6,7},{7,6},{8,9},{9,8},{10,11... | collective-permute-start | bytes 147464 | tf_op jit(solution)/shard_map/ppermute | solution.py:950
  4.9 2.5 %collective-permute-done.peer_ref = bf16[24,1024]{1,0:T(8,128)(2,1)S(1)} collective-permute-done((bf16[24,1024]{1,0:T(8,128)(2,1)S(1)}, bf16[24,1024]{1,0:T(8,128)(2,1)S(1)}, u32[]{:S(2)}, u32[]{:S(2)}) %collective-permute-start) | collective-permute-done | bytes 49184 | tf_op jit(solution)/shard_map/ppermute | solution.py:950
  7.4 0.8 %shard_map.93 = bf16[256,1024]{1,0:T(8,128)(2,1)} custom-call(bf16[24,1024]{1,0:T(8,128)(2,1)S(1)} %get-tuple-element.44.own_ref, bf16[24,1024]{1,0:T(8,128)(2,1)S(1)} %collective-permute-done.peer_ref), custom_call_target="tpu_custom_call" | custom-call | flops 262144 | bytes 1048576 | tf_op jit(solution)/shard_map/pallas_call | solution.py:40
  8.3 8.2 %all-to-all-start = ((bf16[16,16,1024]{2,1,0:T(8,128)(2,1)}), bf16[16,16,1024]{2,1,0:T(8,128)(2,1)S(1)}, u32[]{:S(2)}, u32[]{:S(2)}) async-start(bf16[16,16,1024]{2,1,0:T(8,128)(2,1)} %bitcast.32), calls=%async_computation | async-start | bytes 1048576 | tf_op jit(solution)/shard_map/all_to_all | solution.py:970
  16.5 1.6 %collective-permute-start.1 = (bf16[128,1024]{1,0:T(8,128)(2,1)}, bf16[128,1024]{1,0:T(8,128)(2,1)S(1)}, u32[]{:S(2)}, u32[]{:S(2)}) collective-permute-start(bf16[128,1024]{1,0:T(8,128)(2,1)} %get-tuple-element.47), channel_id=1, source_target_pairs={{0,1},{1,0},{2,3},{3,2},{4,5},{5,4},{6,7},{7,6},{8,9},{9,8},{10,11... | collective-permute-start | bytes 786440 | tf_op jit(solution)/shard_map/ppermute | solution.py:950
  18.0 0.7 collective-permute-start.2
  18.7 0.0 copy-done.3
  18.7 0.1 collective-permute-start.4
  18.8 0.0 copy-done.2
  18.8 0.0 copy-done.1
  18.8 0.0 copy-done
  18.8 5.0 %shard_map.94 = (bf16[128,1024]{1,0:T(8,128)(2,1)}, f32[128,128]{1,0:T(8,128)}, bf16[256,1024]{1,0:T(8,128)(2,1)}) custom-call(bf16[256,1024]{1,0:T(8,128)(2,1)S(1)} %bitcast.17, bf16[256,1024]{1,0:T(8,128)(2,1)S(1)} %bitcast.21, bf16[256,1024]{1,0:T(8,128)(2,1)S(1)} %bitcast.25, bf16[256,1024]{1,0:T(8,128)(2,1)S(1)} %bitcast.30, bf16[1024,1024]{1,0:T(8,128)(2,1)} %w_hbm.3), custom_call_target="tpu_custom_call" | custom-call | flops 939524096 | bytes 1048576 | tf_op jit(solution)/shard_map/pallas_call | solution.py:40
  23.8 1.3 %collective-permute-done.1.inner_ref.inner_hbm = bf16[128,1024]{1,0:T(8,128)(2,1)S(1)} collective-permute-done((bf16[128,1024]{1,0:T(8,128)(2,1)}, bf16[128,1024]{1,0:T(8,128)(2,1)S(1)}, u32[]{:S(2)}, u32[]{:S(2)}) %collective-permute-start.1) | collective-permute-done | bytes 262176 | tf_op jit(solution)/shard_map/ppermute | solution.py:950
  25.1 0.0 copy-start.4
  25.1 0.0 collective-permute-done.2.outer_ref.outer_hbm
  25.1 0.0 copy-start.5
  25.1 2.2 %shard_map.95 = (bf16[128,1024]{1,0:T(8,128)(2,1)}, f32[128,128]{1,0:T(8,128)}) custom-call(bf16[256,1024]{1,0:T(8,128)(2,1)S(1)} %bitcast.18, bf16[256,1024]{1,0:T(8,128)(2,1)S(1)} %bitcast.22, bf16[256,1024]{1,0:T(8,128)(2,1)S(1)} %bitcast.26, bf16[128,1024]{1,0:T(8,128)(2,1)S(1)} %collective-permute-done.1.inner_ref.inner_hbm, ...), custom_call_target="tpu_custom_call" | custom-call | flops 301989888 | bytes 1048576 | tf_op jit(solution)/shard_map/pallas_call | solution.py:40
  27.4 0.2 all-to-all-done
  27.5 4.5 %shard_map.96 = (bf16[256,1024]{1,0:T(8,128)(2,1)S(1)}, f32[8,2,256]{2,1,0:T(2,128)S(1)}, f32[8,2,256]{2,1,0:T(2,128)S(1)}, f32[8,1024]{1,0:T(8,128)S(1)}, bf16[...) custom-call(bf16[8,1024]{1,0:T(8,128)(2,1)S(1)} %get-tuple-element.4, ...), custom_call_target="tpu_custom_call" | custom-call | flops 335544320 | bytes 1048576 | tf_op jit(solution)/shard_map/pallas_call | solution.py:40
  32.0 0.0 copy-done.4
  32.0 0.0 copy-done.5
  32.1 0.0 copy-start.8
  32.1 1.3 %copy-done.8 = bf16[1024,1024]{1,0:T(8,128)(2,1)} copy-done((bf16[1024,1024]{1,0:T(8,128)(2,1)}, bf16[1024,1024]{1,0:T(8,128)(2,1)S(1)}, u32[]{:S(2)}) %copy-start.8) | copy-done | bytes 2097176
  33.4 0.0 copy-start.6
  33.4 0.0 collective-permute-start.3
  33.4 0.0 collective-permute-done.4.peer_cot_ref
  33.4 1.5 %collective-permute-done.3.got_ref = bf16[256,512]{1,0:T(8,128)(2,1)S(1)} collective-permute-done((bf16[256,512]{1,0:T(8,128)(2,1)S(1)}, bf16[256,512]{1,0:T(8,128)(2,1)S(1)}, u32[]{:S(2)}, u32[]{:S(2)}) %collective-permute-start.3) | collective-permute-done | bytes 262176 | tf_op jit(solution)/shard_map/ppermute | solution.py:950
  34.9 2.9 %shard_map.97 = bf16[640,1024]{1,0:T(8,128)(2,1)} custom-call(bf16[256,1024]{1,0:T(8,128)(2,1)S(1)} %get-tuple-element.52.att_ref, bf16[256,512]{1,0:T(8,128)(2,1)S(1)} %collective-permute-done.3.got_ref, bf16[256,1024]{1,0:T(8,128)(2,1)S(1)} %bitcast.31, bf16[256,1024]{1,0:T(8,128)(2,1)} %collective-permute-done.4.peer_cot_ref, ...), custom_call_target="tpu_custom_call" | custom-call | flops 536870912 | bytes 1048576 | tf_op jit(solution)/shard_map/pallas_call | solution.py:40
  37.8 0.0 copy-done.6
  37.8 10.6 %all-to-all-start.1 = ((bf16[16,40,1024]{2,1,0:T(8,128)(2,1)}), bf16[16,40,1024]{2,1,0:T(8,128)(2,1)S(1)}, u32[]{:S(2)}, u32[]{:S(2)}) async-start(bf16[16,40,1024]{2,1,0:T(8,128)(2,1)} %bitcast.7), calls=%async_computation.1 | async-start | bytes 2621440 | tf_op jit(solution)/shard_map/all_to_all | solution.py:970
  48.5 1.9 %collective-permute-start.5 = (bf16[16,1024]{1,0:T(8,128)(2,1)S(1)}, bf16[16,1024]{1,0:T(8,128)(2,1)S(1)}, u32[]{:S(2)}, u32[]{:S(2)}) collective-permute-start(bf16[16,1024]{1,0:T(8,128)(2,1)S(1)} %get-tuple-element.56), channel_id=1, source_target_pairs={{0,2},{1,3},{2,0},{3,1},{4,6},{5,7},{6,4},{7,5},{8,10},{9,11},{10,... | collective-permute-start | bytes 98312 | tf_op jit(solution)/shard_map/ppermute | solution.py:950
  50.4 3.2 %shard_map.98 = (bf16[128,1024]{1,0:T(8,128)(2,1)}, bf16[128,1024]{1,0:T(8,128)(2,1)S(1)}, bf16[256,1024]{1,0:T(8,128)(2,1)S(1)}, bf16[256,1024]{1,0:T(8,128)(2,...) custom-call(bf16[256,1024]{1,0:T(8,128)(2,1)} %bitcast.16, ...), custom_call_target="tpu_custom_call" | custom-call | flops 134217728 | bytes 1048576 | tf_op jit(solution)/shard_map/pallas_call | solution.py:40
  53.6 2.1 %collective-permute-start.9 = (bf16[128,1024]{1,0:T(8,128)(2,1)}, bf16[128,1024]{1,0:T(8,128)(2,1)S(1)}, u32[]{:S(2)}, u32[]{:S(2)}) collective-permute-start(bf16[128,1024]{1,0:T(8,128)(2,1)} %get-tuple-element.76), channel_id=1, source_target_pairs={{0,1},{1,0},{2,3},{3,2},{4,5},{5,4},{6,7},{7,6},{8,9},{9,8},{10,11... | collective-permute-start | bytes 786440 | tf_op jit(solution)/shard_map/ppermute | solution.py:950
  55.8 0.7 collective-permute-start.10
  56.5 4.5 %shard_map.99 = (bf16[256,1024]{1,0:T(8,128)(2,1)}, bf16[256,1024]{1,0:T(8,128)(2,1)}, bf16[256,1024]{1,0:T(8,128)(2,1)}) custom-call(bf16[256,1024]{1,0:T(8,128)(2,1)S(1)} %get-tuple-element.60.q_ref, bf16[256,1024]{1,0:T(8,128)(2,1)S(1)} %get-tuple-element.61.k_ref, bf16[256,1024]{1,0:T(8,128)(2,1)S(1)} %get-tuple-element.62.v_ref, ...), custom_call_target="tpu_custom_call" | custom-call | flops 1342177280 | bytes 1048576 | tf_op jit(solution)/shard_map/pallas_call | solution.py:40
  61.0 0.0 copy-start.7
  61.0 0.4 collective-permute-done.5.near_ref
  61.4 10.7 %all-to-all-done.1 = bf16[16,40,1024]{2,1,0:T(8,128)(2,1)S(1)} async-done(((bf16[16,40,1024]{2,1,0:T(8,128)(2,1)}), bf16[16,40,1024]{2,1,0:T(8,128)(2,1)S(1)}, u32[]{:S(2)}, u32[]{:S(2)}) %all-to-all-start.1) | async-done | bytes 1310752 | tf_op jit(solution)/shard_map/all_to_all | solution.py:970
  72.1 1.5 %shard_map.100 = (f32[16,1024]{1,0:T(8,128)S(1)}, f32[8,1024]{1,0:T(8,128)S(1)}, bf16[24,1024]{1,0:T(8,128)(2,1)S(1)}, bf16[8,1024]{1,0:T(8,128)(2,1)S(1)}, bf16...) custom-call(bf16[640,1024]{1,0:T(8,128)(2,1)S(1)} %bitcast.27, ...), custom_call_target="tpu_custom_call" | custom-call | flops 83886080 | bytes 1048576 | tf_op jit(solution)/shard_map/pallas_call | solution.py:40
  73.6 3.1 %collective-permute-start.7 = (bf16[8,1024]{1,0:T(8,128)(2,1)S(1)}, bf16[8,1024]{1,0:T(8,128)(2,1)S(1)}, u32[]{:S(2)}, u32[]{:S(2)}) collective-permute-start(bf16[8,1024]{1,0:T(8,128)(2,1)S(1)} %get-tuple-element.71), channel_id=1, source_target_pairs={{0,64},{32,96},{64,0},{96,32},{1,65},{33,97},{65,1},{97,33},{2,66}... | collective-permute-start | bytes 49160 | tf_op jit(solution)/shard_map/ppermute | solution.py:950
  76.7 1.0 %collective-permute-start.8 = (bf16[8,1024]{1,0:T(8,128)(2,1)S(1)}, bf16[8,1024]{1,0:T(8,128)(2,1)S(1)}, u32[]{:S(2)}, u32[]{:S(2)}) collective-permute-start(bf16[8,1024]{1,0:T(8,128)(2,1)S(1)} %get-tuple-element.72), channel_id=1, source_target_pairs={{0,65},{1,64},{2,67},{3,66},{4,69},{5,68},{6,71},{7,70},{8,73},{9,... | collective-permute-start | bytes 49160 | tf_op jit(solution)/shard_map/ppermute | solution.py:965
  77.7 0.0 collective-permute-start.6
  77.7 0.0 copy-done.7
  77.7 3.1 %fusion = bf16[1,256,1024]{2,1,0:T(8,128)(2,1)} fusion(bf16[256,1024]{1,0:T(8,128)(2,1)S(1)} %copy-done.7, bf16[1024,1024]{1,0:T(8,128)(2,1)} %copy-done.8), kind=kOutput, calls=%fused_computation.1 | convolution fusion | flops 537133056 | bytes 3145728 | tf_op jit(solution)/shard_map/dot_general | solution.py:995
  80.8 0.0 collective-permute-done.7
  80.8 0.8 %collective-permute-done.8 = bf16[8,1024]{1,0:T(8,128)(2,1)S(1)} collective-permute-done((bf16[8,1024]{1,0:T(8,128)(2,1)S(1)}, bf16[8,1024]{1,0:T(8,128)(2,1)S(1)}, u32[]{:S(2)}, u32[]{:S(2)}) %collective-permute-start.8) | collective-permute-done | bytes 16416 | tf_op jit(solution)/shard_map/ppermute | solution.py:965
  81.6 0.1 collective-permute-done.6.low_ref
  81.8 0.6 add_add_fusion
  82.4 0.0 collective-permute-done.9.inner_ref
  82.4 0.0 collective-permute-done.10.outer_ref
  82.4 1.1 %shard_map.101 = (bf16[256,1024]{1,0:T(8,128)(2,1)}, bf16[256,1024]{1,0:T(8,128)(2,1)}) custom-call(bf16[256,1024]{1,0:T(8,128)(2,1)S(1)} %get-tuple-element.74.dk_ref, bf16[256,1024]{1,0:T(8,128)(2,1)S(1)} %get-tuple-element.75.dv_ref, bf16[128,1024]{1,0:T(8,128)(2,1)S(1)} %collective-permute-done.9.inner_ref, ...), custom_call_target="tpu_custom_call" | custom-call | flops 4194304 | bytes 1048576 | tf_op jit(solution)/shard_map/pallas_call | solution.py:40
Async XLA Ops:
  0.6 18.2 %copy-start.2 = (bf16[1,256,1024]{2,1,0:T(8,128)(2,1)S(1)}, bf16[1,256,1024]{2,1,0:T(8,128)(2,1)}, u32[]{:S(2)}) copy-start(bf16[1,256,1024]{2,1,0:T(8,128)(2,1)} %param.7) | copy-start | bytes 1572868
  0.6 18.2 %copy-start.1 = (bf16[1,256,1024]{2,1,0:T(8,128)(2,1)S(1)}, bf16[1,256,1024]{2,1,0:T(8,128)(2,1)}, u32[]{:S(2)}) copy-start(bf16[1,256,1024]{2,1,0:T(8,128)(2,1)} %param.6) | copy-start | bytes 1572868
  0.7 18.2 %copy-start = (bf16[1,256,1024]{2,1,0:T(8,128)(2,1)S(1)}, bf16[1,256,1024]{2,1,0:T(8,128)(2,1)}, u32[]{:S(2)}) copy-start(bf16[1,256,1024]{2,1,0:T(8,128)(2,1)} %param.5) | copy-start | bytes 1572868
  0.7 18.0 %copy-start.3 = (bf16[1,256,1024]{2,1,0:T(8,128)(2,1)S(1)}, bf16[1,256,1024]{2,1,0:T(8,128)(2,1)}, u32[]{:S(2)}) copy-start(bf16[1,256,1024]{2,1,0:T(8,128)(2,1)} %param.9) | copy-start | bytes 1572868
  3.3 4.2 %collective-permute-start = (bf16[24,1024]{1,0:T(8,128)(2,1)S(1)}, bf16[24,1024]{1,0:T(8,128)(2,1)S(1)}, u32[]{:S(2)}, u32[]{:S(2)}) collective-permute-start(bf16[24,1024]{1,0:T(8,128)(2,1)S(1)} %get-tuple-element.44.own_ref), channel_id=1, source_target_pairs={{0,1},{1,0},{2,3},{3,2},{4,5},{5,4},{6,7},{7,6},{8,9},{9,8},{10,11... | collective-permute-start | bytes 147464 | tf_op jit(solution)/shard_map/ppermute | solution.py:950
  8.3 19.2 %all-to-all-start = ((bf16[16,16,1024]{2,1,0:T(8,128)(2,1)}), bf16[16,16,1024]{2,1,0:T(8,128)(2,1)S(1)}, u32[]{:S(2)}, u32[]{:S(2)}) async-start(bf16[16,16,1024]{2,1,0:T(8,128)(2,1)} %bitcast.32), calls=%async_computation | async-start | bytes 1048576 | tf_op jit(solution)/shard_map/all_to_all | solution.py:970
  16.5 8.6 %collective-permute-start.1 = (bf16[128,1024]{1,0:T(8,128)(2,1)}, bf16[128,1024]{1,0:T(8,128)(2,1)S(1)}, u32[]{:S(2)}, u32[]{:S(2)}) collective-permute-start(bf16[128,1024]{1,0:T(8,128)(2,1)} %get-tuple-element.47), channel_id=1, source_target_pairs={{0,1},{1,0},{2,3},{3,2},{4,5},{5,4},{6,7},{7,6},{8,9},{9,8},{10,11... | collective-permute-start | bytes 786440 | tf_op jit(solution)/shard_map/ppermute | solution.py:950
  18.0 7.1 %collective-permute-start.2 = (bf16[128,1024]{1,0:T(8,128)(2,1)S(1)}, bf16[128,1024]{1,0:T(8,128)(2,1)S(1)}, u32[]{:S(2)}, u32[]{:S(2)}) collective-permute-start(bf16[128,1024]{1,0:T(8,128)(2,1)S(1)} %get-tuple-element.48), channel_id=1, source_target_pairs={{1,2},{2,1},{3,4},{4,3},{5,6},{6,5},{7,8},{8,7},{9,10},{10,9},{11,... | collective-permute-start | bytes 786440 | tf_op jit(solution)/shard_map/ppermute | solution.py:959
  18.7 14.7 %collective-permute-start.4 = (bf16[256,1024]{1,0:T(8,128)(2,1)S(1)}, bf16[256,1024]{1,0:T(8,128)(2,1)}, u32[]{:S(2)}, u32[]{:S(2)}) collective-permute-start(bf16[256,1024]{1,0:T(8,128)(2,1)S(1)} %bitcast.29), channel_id=1, source_target_pairs={{0,32},{32,0},{64,96},{96,64},{1,33},{33,1},{65,97},{97,65},{2,34}... | collective-permute-start | bytes 1572872 | tf_op jit(solution)/shard_map/ppermute | solution.py:950
  25.1 6.9 %copy-start.4 = (bf16[128,1024]{1,0:T(8,128)(2,1)}, bf16[128,1024]{1,0:T(8,128)(2,1)S(1)}, u32[]{:S(2)}) copy-start(bf16[128,1024]{1,0:T(8,128)(2,1)S(1)} %collective-permute-done.1.inner_ref.inner_hbm) | copy-start | bytes 786436
  25.1 6.9 %copy-start.5 = (bf16[128,1024]{1,0:T(8,128)(2,1)}, bf16[128,1024]{1,0:T(8,128)(2,1)S(1)}, u32[]{:S(2)}) copy-start(bf16[128,1024]{1,0:T(8,128)(2,1)S(1)} %collective-permute-done.2.outer_ref.outer_hbm) | copy-start | bytes 786436
  32.1 1.3 %copy-start.8 = (bf16[1024,1024]{1,0:T(8,128)(2,1)}, bf16[1024,1024]{1,0:T(8,128)(2,1)S(1)}, u32[]{:S(2)}) copy-start(bf16[1024,1024]{1,0:T(8,128)(2,1)S(1)} %get-tuple-element.53) | copy-start | bytes 6291460
  33.4 4.4 %copy-start.6 = (bf16[256,1024]{1,0:T(8,128)(2,1)}, bf16[256,1024]{1,0:T(8,128)(2,1)S(1)}, u32[]{:S(2)}) copy-start(bf16[256,1024]{1,0:T(8,128)(2,1)S(1)} %get-tuple-element.52.att_ref) | copy-start | bytes 1572868
  33.4 1.5 %collective-permute-start.3 = (bf16[256,512]{1,0:T(8,128)(2,1)S(1)}, bf16[256,512]{1,0:T(8,128)(2,1)S(1)}, u32[]{:S(2)}, u32[]{:S(2)}) collective-permute-start(bf16[256,512]{1,0:T(8,128)(2,1)S(1)} %get-tuple-element.54), channel_id=1, source_target_pairs={{0,32},{32,0},{64,96},{96,64},{1,33},{33,1},{65,97},{97,65},{2,34}... | collective-permute-start | bytes 786440 | tf_op jit(solution)/shard_map/ppermute | solution.py:950
  37.8 34.3 %all-to-all-start.1 = ((bf16[16,40,1024]{2,1,0:T(8,128)(2,1)}), bf16[16,40,1024]{2,1,0:T(8,128)(2,1)S(1)}, u32[]{:S(2)}, u32[]{:S(2)}) async-start(bf16[16,40,1024]{2,1,0:T(8,128)(2,1)} %bitcast.7), calls=%async_computation.1 | async-start | bytes 2621440 | tf_op jit(solution)/shard_map/all_to_all | solution.py:970
  48.5 12.9 %collective-permute-start.5 = (bf16[16,1024]{1,0:T(8,128)(2,1)S(1)}, bf16[16,1024]{1,0:T(8,128)(2,1)S(1)}, u32[]{:S(2)}, u32[]{:S(2)}) collective-permute-start(bf16[16,1024]{1,0:T(8,128)(2,1)S(1)} %get-tuple-element.56), channel_id=1, source_target_pairs={{0,2},{1,3},{2,0},{3,1},{4,6},{5,7},{6,4},{7,5},{8,10},{9,11},{10,... | collective-permute-start | bytes 98312 | tf_op jit(solution)/shard_map/ppermute | solution.py:950
  53.6 28.7 %collective-permute-start.9 = (bf16[128,1024]{1,0:T(8,128)(2,1)}, bf16[128,1024]{1,0:T(8,128)(2,1)S(1)}, u32[]{:S(2)}, u32[]{:S(2)}) collective-permute-start(bf16[128,1024]{1,0:T(8,128)(2,1)} %get-tuple-element.76), channel_id=1, source_target_pairs={{0,1},{1,0},{2,3},{3,2},{4,5},{5,4},{6,7},{7,6},{8,9},{9,8},{10,11... | collective-permute-start | bytes 786440 | tf_op jit(solution)/shard_map/ppermute | solution.py:950
  55.8 26.6 %collective-permute-start.10 = (bf16[128,1024]{1,0:T(8,128)(2,1)S(1)}, bf16[128,1024]{1,0:T(8,128)(2,1)S(1)}, u32[]{:S(2)}, u32[]{:S(2)}) collective-permute-start(bf16[128,1024]{1,0:T(8,128)(2,1)S(1)} %get-tuple-element.77), channel_id=1, source_target_pairs={{1,2},{2,1},{3,4},{4,3},{5,6},{6,5},{7,8},{8,7},{9,10},{10,9},{11,... | collective-permute-start | bytes 786440 | tf_op jit(solution)/shard_map/ppermute | solution.py:959
  61.0 16.7 %copy-start.7 = (bf16[256,1024]{1,0:T(8,128)(2,1)S(1)}, bf16[256,1024]{1,0:T(8,128)(2,1)}, u32[]{:S(2)}) copy-start(bf16[256,1024]{1,0:T(8,128)(2,1)} %copy-done.6) | copy-start | bytes 1572868
  73.6 7.2 %collective-permute-start.7 = (bf16[8,1024]{1,0:T(8,128)(2,1)S(1)}, bf16[8,1024]{1,0:T(8,128)(2,1)S(1)}, u32[]{:S(2)}, u32[]{:S(2)}) collective-permute-start(bf16[8,1024]{1,0:T(8,128)(2,1)S(1)} %get-tuple-element.71), channel_id=1, source_target_pairs={{0,64},{32,96},{64,0},{96,32},{1,65},{33,97},{65,1},{97,33},{2,66}... | collective-permute-start | bytes 49160 | tf_op jit(solution)/shard_map/ppermute | solution.py:950
  76.7 4.9 %collective-permute-start.8 = (bf16[8,1024]{1,0:T(8,128)(2,1)S(1)}, bf16[8,1024]{1,0:T(8,128)(2,1)S(1)}, u32[]{:S(2)}, u32[]{:S(2)}) collective-permute-start(bf16[8,1024]{1,0:T(8,128)(2,1)S(1)} %get-tuple-element.72), channel_id=1, source_target_pairs={{0,65},{1,64},{2,67},{3,66},{4,69},{5,68},{6,71},{7,70},{8,73},{9,... | collective-permute-start | bytes 49160 | tf_op jit(solution)/shard_map/ppermute | solution.py:965
  77.7 4.1 %collective-permute-start.6 = (bf16[24,1024]{1,0:T(8,128)(2,1)S(1)}, bf16[24,1024]{1,0:T(8,128)(2,1)S(1)}, u32[]{:S(2)}, u32[]{:S(2)}) collective-permute-start(bf16[24,1024]{1,0:T(8,128)(2,1)S(1)} %get-tuple-element.70), channel_id=1, source_target_pairs={{0,1},{1,0},{2,3},{3,2},{4,5},{5,4},{6,7},{7,6},{8,9},{9,8},{10,11... | collective-permute-start | bytes 147464 | tf_op jit(solution)/shard_map/ppermute | solution.py:950

commit v3 on v2

--- a/solution.py
+++ b/solution.py
@@ -402,6 +402,43 @@
     return jnp.concatenate([first, second, third], axis=1)
 
 
+def stat_row(ref, pair, start, count):
+    half, at = start // 128, start % 128
+    row = ref[pair, half : half + 1, :]
+    if count == 128:
+        return row
+    return jnp.concatenate([row[:, at : at + count], row[:, 128 + at : 128 + at + count]], axis=1)
+
+
+def edge_terms(q_ref, da_ref, lse_ref, delta_ref, left_ref, right_ref, to_left_ref, to_right_ref):
+    me = lax.axis_index("seq")
+    masks = head_masks(1.0)
+    scaled = head_masks(SCALE)
+    last = lax.axis_size("seq") - 1
+    left_bias = jnp.where(me > 0, 0.0, MASKED).astype(F32)
+    right_bias = jnp.where(me < last, 0.0, MASKED).astype(F32)
+    units = []
+    for pair in range(PAIRS):
+        lanes = slice(128 * pair, 128 * (pair + 1))
+        units.append((pair, lanes, 0, 0, left_ref, to_left_ref, left_bias))
+        units.append((pair, lanes, TOKENS - BLOCK, BLOCK, right_ref, to_right_ref, right_bias))
+    held = []
+    for pair, lanes, start, at, near_ref, out_ref, bias in units:
+        query = two_heads(q_ref[at : at + BLOCK, lanes], scaled)
+        grad = two_heads(da_ref[start : start + BLOCK, lanes], masks)
+        scores = mm(near_ref[:BLOCK, lanes], query, ((1,), (1,))) + bias
+        prob_grad = mm(near_ref[BLOCK:, lanes], grad, ((1,), (1,)))
+        held.append((query, grad, scores, prob_grad))
+    probs = [jnp.exp(h[2] - stat_row(lse_ref, u[0], u[2], BLOCK)) for u, h in zip(units, held)]
+    for (pair, lanes, start, at, near_ref, out_ref, bias), (query, grad, _, prob_grad), prob in zip(
+        units, held, probs
+    ):
+        delta = stat_row(delta_ref, pair, start, BLOCK)
+        score_grad = (prob * (prob_grad - delta)).astype(BF16)
+        out_ref[:BLOCK, lanes] = mm(score_grad, query, ((1,), (0,))).astype(BF16)
+        out_ref[BLOCK:, lanes] = mm(prob.astype(BF16), grad, ((1,), (0,))).astype(BF16)
+
+
 def join_kernel(
     cq_ref,
     kv_ref,
@@ -410,7 +447,9 @@
     a_rim_hbm,
     lse_rim_hbm,
     da_hbm,
-    w_hbm,
+    q_hbm,
+    inner_hbm,
+    outer_hbm,
     att_ref,
     lse_ref,
     delta_ref,
@@ -419,7 +458,8 @@
     own_ref,
     near_ref,
     give_ref,
-    w_ref,
+    to_inner_ref,
+    to_outer_ref,
     a_ref,
     da_ref,
     lse0_ref,
@@ -429,7 +469,15 @@
     g_ref,
     h_ref,
     dkv_ref,
+    q_ref,
+    inner_ref,
+    outer_ref,
+    left_ref,
+    right_ref,
+    to_left_ref,
+    to_right_ref,
     sems,
+    edge_sems,
 ):
     loads = [
         pltpu.make_async_copy(da_hbm, da_ref, sems.at[0]),
@@ -444,10 +492,18 @@
             rows = pl.ds(side * BLOCK, BLOCK)
             sem = sems.at[3 + 3 * i + side]
             loads.append(pltpu.make_async_copy(rim_hbm.at[rows], ref.at[to], sem))
-    w_copy = pltpu.make_async_copy(w_hbm, w_ref, sems.at[1])
-    for load in loads:
+    edge_loads = [
+        pltpu.make_async_copy(inner_hbm, inner_ref, edge_sems.at[0]),
+        pltpu.make_async_copy(outer_hbm, outer_ref, edge_sems.at[1]),
+    ]
+    for side in range(2):
+        rows = pl.ds(side * (TOKENS - BLOCK), BLOCK)
+        to = pl.ds(side * BLOCK, BLOCK)
+        edge_loads.append(
+            pltpu.make_async_copy(q_hbm.at[rows], q_ref.at[to], edge_sems.at[2 + side])
+        )
+    for load in loads + edge_loads:
         load.start()
-    w_copy.start()
     own = jnp.where(
         iota((128, HIDDEN), 0) // LEVEL_ROWS == iota((128, HIDDEN), 1) // HEAD_DIM, 1.0, 0.0
     ).astype(F32)
@@ -518,6 +574,11 @@
                 )
         g_ref[:, lanes] = rows_of(g_parts)
         h_ref[:, lanes] = rows_of(h_parts)
+    for load in edge_loads:
+        load.wait()
+    left_ref[...], right_ref[...] = by_parity(inner_ref[...], outer_ref[...])
+    edge_terms(q_ref, da_ref, lse_ref, delta_ref, left_ref, right_ref, to_left_ref, to_right_ref)
+    to_inner_ref[...], to_outer_ref[...] = by_parity(to_left_ref[...], to_right_ref[...])
     core = lax.axis_index("dp") % 2
     for hi in range(2):
         start = pl.multiple_of((2 * hi + 1 - core) * 256, 256)
@@ -541,12 +602,12 @@
     other = column + 1 - 2 * (column % 2)
     own_ref[...] = dkv_ref[pl.ds(pl.multiple_of(16 * column, 16), 16), :]
     near_ref[...] = dkv_ref[pl.ds(pl.multiple_of(16 * other, 16), 16), :]
-    w_copy.wait()
-
-
-def join(cq, kv, inside, rim, da, w):
+
+
+def join(cq, kv, inside, rim, da, q, inner, outer):
     stat = ((PAIRS, 2, 256), F32)
     level = pltpu.VMEM((LEVEL_ROWS, HIDDEN), F32)
+    slab = ((2 * BLOCK, HIDDEN), BF16)
     return local_call(
         join_kernel,
         [
@@ -558,9 +619,10 @@
             ((16, HIDDEN), BF16),
             ((16, HIDDEN), BF16),
             ((TOKENS, 512), BF16),
-            ((HIDDEN, HIDDEN), BF16),
+            slab,
+            slab,
         ],
-        (cq, kv, *inside, *rim, da, w),
+        (cq, kv, *inside, *rim, da, q, inner, outer),
         5 * 2 * 128 * 256 * 1024,
         scratch=[
             pltpu.VMEM((TOKENS, HIDDEN), BF16),
@@ -572,10 +634,12 @@
             level,
             level,
             pltpu.VMEM((256, HIDDEN), BF16),
+            *[pltpu.VMEM(*slab)] * 7,
             pltpu.SemaphoreType.DMA((8,)),
+            pltpu.SemaphoreType.DMA((4,)),
         ],
         exps=6 * 256 * 1024,
-        far_in=(2, 3, 4, 5, 6, 7),
+        far_in=(2, 3, 4, 5, 6, 7, 8, 9),
     )
 
 
@@ -583,8 +647,10 @@
 
 
 def weight_kernel(
-    att_ref, got_ref, cot_ref, peer_cot_ref, packed_ref, send_ref, lhs_ref
+    att_ref, got_ref, cot_ref, peer_cot_ref, packed_ref, send_ref, att_out, lhs_ref, att_sem
 ):
+    att_copy = pltpu.make_async_copy(att_ref, att_out, att_sem)
+    att_copy.start()
     core = lax.axis_index("dp") % 2
     for hi in range(2):
         start = pl.multiple_of((2 * hi + core) * 256, 256)
@@ -599,141 +665,75 @@
         coarse = packed_ref[:, cols].astype(F32).reshape(16, 8, width)
         slots = jnp.concatenate([coarse, terms[0], terms[1]], axis=1)
         send_ref[:, cols] = slots.reshape(16 * SLOT, width).astype(BF16)
+    att_copy.wait()
 
 
 def weight_terms(att, got, cot, peer_cot, packed):
     return local_call(
         weight_kernel,
-        [((16 * SLOT, HIDDEN), BF16)],
+        [((16 * SLOT, HIDDEN), BF16), ((TOKENS, HIDDEN), BF16)],
         (att, got, cot, peer_cot, packed),
         2 * 512 * 512 * 1024,
-        scratch=[pltpu.VMEM((512, 512), BF16)],
-    )[0]
-
-
-def stat_row(ref, pair, start, count):
-    half, at = start // 128, start % 128
-    row = ref[pair, half : half + 1, :]
-    if count == 128:
-        return row
-    return jnp.concatenate([row[:, at : at + count], row[:, 128 + at : 128 + at + count]], axis=1)
-
-
-def edge_backward_kernel(
+        scratch=[pltpu.VMEM((512, 512), BF16), pltpu.SemaphoreType.DMA],
+        far_out=(1,),
+    )
+
+
+def fine_backward_kernel(
     q_hbm,
-    da_hbm,
     k_hbm,
     v_hbm,
     inner_hbm,
     outer_hbm,
-    lse_ref,
-    delta_ref,
-    to_inner_ref,
-    to_outer_ref,
-    q_ref,
-    da_ref,
-    k_ref,
-    v_ref,
-    left_ref,
-    right_ref,
-    to_left_ref,
-    to_right_ref,
-    inner_ref,
-    outer_ref,
-    part_sems,
-    sems,
-):
-    me = lax.axis_index("seq")
-    now, later = [], []
-    for i, (far, near) in enumerate(((inner_hbm, inner_ref), (outer_hbm, outer_ref))):
-        now.append(pltpu.make_async_copy(far, near, sems.at[i]))
-    for i, (far, near) in enumerate(((q_hbm, q_ref), (da_hbm, da_ref))):
-        for at, (start, size) in enumerate(
-            ((0, BLOCK), (TOKENS - BLOCK, BLOCK), (BLOCK, TOKENS - 2 * BLOCK))
-        ):
-            rows = pl.ds(start, size)
-            copy = pltpu.make_async_copy(far.at[rows], near.at[rows], part_sems.at[i, at])
-            (now if at < 2 else later).append(copy)
-    for i, (far, near) in enumerate(((k_hbm, k_ref), (v_hbm, v_ref))):
-        later.append(pltpu.make_async_copy(far, near, sems.at[2 + i]))
-    for copy in now + later:
-        copy.start()
-    for copy in now:
-        copy.wait()
-    left_ref[...], right_ref[...] = by_parity(inner_ref[...], outer_ref[...])
-    masks = head_masks(1.0)
-    scaled = head_masks(SCALE)
-    last = lax.axis_size("seq") - 1
-    left_bias = jnp.where(me > 0, 0.0, MASKED).astype(F32)
-    right_bias = jnp.where(me < last, 0.0, MASKED).astype(F32)
-
-    def body(g, groups, span):
-        units = []
-        for p, lanes in enumerate(groups):
-            pair = g * len(groups) + p
-            units.append((pair, lanes, 0, left_ref, to_left_ref, left_bias))
-            units.append((pair, lanes, TOKENS - BLOCK, right_ref, to_right_ref, right_bias))
-        held = []
-        for pair, lanes, start, near_ref, out_ref, bias in units:
-            rows = slice(start, start + BLOCK)
-            query = two_heads(q_ref[rows, lanes], scaled)
-            grad = two_heads(da_ref[rows, lanes], masks)
-            scores = mm(near_ref[:BLOCK, lanes], query, ((1,), (1,))) + bias
-            prob_grad = mm(near_ref[BLOCK:, lanes], grad, ((1,), (1,)))
-            held.append((query, grad, scores, prob_grad))
-        probs = [
-            jnp.exp(h[2] - stat_row(lse_ref, u[0], u[2], BLOCK)) for u, h in zip(units, held)
-        ]
-        for (pair, lanes, start, near_ref, out_ref, bias), (query, grad, _, prob_grad), prob in zip(
-            units, held, probs
-        ):
-            delta = stat_row(delta_ref, pair, start, BLOCK)
-            score_grad = (prob * (prob_grad - delta)).astype(BF16)
-            out_ref[:BLOCK, lanes] = mm(score_grad, query, ((1,), (0,))).astype(BF16)
-            out_ref[BLOCK:, lanes] = mm(prob.astype(BF16), grad, ((1,), (0,))).astype(BF16)
-
-    over_groups(body, PAIRS)
-    to_inner_ref[...], to_outer_ref[...] = by_parity(to_left_ref[...], to_right_ref[...])
-    for copy in later:
-        copy.wait()
-
-
-def edge_backward(q, da, k, v, inner, outer, lse, delta):
-    slab = ((2 * BLOCK, HIDDEN), BF16)
-    tokens = ((TOKENS, HIDDEN), BF16)
-    return local_call(
-        edge_backward_kernel,
-        [slab, slab, tokens, tokens, tokens, tokens, slab, slab],
-        (q, da, k, v, inner, outer, lse, delta),
-        4 * 16 * 2 * 64 * 128 * 128,
-        scratch=[pltpu.VMEM((2 * BLOCK, HIDDEN), BF16)] * 4
-        + [pltpu.SemaphoreType.DMA((2, 3)), pltpu.SemaphoreType.DMA((4,))],
-        far_in=(0, 1, 2, 3, 4, 5),
-        exps=16 * 64 * 128,
-    )
-
-
-def fine_backward_kernel(
-    q_ref,
-    k_ref,
-    v_ref,
-    left_ref,
-    right_ref,
-    da_ref,
+    da_hbm,
+    att_hbm,
+    w_hbm,
     lse_ref,
     delta_ref,
     cdq_ref,
     gq_out,
     dk_out,
     dv_out,
+    mixed_out,
     bias_ref,
     gq_ref,
     dk_ref,
     dv_ref,
+    mixed_ref,
+    q_ref,
+    k_ref,
+    v_ref,
+    da_ref,
+    att_ref,
+    w_ref,
+    inner_ref,
+    outer_ref,
+    left_ref,
+    right_ref,
     sems,
+    load_sems,
+    mixed_sem,
 ):
+    pairs = (
+        (inner_hbm, inner_ref),
+        (outer_hbm, outer_ref),
+        (k_hbm, k_ref),
+        (q_hbm, q_ref),
+        (v_hbm, v_ref),
+        (da_hbm, da_ref),
+        (att_hbm, att_ref),
+        (w_hbm, w_ref),
+    )
+    loads = [
+        pltpu.make_async_copy(far, near, load_sems.at[i]) for i, (far, near) in enumerate(pairs)
+    ]
+    for load in loads:
+        load.start()
     bias_ref[0] = band_bias(0, 0)
     bias_ref[1] = band_bias(1, 0)
+    for load in loads[:6]:
+        load.wait()
+    left_ref[...], right_ref[...] = by_parity(inner_ref[...], outer_ref[...])
     masks = head_masks(1.0)
     scaled = head_masks(SCALE)
     low_lane = iota((128, 128), 1) < HEAD_DIM
@@ -794,24 +794,37 @@
             copy.start()
 
     over_groups(body, BACKWARD_GROUP)
+    for load in loads[6:]:
+        load.wait()
+    mixed_ref[...] = mm(att_ref[...], w_ref[...], ((1,), (0,))).astype(BF16)
+    mixed_copy = pltpu.make_async_copy(mixed_ref, mixed_out, mixed_sem)
+    mixed_copy.start()
     width = 128 * BACKWARD_GROUP
     for g in range(PAIRS // BACKWARD_GROUP):
         for copy in copies(g, pl.ds(width * g, width)):
             copy.wait()
-
-
-def fine_backward(q, k, v, left, right, da, lse, delta, cdq):
+    mixed_copy.wait()
+
+
+def fine_backward(q, k, v, inner, outer, da, att, w, lse, delta, cdq):
     out = ((TOKENS, HIDDEN), BF16)
     return local_call(
         fine_backward_kernel,
-        [out, out, out],
-        (q, k, v, left, right, da, lse, delta, cdq),
-        5 * 16 * 2 * 256 * 256 * 128,
+        [out, out, out, out],
+        (q, k, v, inner, outer, da, att, w, lse, delta, cdq),
+        5 * 16 * 2 * 256 * 256 * 128 + 2 * 256 * 1024 * 1024,
         scratch=[pltpu.VMEM((2, 256, 256), F32)]
-        + [pltpu.VMEM((TOKENS, HIDDEN), BF16)] * 3
-        + [pltpu.SemaphoreType.DMA((3, PAIRS // BACKWARD_GROUP))],
+        + [pltpu.VMEM((TOKENS, HIDDEN), BF16)] * 9
+        + [pltpu.VMEM((HIDDEN, HIDDEN), BF16)]
+        + [pltpu.VMEM((2 * BLOCK, HIDDEN), BF16)] * 4
+        + [
+            pltpu.SemaphoreType.DMA((3, PAIRS // BACKWARD_GROUP)),
+            pltpu.SemaphoreType.DMA((8,)),
+            pltpu.SemaphoreType.DMA,
+        ],
         exps=16 * 256 * 256,
-        far_out=(0, 1, 2),
+        far_in=tuple(range(8)),
+        far_out=(0, 1, 2, 3),
     )
 
 
@@ -988,20 +1001,17 @@
     peer_cot = swap(cot, "dp", 1)
     *inside, d_att = inside_forward(q, k, v, cot, out_weight)
     rim = rim_forward(q, k, v, inner, outer)
-    att, lse, delta, cdq, packed, own_rows, near_rows, give, near_w = join(
-        cq, coarse_kv, inside, rim, d_att, out_weight
+    att, lse, delta, cdq, packed, own_rows, near_rows, give, to_inner, to_outer = join(
+        cq, coarse_kv, inside, rim, d_att, q, inner, outer
     )
     got = swap(give, "dp", 1)
-    mixed = jnp.dot(att, near_w, preferred_element_type=F32).astype(BF16)
-    send_back = weight_terms(att, got, cot, peer_cot, packed)
+    from_outer = swap_outer(to_outer)
+    from_inner = swap_inner(to_inner)
+    send_back, far_att = weight_terms(att, got, cot, peer_cot, packed)
     back = exchanged(send_back, SLOT)
     near_rows = swap(near_rows, "seq", 2)
-    to_inner, to_outer, *near = edge_backward(q, d_att, k, v, inner, outer, lse, delta)
-    from_outer = swap_outer(to_outer)
-    from_inner = swap_inner(to_inner)
-    near_q, near_da, near_k, near_v, near_left, near_right = near
-    gq, dk, dv = fine_backward(
-        near_q, near_k, near_v, near_left, near_right, near_da, lse, delta, cdq
+    gq, dk, dv, mixed = fine_backward(
+        q, k, v, inner, outer, d_att, far_att, out_weight, lse, delta, cdq
     )
     sums, mine, to_low, to_high, to_both, dk, dv = all_sums(
         back, near_rows, own_rows, dk, dv

time: 84 us -> 87.9 us (1.046)
  the two profiles are of different devices: /device:TPU:0 before, /device:TPU:32 now
where the time goes in v3:
time: 87.9 us; the launch traced here: 87.6 us
  starting transfers between devices  30.3 us (34%)
  Pallas kernels  28.7 us (33%)
  waiting for transfers between devices  26.4 us (30%)
    pallas_call x9, Pallas kernels, local_call(): pl.pallas_call(kernel, in_specs=[far if i in far_in else near for i in ra...  28.7 us
    all_to_all x2, starting transfers between devices, exchanged(): lax.all_to_all(x.reshape(16, rows, HIDDEN), 'seq', split_axis=0, concat_a...  15 us
    all_to_all x2, waiting for transfers between devices, exchanged(): lax.all_to_all(x.reshape(16, rows, HIDDEN), 'seq', split_axis=0, concat_a...  12.5 us
    ppermute x8, waiting for transfers between devices, swap(): lax.ppermute(x, axis, [(i, i ^ bit) for i in range(lax.axis_size(axis))])  10.1 us
    ppermute x8, starting transfers between devices, swap(): lax.ppermute(x, axis, [(i, i ^ bit) for i in range(lax.axis_size(axis))])  8.46 us
    ppermute x2, starting transfers between devices, swap_outer(): lax.ppermute(x, 'seq', [(i, i + 1 if i % 2 else i - 1) for i in range(1,...  6.78 us
    ppermute x2, waiting for transfers between devices, swap_outer(): lax.ppermute(x, 'seq', [(i, i + 1 if i % 2 else i - 1) for i in range(1,...  3.79 us
  transfers between devices with their start and end apart: 13, of which 5 were waited for; matrix products, arithmetic and copies ran while one was open for 1% of the time, Pallas kernels for 24%

profile of v3, /device:TPU:32, one launch (start us, length us, event | category | flops | bytes accessed | tf_op | source)
XLA Modules:
  0.0 87.6 jit_solution(9420872266296908522)
XLA Ops:
  0.6 0.0 copy-start.3
  0.6 0.0 copy-start
  0.7 0.0 copy-start.1
  0.7 0.0 copy-start.2
  0.7 2.7 %shard_map.92 = (bf16[24,1024]{1,0:T(8,128)(2,1)S(1)}, bf16[8,1024]{1,0:T(8,128)(2,1)S(1)}, bf16[128,1024]{1,0:T(8,128)(2,1)}, bf16[128,1024]{1,0:T(8,128)(2,1)}) custom-call(bf16[256,1024]{1,0:T(8,128)(2,1)} %bitcast.13, bf16[256,1024]{1,0:T(8,128)(2,1)} %bitcast.18, bf16[256,1024]{1,0:T(8,128)(2,1)} %bitcast.22), custom_call_target="tpu_custom_call" | custom-call | flops 786432 | bytes 1048576 | tf_op jit(solution)/shard_map/pallas_call | solution.py:40
  3.4 1.6 %collective-permute-start.2 = (bf16[24,1024]{1,0:T(8,128)(2,1)S(1)}, bf16[24,1024]{1,0:T(8,128)(2,1)S(1)}, u32[]{:S(2)}, u32[]{:S(2)}) collective-permute-start(bf16[24,1024]{1,0:T(8,128)(2,1)S(1)} %get-tuple-element.43.own_ref), channel_id=1, source_target_pairs={{0,1},{1,0},{2,3},{3,2},{4,5},{5,4},{6,7},{7,6},{8,9},{9,8},{10,11... | collective-permute-start | bytes 147464 | tf_op jit(solution)/shard_map/ppermute | solution.py:963
  4.9 2.6 %collective-permute-done.2.peer_ref = bf16[24,1024]{1,0:T(8,128)(2,1)S(1)} collective-permute-done((bf16[24,1024]{1,0:T(8,128)(2,1)S(1)}, bf16[24,1024]{1,0:T(8,128)(2,1)S(1)}, u32[]{:S(2)}, u32[]{:S(2)}) %collective-permute-start.2) | collective-permute-done | bytes 49184 | tf_op jit(solution)/shard_map/ppermute | solution.py:963
  7.5 0.8 shard_map.94
  8.4 8.1 %all-to-all-start = ((bf16[16,16,1024]{2,1,0:T(8,128)(2,1)}), bf16[16,16,1024]{2,1,0:T(8,128)(2,1)S(1)}, u32[]{:S(2)}, u32[]{:S(2)}) async-start(bf16[16,16,1024]{2,1,0:T(8,128)(2,1)} %bitcast.30), calls=%async_computation | async-start | bytes 1048576 | tf_op jit(solution)/shard_map/all_to_all | solution.py:983
  16.5 1.5 %collective-permute-start = (bf16[128,1024]{1,0:T(8,128)(2,1)}, bf16[128,1024]{1,0:T(8,128)(2,1)S(1)}, u32[]{:S(2)}, u32[]{:S(2)}) collective-permute-start(bf16[128,1024]{1,0:T(8,128)(2,1)} %get-tuple-element.39), channel_id=1, source_target_pairs={{0,1},{1,0},{2,3},{3,2},{4,5},{5,4},{6,7},{7,6},{8,9},{9,8},{10,11... | collective-permute-start | bytes 786440 | tf_op jit(solution)/shard_map/ppermute | solution.py:963
  17.9 2.0 %collective-permute-start.1 = (bf16[128,1024]{1,0:T(8,128)(2,1)}, bf16[128,1024]{1,0:T(8,128)(2,1)S(1)}, u32[]{:S(2)}, u32[]{:S(2)}) collective-permute-start(bf16[128,1024]{1,0:T(8,128)(2,1)} %get-tuple-element.40), channel_id=1, source_target_pairs={{1,2},{2,1},{3,4},{4,3},{5,6},{6,5},{7,8},{8,7},{9,10},{10,9},{11,... | collective-permute-start | bytes 786440 | tf_op jit(solution)/shard_map/ppermute | solution.py:972
  20.0 0.0 copy-done.3
  20.0 0.1 collective-permute-start.4
  20.1 0.0 copy-done
  20.1 0.0 copy-done.1
  20.1 0.0 copy-done.2
  20.1 5.0 %shard_map.93 = (bf16[128,1024]{1,0:T(8,128)(2,1)}, f32[128,128]{1,0:T(8,128)}, bf16[256,1024]{1,0:T(8,128)(2,1)}) custom-call(bf16[256,1024]{1,0:T(8,128)(2,1)S(1)} %bitcast.16, bf16[256,1024]{1,0:T(8,128)(2,1)S(1)} %bitcast.20, bf16[256,1024]{1,0:T(8,128)(2,1)S(1)} %bitcast.24, bf16[256,1024]{1,0:T(8,128)(2,1)S(1)} %bitcast.27, bf16[1024,1024]{1,0:T(8,128)(2,1)} %w_hbm.3), custom_call_target="tpu_custom_call" | custom-call | flops 939524096 | bytes 1048576 | tf_op jit(solution)/shard_map/pallas_call | solution.py:40
  25.1 0.0 collective-permute-done.inner_ref.inner_hbm
  25.1 0.0 copy-start.4
  25.2 3.8 %collective-permute-done.1.outer_ref.outer_hbm = bf16[128,1024]{1,0:T(8,128)(2,1)S(1)} collective-permute-done((bf16[128,1024]{1,0:T(8,128)(2,1)}, bf16[128,1024]{1,0:T(8,128)(2,1)S(1)}, u32[]{:S(2)}, u32[]{:S(2)}) %collective-permute-start.1) | collective-permute-done | bytes 262176 | tf_op jit(solution)/shard_map/ppermute | solution.py:972
  28.9 2.2 %shard_map.95 = (bf16[128,1024]{1,0:T(8,128)(2,1)}, f32[128,128]{1,0:T(8,128)}) custom-call(bf16[256,1024]{1,0:T(8,128)(2,1)S(1)} %bitcast.17, bf16[256,1024]{1,0:T(8,128)(2,1)S(1)} %bitcast.21, bf16[256,1024]{1,0:T(8,128)(2,1)S(1)} %bitcast.25, bf16[128,1024]{1,0:T(8,128)(2,1)S(1)} %collective-permute-done.inner_ref.inner_hbm, ...), custom_call_target="tpu_custom_call" | custom-call | flops 301989888 | bytes 1048576 | tf_op jit(solution)/shard_map/pallas_call | solution.py:40
  31.2 0.0 copy-start.5
  31.2 0.7 copy-done.5
  31.9 0.0 all-to-all-done
  31.9 0.0 copy-done.4
  31.9 6.4 %shard_map.96 = (bf16[256,1024]{1,0:T(8,128)(2,1)S(1)}, f32[8,2,256]{2,1,0:T(2,128)S(1)}, f32[8,2,256]{2,1,0:T(2,128)S(1)}, f32[8,1024]{1,0:T(8,128)S(1)}, bf16[...) custom-call(bf16[8,1024]{1,0:T(8,128)(2,1)S(1)} %get-tuple-element.4, ...), custom_call_target="tpu_custom_call" | custom-call | flops 335544320 | bytes 1048576 | tf_op jit(solution)/shard_map/pallas_call | solution.py:40
  38.4 0.1 collective-permute-start.3
  38.5 0.0 collective-permute-done.4.peer_cot_ref
  38.5 1.5 %collective-permute-done.3.got_ref = bf16[256,512]{1,0:T(8,128)(2,1)S(1)} collective-permute-done((bf16[256,512]{1,0:T(8,128)(2,1)S(1)}, bf16[256,512]{1,0:T(8,128)(2,1)S(1)}, u32[]{:S(2)}, u32[]{:S(2)}) %collective-permute-start.3) | collective-permute-done | bytes 262176 | tf_op jit(solution)/shard_map/ppermute | solution.py:963
  40.0 1.9 %shard_map.97 = (bf16[640,1024]{1,0:T(8,128)(2,1)}, bf16[256,1024]{1,0:T(8,128)(2,1)}) custom-call(bf16[256,1024]{1,0:T(8,128)(2,1)S(1)} %get-tuple-element.48.att_ref, bf16[256,512]{1,0:T(8,128)(2,1)S(1)} %collective-permute-done.3.got_ref, bf16[256,1024]{1,0:T(8,128)(2,1)S(1)} %bitcast.28, bf16[256,1024]{1,0:T(8,128)(2,1)S(1)} %collective-permute-done.4.peer_cot_ref, ...), custom_call_target="tpu_custom_call" | custom-call | flops 536870912 | bytes 1048576 | tf_op jit(solution)/shard_map/pallas_call | solution.py:40
  42.0 7.0 %all-to-all-start.1 = ((bf16[16,40,1024]{2,1,0:T(8,128)(2,1)}), bf16[16,40,1024]{2,1,0:T(8,128)(2,1)S(1)}, u32[]{:S(2)}, u32[]{:S(2)}) async-start(bf16[16,40,1024]{2,1,0:T(8,128)(2,1)} %bitcast.7), calls=%async_computation.1 | async-start | bytes 2621440 | tf_op jit(solution)/shard_map/all_to_all | solution.py:983
  48.9 0.2 collective-permute-start.5
  49.1 7.0 %shard_map.98 = (bf16[256,1024]{1,0:T(8,128)(2,1)}, bf16[256,1024]{1,0:T(8,128)(2,1)}, bf16[256,1024]{1,0:T(8,128)(2,1)}, bf16[256,1024]{1,0:T(8,128)(2,1)}) custom-call(bf16[256,1024]{1,0:T(8,128)(2,1)} %bitcast.15, bf16[256,1024]{1,0:T(8,128)(2,1)} %bitcast.19, bf16[256,1024]{1,0:T(8,128)(2,1)} %bitcast.23, bf16[128,1024]{1,0:T(8,128)(2,1)} %copy-done.4, ...), custom_call_target="tpu_custom_call" | custom-call | flops 1879048192 | bytes 1048576 | tf_op jit(solution)/shard_map/pallas_call | solution.py:40
  56.1 0.0 collective-permute-done.5.near_ref
  56.1 12.5 %all-to-all-done.1 = bf16[16,40,1024]{2,1,0:T(8,128)(2,1)S(1)} async-done(((bf16[16,40,1024]{2,1,0:T(8,128)(2,1)}), bf16[16,40,1024]{2,1,0:T(8,128)(2,1)S(1)}, u32[]{:S(2)}, u32[]{:S(2)}) %all-to-all-start.1) | async-done | bytes 1310752 | tf_op jit(solution)/shard_map/all_to_all | solution.py:983
  68.6 1.5 %shard_map.99 = (f32[16,1024]{1,0:T(8,128)S(1)}, f32[8,1024]{1,0:T(8,128)S(1)}, bf16[24,1024]{1,0:T(8,128)(2,1)S(1)}, bf16[8,1024]{1,0:T(8,128)(2,1)S(1)}, bf16[...) custom-call(bf16[640,1024]{1,0:T(8,128)(2,1)S(1)} %bitcast.12, ...), custom_call_target="tpu_custom_call" | custom-call | flops 83886080 | bytes 1048576 | tf_op jit(solution)/shard_map/pallas_call | solution.py:40
  70.1 2.1 %collective-permute-start.6 = (bf16[24,1024]{1,0:T(8,128)(2,1)S(1)}, bf16[24,1024]{1,0:T(8,128)(2,1)S(1)}, u32[]{:S(2)}, u32[]{:S(2)}) collective-permute-start(bf16[24,1024]{1,0:T(8,128)(2,1)S(1)} %get-tuple-element.62), channel_id=1, source_target_pairs={{0,1},{1,0},{2,3},{3,2},{4,5},{5,4},{6,7},{7,6},{8,9},{9,8},{10,11... | collective-permute-start | bytes 147464 | tf_op jit(solution)/shard_map/ppermute | solution.py:963
  72.3 0.1 collective-permute-start.9
  72.3 4.7 %collective-permute-start.10 = (bf16[128,1024]{1,0:T(8,128)(2,1)S(1)}, bf16[128,1024]{1,0:T(8,128)(2,1)S(1)}, u32[]{:S(2)}, u32[]{:S(2)}) collective-permute-start(bf16[128,1024]{1,0:T(8,128)(2,1)S(1)} %get-tuple-element.69), channel_id=1, source_target_pairs={{1,2},{2,1},{3,4},{4,3},{5,6},{6,5},{7,8},{8,7},{9,10},{10,9},{11,... | collective-permute-start | bytes 786440 | tf_op jit(solution)/shard_map/ppermute | solution.py:972
  77.1 2.8 %collective-permute-start.7 = (bf16[8,1024]{1,0:T(8,128)(2,1)S(1)}, bf16[8,1024]{1,0:T(8,128)(2,1)S(1)}, u32[]{:S(2)}, u32[]{:S(2)}) collective-permute-start(bf16[8,1024]{1,0:T(8,128)(2,1)S(1)} %get-tuple-element.63), channel_id=1, source_target_pairs={{0,64},{32,96},{64,0},{96,32},{1,65},{33,97},{65,1},{97,33},{2,66}... | collective-permute-start | bytes 49160 | tf_op jit(solution)/shard_map/ppermute | solution.py:963
  79.9 0.0 collective-permute-start.8
  79.9 5.9 %collective-permute-done.7 = bf16[8,1024]{1,0:T(8,128)(2,1)S(1)} collective-permute-done((bf16[8,1024]{1,0:T(8,128)(2,1)S(1)}, bf16[8,1024]{1,0:T(8,128)(2,1)S(1)}, u32[]{:S(2)}, u32[]{:S(2)}) %collective-permute-start.7) | collective-permute-done | bytes 16416 | tf_op jit(solution)/shard_map/ppermute | solution.py:963
  85.8 0.0 collective-permute-done.8
  85.8 0.0 collective-permute-done.6.low_ref
  85.8 0.6 add_add_fusion
  86.5 0.0 collective-permute-done.9.inner_ref
  86.5 0.0 collective-permute-done.10.outer_ref
  86.5 1.1 %shard_map.100 = (bf16[256,1024]{1,0:T(8,128)(2,1)}, bf16[256,1024]{1,0:T(8,128)(2,1)}) custom-call(bf16[256,1024]{1,0:T(8,128)(2,1)S(1)} %get-tuple-element.66.dk_ref, bf16[256,1024]{1,0:T(8,128)(2,1)S(1)} %get-tuple-element.67.dv_ref, bf16[128,1024]{1,0:T(8,128)(2,1)S(1)} %collective-permute-done.9.inner_ref, ...), custom_call_target="tpu_custom_call" | custom-call | flops 4194304 | bytes 1048576 | tf_op jit(solution)/shard_map/pallas_call | solution.py:40
Async XLA Ops:
  0.6 19.4 %copy-start.3 = (bf16[1,256,1024]{2,1,0:T(8,128)(2,1)S(1)}, bf16[1,256,1024]{2,1,0:T(8,128)(2,1)}, u32[]{:S(2)}) copy-start(bf16[1,256,1024]{2,1,0:T(8,128)(2,1)} %param.9) | copy-start | bytes 1572868
  0.6 19.5 %copy-start = (bf16[1,256,1024]{2,1,0:T(8,128)(2,1)S(1)}, bf16[1,256,1024]{2,1,0:T(8,128)(2,1)}, u32[]{:S(2)}) copy-start(bf16[1,256,1024]{2,1,0:T(8,128)(2,1)} %param.5) | copy-start | bytes 1572868
  0.7 19.5 %copy-start.1 = (bf16[1,256,1024]{2,1,0:T(8,128)(2,1)S(1)}, bf16[1,256,1024]{2,1,0:T(8,128)(2,1)}, u32[]{:S(2)}) copy-start(bf16[1,256,1024]{2,1,0:T(8,128)(2,1)} %param.6) | copy-start | bytes 1572868
  0.7 19.5 %copy-start.2 = (bf16[1,256,1024]{2,1,0:T(8,128)(2,1)S(1)}, bf16[1,256,1024]{2,1,0:T(8,128)(2,1)}, u32[]{:S(2)}) copy-start(bf16[1,256,1024]{2,1,0:T(8,128)(2,1)} %param.7) | copy-start | bytes 1572868
  3.4 4.2 %collective-permute-start.2 = (bf16[24,1024]{1,0:T(8,128)(2,1)S(1)}, bf16[24,1024]{1,0:T(8,128)(2,1)S(1)}, u32[]{:S(2)}, u32[]{:S(2)}) collective-permute-start(bf16[24,1024]{1,0:T(8,128)(2,1)S(1)} %get-tuple-element.43.own_ref), channel_id=1, source_target_pairs={{0,1},{1,0},{2,3},{3,2},{4,5},{5,4},{6,7},{7,6},{8,9},{9,8},{10,11... | collective-permute-start | bytes 147464 | tf_op jit(solution)/shard_map/ppermute | solution.py:963
  8.4 23.6 %all-to-all-start = ((bf16[16,16,1024]{2,1,0:T(8,128)(2,1)}), bf16[16,16,1024]{2,1,0:T(8,128)(2,1)S(1)}, u32[]{:S(2)}, u32[]{:S(2)}) async-start(bf16[16,16,1024]{2,1,0:T(8,128)(2,1)} %bitcast.30), calls=%async_computation | async-start | bytes 1048576 | tf_op jit(solution)/shard_map/all_to_all | solution.py:983
  16.5 8.7 %collective-permute-start = (bf16[128,1024]{1,0:T(8,128)(2,1)}, bf16[128,1024]{1,0:T(8,128)(2,1)S(1)}, u32[]{:S(2)}, u32[]{:S(2)}) collective-permute-start(bf16[128,1024]{1,0:T(8,128)(2,1)} %get-tuple-element.39), channel_id=1, source_target_pairs={{0,1},{1,0},{2,3},{3,2},{4,5},{5,4},{6,7},{7,6},{8,9},{9,8},{10,11... | collective-permute-start | bytes 786440 | tf_op jit(solution)/shard_map/ppermute | solution.py:963
  17.9 11.0 %collective-permute-start.1 = (bf16[128,1024]{1,0:T(8,128)(2,1)}, bf16[128,1024]{1,0:T(8,128)(2,1)S(1)}, u32[]{:S(2)}, u32[]{:S(2)}) collective-permute-start(bf16[128,1024]{1,0:T(8,128)(2,1)} %get-tuple-element.40), channel_id=1, source_target_pairs={{1,2},{2,1},{3,4},{4,3},{5,6},{6,5},{7,8},{8,7},{9,10},{10,9},{11,... | collective-permute-start | bytes 786440 | tf_op jit(solution)/shard_map/ppermute | solution.py:972
  20.0 18.5 %collective-permute-start.4 = (bf16[256,1024]{1,0:T(8,128)(2,1)S(1)}, bf16[256,1024]{1,0:T(8,128)(2,1)S(1)}, u32[]{:S(2)}, u32[]{:S(2)}) collective-permute-start(bf16[256,1024]{1,0:T(8,128)(2,1)S(1)} %bitcast.26), channel_id=1, source_target_pairs={{0,32},{32,0},{64,96},{96,64},{1,33},{33,1},{65,97},{97,65},{2,34}... | collective-permute-start | bytes 1572872 | tf_op jit(solution)/shard_map/ppermute | solution.py:963
  25.1 6.8 %copy-start.4 = (bf16[128,1024]{1,0:T(8,128)(2,1)}, bf16[128,1024]{1,0:T(8,128)(2,1)S(1)}, u32[]{:S(2)}) copy-start(bf16[128,1024]{1,0:T(8,128)(2,1)S(1)} %collective-permute-done.inner_ref.inner_hbm) | copy-start | bytes 786436
  31.2 0.7 copy-start.5
  38.4 1.6 %collective-permute-start.3 = (bf16[256,512]{1,0:T(8,128)(2,1)S(1)}, bf16[256,512]{1,0:T(8,128)(2,1)S(1)}, u32[]{:S(2)}, u32[]{:S(2)}) collective-permute-start(bf16[256,512]{1,0:T(8,128)(2,1)S(1)} %get-tuple-element.49), channel_id=1, source_target_pairs={{0,32},{32,0},{64,96},{96,64},{1,33},{33,1},{65,97},{97,65},{2,34}... | collective-permute-start | bytes 786440 | tf_op jit(solution)/shard_map/ppermute | solution.py:963
  42.0 26.7 %all-to-all-start.1 = ((bf16[16,40,1024]{2,1,0:T(8,128)(2,1)}), bf16[16,40,1024]{2,1,0:T(8,128)(2,1)S(1)}, u32[]{:S(2)}, u32[]{:S(2)}) async-start(bf16[16,40,1024]{2,1,0:T(8,128)(2,1)} %bitcast.7), calls=%async_computation.1 | async-start | bytes 2621440 | tf_op jit(solution)/shard_map/all_to_all | solution.py:983
  48.9 7.2 %collective-permute-start.5 = (bf16[16,1024]{1,0:T(8,128)(2,1)S(1)}, bf16[16,1024]{1,0:T(8,128)(2,1)S(1)}, u32[]{:S(2)}, u32[]{:S(2)}) collective-permute-start(bf16[16,1024]{1,0:T(8,128)(2,1)S(1)} %get-tuple-element.57), channel_id=1, source_target_pairs={{0,2},{1,3},{2,0},{3,1},{4,6},{5,7},{6,4},{7,5},{8,10},{9,11},{10,... | collective-permute-start | bytes 98312 | tf_op jit(solution)/shard_map/ppermute | solution.py:963
  70.1 15.7 %collective-permute-start.6 = (bf16[24,1024]{1,0:T(8,128)(2,1)S(1)}, bf16[24,1024]{1,0:T(8,128)(2,1)S(1)}, u32[]{:S(2)}, u32[]{:S(2)}) collective-permute-start(bf16[24,1024]{1,0:T(8,128)(2,1)S(1)} %get-tuple-element.62), channel_id=1, source_target_pairs={{0,1},{1,0},{2,3},{3,2},{4,5},{5,4},{6,7},{7,6},{8,9},{9,8},{10,11... | collective-permute-start | bytes 147464 | tf_op jit(solution)/shard_map/ppermute | solution.py:963
  72.3 14.2 %collective-permute-start.9 = (bf16[128,1024]{1,0:T(8,128)(2,1)S(1)}, bf16[128,1024]{1,0:T(8,128)(2,1)S(1)}, u32[]{:S(2)}, u32[]{:S(2)}) collective-permute-start(bf16[128,1024]{1,0:T(8,128)(2,1)S(1)} %get-tuple-element.68), channel_id=1, source_target_pairs={{0,1},{1,0},{2,3},{3,2},{4,5},{5,4},{6,7},{7,6},{8,9},{9,8},{10,11... | collective-permute-start | bytes 786440 | tf_op jit(solution)/shard_map/ppermute | solution.py:963
  72.3 14.1 %collective-permute-start.10 = (bf16[128,1024]{1,0:T(8,128)(2,1)S(1)}, bf16[128,1024]{1,0:T(8,128)(2,1)S(1)}, u32[]{:S(2)}, u32[]{:S(2)}) collective-permute-start(bf16[128,1024]{1,0:T(8,128)(2,1)S(1)} %get-tuple-element.69), channel_id=1, source_target_pairs={{1,2},{2,1},{3,4},{4,3},{5,6},{6,5},{7,8},{8,7},{9,10},{10,9},{11,... | collective-permute-start | bytes 786440 | tf_op jit(solution)/shard_map/ppermute | solution.py:972
  77.1 8.7 %collective-permute-start.7 = (bf16[8,1024]{1,0:T(8,128)(2,1)S(1)}, bf16[8,1024]{1,0:T(8,128)(2,1)S(1)}, u32[]{:S(2)}, u32[]{:S(2)}) collective-permute-start(bf16[8,1024]{1,0:T(8,128)(2,1)S(1)} %get-tuple-element.63), channel_id=1, source_target_pairs={{0,64},{32,96},{64,0},{96,32},{1,65},{33,97},{65,1},{97,33},{2,66}... | collective-permute-start | bytes 49160 | tf_op jit(solution)/shard_map/ppermute | solution.py:963
  79.9 5.9 %collective-permute-start.8 = (bf16[8,1024]{1,0:T(8,128)(2,1)S(1)}, bf16[8,1024]{1,0:T(8,128)(2,1)S(1)}, u32[]{:S(2)}, u32[]{:S(2)}) collective-permute-start(bf16[8,1024]{1,0:T(8,128)(2,1)S(1)} %get-tuple-element.64), channel_id=1, source_target_pairs={{0,65},{1,64},{2,67},{3,66},{4,69},{5,68},{6,71},{7,70},{8,73},{9,... | collective-permute-start | bytes 49160 | tf_op jit(solution)/shard_map/ppermute | solution.py:978

commit v4 on v3

--- a/solution.py
+++ b/solution.py
@@ -56,62 +56,49 @@
     return [[x / root for x in rows] for rows, root in zip((one, two, three), ROOTS)]
 
 
-def pool_kernel(
-    q_ref, k_ref, v_ref, levels_ref, cq_ref, inner_ref, outer_ref, held_ref, sems, edge_sems
-):
+def pool_kernel(k_hbm, v_hbm, levels_ref, inner_ref, outer_ref, k_ref, v_ref, sems):
     me = lax.axis_index("seq")
-    copies = {}
-    for i, ref in ((1, k_ref), (2, v_ref), (0, q_ref)):
-        for b in range(4):
-            rows = pl.ds(BLOCK * b, BLOCK)
-            copies[i, b] = pltpu.make_async_copy(ref.at[rows], held_ref.at[i, rows], sems.at[i, b])
-            copies[i, b].start()
+    copies = [
+        pltpu.make_async_copy(k_hbm, k_ref, sems.at[0]),
+        pltpu.make_async_copy(v_hbm, v_ref, sems.at[1]),
+    ]
+    for copy in copies:
+        copy.start()
     inner = pl.multiple_of((1 - me % 2) * (TOKENS - BLOCK), BLOCK)
     outer = pl.multiple_of((me % 2) * (TOKENS - BLOCK), BLOCK)
-    edges = []
-    for i, ref in enumerate((k_ref, v_ref)):
-        to = pl.ds(BLOCK * i, BLOCK)
-        for j, (start, out) in enumerate(((inner, inner_ref), (outer, outer_ref))):
-            edges.append(
-                pltpu.make_async_copy(ref.at[pl.ds(start, BLOCK)], out.at[to], edge_sems.at[i, j])
-            )
-    for copy in edges:
-        copy.start()
-
-    def sums(i):
-        parts = []
-        for b in range(4):
-            copies[i, b].wait()
-            rows = held_ref[i, BLOCK * b : BLOCK * (b + 1), :].astype(F32)
-            parts.append(jnp.sum(rows, axis=0, keepdims=True))
-        return parts
+
+    def sums(i, ref):
+        copies[i].wait()
+        to = slice(BLOCK * i, BLOCK * (i + 1))
+        inner_ref[to, :] = ref[pl.ds(inner, BLOCK), :]
+        outer_ref[to, :] = ref[pl.ds(outer, BLOCK), :]
+        return [
+            jnp.sum(ref[BLOCK * b : BLOCK * (b + 1), :].astype(F32), axis=0, keepdims=True)
+            for b in range(4)
+        ]
 
     zero = jnp.zeros((1, HIDDEN), F32)
-    k1, k2, k3 = pooled_levels(sums(1))
-    v1, v2, v3 = pooled_levels(sums(2))
+    k1, k2, k3 = pooled_levels(sums(0, k_ref))
+    v1, v2, v3 = pooled_levels(sums(1, v_ref))
     slot1 = jnp.concatenate(k1 + v1, axis=0)
     slot2 = jnp.concatenate(k2 + [zero] * 2 + v2 + [zero] * 2, axis=0)
     slot3 = jnp.concatenate(k3 + [zero] * 3 + v3 + [zero] * 3, axis=0)
     levels_ref[...] = jnp.concatenate([slot1, slot2, slot3], axis=0).astype(BF16)
-    q1, q2, q3 = pooled_levels(sums(0))
-    cq_ref[...] = jnp.concatenate(q1 + q2 + q3 + [zero], axis=0).astype(BF16)
-    for copy in edges:
-        copy.wait()
-
-
-def pool(q, k, v):
+
+
+def pool(k, v):
     slab = ((2 * BLOCK, HIDDEN), BF16)
     return local_call(
         pool_kernel,
-        [((24, HIDDEN), BF16), ((LEVEL_ROWS, HIDDEN), BF16), slab, slab],
-        (q, k, v),
-        3 * 256 * 1024,
+        [((24, HIDDEN), BF16), slab, slab],
+        (k, v),
+        2 * 256 * 1024,
         scratch=[
-            pltpu.VMEM((3, TOKENS, HIDDEN), BF16),
-            pltpu.SemaphoreType.DMA((3, 4)),
-            pltpu.SemaphoreType.DMA((2, 2)),
+            pltpu.VMEM((TOKENS, HIDDEN), BF16),
+            pltpu.VMEM((TOKENS, HIDDEN), BF16),
+            pltpu.SemaphoreType.DMA((2,)),
         ],
-        far_in=(0, 1, 2),
+        far_in=(0, 1),
     )
 
 
@@ -227,6 +214,7 @@
     a_out,
     lse_out,
     da_out,
+    cq_ref,
     a_ref,
     lse_ref,
     w_ref,
@@ -273,6 +261,14 @@
         da_copy(g, span).start()
 
     over_groups(body, FORWARD_GROUP)
+    q1, q2, q3 = pooled_levels(
+        [
+            jnp.sum(q_ref[BLOCK * b : BLOCK * (b + 1), :].astype(F32), axis=0, keepdims=True)
+            for b in range(4)
+        ]
+    )
+    zero = jnp.zeros((1, HIDDEN), F32)
+    cq_ref[...] = jnp.concatenate(q1 + q2 + q3 + [zero], axis=0).astype(BF16)
     lse_copy = pltpu.make_async_copy(lse_ref, lse_out, lse_sem)
     lse_copy.start()
     for g in range(steps):
@@ -285,7 +281,12 @@
     steps = PAIRS // FORWARD_GROUP
     return local_call(
         inside_kernel,
-        [((128, HIDDEN), BF16), ((128, 128), F32), ((TOKENS, HIDDEN), BF16)],
+        [
+            ((128, HIDDEN), BF16),
+            ((128, 128), F32),
+            ((TOKENS, HIDDEN), BF16),
+            ((LEVEL_ROWS, HIDDEN), BF16),
+        ],
         (q, k, v, cot, w),
         3 * 16 * 2 * 128 * 256 * 128 + 2 * 256 * 1024 * 1024,
         scratch=[
@@ -574,11 +575,6 @@
                 )
         g_ref[:, lanes] = rows_of(g_parts)
         h_ref[:, lanes] = rows_of(h_parts)
-    for load in edge_loads:
-        load.wait()
-    left_ref[...], right_ref[...] = by_parity(inner_ref[...], outer_ref[...])
-    edge_terms(q_ref, da_ref, lse_ref, delta_ref, left_ref, right_ref, to_left_ref, to_right_ref)
-    to_inner_ref[...], to_outer_ref[...] = by_parity(to_left_ref[...], to_right_ref[...])
     core = lax.axis_index("dp") % 2
     for hi in range(2):
         start = pl.multiple_of((2 * hi + 1 - core) * 256, 256)
@@ -590,6 +586,11 @@
     row = iota((LEVEL_ROWS, 1), 0)
     share = jnp.where(row < 4, 1.0 / ROOTS[0], jnp.where(row < 6, 1.0 / ROOTS[1], 1.0 / ROOTS[2]))
     dq_ref[...] = over_heads(mm(score_grad, kv, ((1,), (0,))), own) * (share.astype(F32) * SCALE)
+    for load in edge_loads:
+        load.wait()
+    left_ref[...], right_ref[...] = by_parity(inner_ref[...], outer_ref[...])
+    edge_terms(q_ref, da_ref, lse_ref, delta_ref, left_ref, right_ref, to_left_ref, to_right_ref)
+    to_inner_ref[...], to_outer_ref[...] = by_parity(to_left_ref[...], to_right_ref[...])
     left = jnp.concatenate([score_grad, on_values], axis=0)
     right = jnp.concatenate([query, grads], axis=0)
     dkv = mm(left, right, ((0,), (0,))).astype(BF16)
@@ -992,14 +993,14 @@
 
 
 def body(q, k, v, out_weight, cot):
-    levels, cq, inner, outer = pool(q, k, v)
+    levels, inner, outer = pool(k, v)
     peer_levels = swap(levels, "seq", 1)
     outer = swap_outer(outer)
     inner = swap_inner(inner)
     send = slots(levels, peer_levels)
     coarse_kv = exchanged(send, 16)
     peer_cot = swap(cot, "dp", 1)
-    *inside, d_att = inside_forward(q, k, v, cot, out_weight)
+    *inside, d_att, cq = inside_forward(q, k, v, cot, out_weight)
     rim = rim_forward(q, k, v, inner, outer)
     att, lse, delta, cdq, packed, own_rows, near_rows, give, to_inner, to_outer = join(
         cq, coarse_kv, inside, rim, d_att, q, inner, outer

time: 87.9 us -> 87.2 us (level)
  no operation moved by 1% of the time
where the time goes in v4:
time: 87.2 us; the launch traced here: 86.9 us
  starting transfers between devices  30.3 us (35%)
  Pallas kernels  28 us (32%)
  waiting for transfers between devices  26.4 us (30%)
    pallas_call x9, Pallas kernels, local_call(): pl.pallas_call(kernel, in_specs=[far if i in far_in else near for i in ra...  28 us
    all_to_all x2, starting transfers between devices, exchanged(): lax.all_to_all(x.reshape(16, rows, HIDDEN), 'seq', split_axis=0, concat_a...  15 us
    all_to_all x2, waiting for transfers between devices, exchanged(): lax.all_to_all(x.reshape(16, rows, HIDDEN), 'seq', split_axis=0, concat_a...  12.5 us
    ppermute x8, waiting for transfers between devices, swap(): lax.ppermute(x, axis, [(i, i ^ bit) for i in range(lax.axis_size(axis))])  10.1 us
    ppermute x8, starting transfers between devices, swap(): lax.ppermute(x, axis, [(i, i ^ bit) for i in range(lax.axis_size(axis))])  8.46 us
    ppermute x2, starting transfers between devices, swap_outer(): lax.ppermute(x, 'seq', [(i, i + 1 if i % 2 else i - 1) for i in range(1,...  6.77 us
    ppermute x2, waiting for transfers between devices, swap_outer(): lax.ppermute(x, 'seq', [(i, i + 1 if i % 2 else i - 1) for i in range(1,...  3.78 us
  transfers between devices with their start and end apart: 13, of which 5 were waited for; matrix products, arithmetic and copies ran while one was open for 1% of the time, Pallas kernels for 24%

profile of v4, /device:TPU:32, one launch (start us, length us, event | category | flops | bytes accessed | tf_op | source)
XLA Modules:
  0.0 86.9 jit_solution(16374766662443510946)
XLA Ops:
  0.6 0.0 copy-start.2
  0.6 0.0 copy-start
  0.7 0.0 copy-start.1
  0.7 0.0 copy-start.3
  0.7 2.2 %shard_map.92 = (bf16[24,1024]{1,0:T(8,128)(2,1)S(1)}, bf16[128,1024]{1,0:T(8,128)(2,1)}, bf16[128,1024]{1,0:T(8,128)(2,1)}) custom-call(bf16[256,1024]{1,0:T(8,128)(2,1)} %bitcast.13, bf16[256,1024]{1,0:T(8,128)(2,1)} %bitcast.17), custom_call_target="tpu_custom_call" | custom-call | flops 524288 | bytes 1048576 | tf_op jit(solution)/shard_map/pallas_call | solution.py:40
  2.8 1.6 %collective-permute-start.2 = (bf16[24,1024]{1,0:T(8,128)(2,1)S(1)}, bf16[24,1024]{1,0:T(8,128)(2,1)S(1)}, u32[]{:S(2)}, u32[]{:S(2)}) collective-permute-start(bf16[24,1024]{1,0:T(8,128)(2,1)S(1)} %get-tuple-element.43.own_ref), channel_id=1, source_target_pairs={{0,1},{1,0},{2,3},{3,2},{4,5},{5,4},{6,7},{7,6},{8,9},{9,8},{10,11... | collective-permute-start | bytes 147464 | tf_op jit(solution)/shard_map/ppermute | solution.py:964
  4.4 2.6 %collective-permute-done.2.peer_ref = bf16[24,1024]{1,0:T(8,128)(2,1)S(1)} collective-permute-done((bf16[24,1024]{1,0:T(8,128)(2,1)S(1)}, bf16[24,1024]{1,0:T(8,128)(2,1)S(1)}, u32[]{:S(2)}, u32[]{:S(2)}) %collective-permute-start.2) | collective-permute-done | bytes 49184 | tf_op jit(solution)/shard_map/ppermute | solution.py:964
  7.0 0.8 shard_map.94
  7.9 8.1 %all-to-all-start = ((bf16[16,16,1024]{2,1,0:T(8,128)(2,1)}), bf16[16,16,1024]{2,1,0:T(8,128)(2,1)S(1)}, u32[]{:S(2)}, u32[]{:S(2)}) async-start(bf16[16,16,1024]{2,1,0:T(8,128)(2,1)} %bitcast.29), calls=%async_computation | async-start | bytes 1048576 | tf_op jit(solution)/shard_map/all_to_all | solution.py:984
  16.0 1.5 %collective-permute-start = (bf16[128,1024]{1,0:T(8,128)(2,1)}, bf16[128,1024]{1,0:T(8,128)(2,1)S(1)}, u32[]{:S(2)}, u32[]{:S(2)}) collective-permute-start(bf16[128,1024]{1,0:T(8,128)(2,1)} %get-tuple-element.39), channel_id=1, source_target_pairs={{0,1},{1,0},{2,3},{3,2},{4,5},{5,4},{6,7},{7,6},{8,9},{9,8},{10,11... | collective-permute-start | bytes 786440 | tf_op jit(solution)/shard_map/ppermute | solution.py:964
  17.4 2.0 %collective-permute-start.1 = (bf16[128,1024]{1,0:T(8,128)(2,1)}, bf16[128,1024]{1,0:T(8,128)(2,1)S(1)}, u32[]{:S(2)}, u32[]{:S(2)}) collective-permute-start(bf16[128,1024]{1,0:T(8,128)(2,1)} %get-tuple-element.40), channel_id=1, source_target_pairs={{1,2},{2,1},{3,4},{4,3},{5,6},{6,5},{7,8},{8,7},{9,10},{10,9},{11,... | collective-permute-start | bytes 786440 | tf_op jit(solution)/shard_map/ppermute | solution.py:973
  19.5 0.0 copy-done.2
  19.5 0.1 collective-permute-start.4
  19.6 0.0 copy-done
  19.6 0.0 copy-done.1
  19.6 0.0 copy-done.3
  19.6 5.0 %shard_map.93 = (bf16[128,1024]{1,0:T(8,128)(2,1)}, f32[128,128]{1,0:T(8,128)}, bf16[256,1024]{1,0:T(8,128)(2,1)}, bf16[8,1024]{1,0:T(8,128)(2,1)S(1)}) custom-call(bf16[256,1024]{1,0:T(8,128)(2,1)S(1)} %bitcast.26, bf16[256,1024]{1,0:T(8,128)(2,1)S(1)} %bitcast.15, bf16[256,1024]{1,0:T(8,128)(2,1)S(1)} %bitcast.19, bf16[256,1024]{1,0:T(8,128)(2,1)S(1)} %bitcast.22, ...), custom_call_target="tpu_custom_call" | custom-call | flops 939524096 | bytes 1048576 | tf_op jit(solution)/shard_map/pallas_call | solution.py:40
  24.6 0.0 collective-permute-done.inner_ref.inner_hbm
  24.6 0.0 copy-start.4
  24.7 3.8 %collective-permute-done.1.outer_ref.outer_hbm = bf16[128,1024]{1,0:T(8,128)(2,1)S(1)} collective-permute-done((bf16[128,1024]{1,0:T(8,128)(2,1)}, bf16[128,1024]{1,0:T(8,128)(2,1)S(1)}, u32[]{:S(2)}, u32[]{:S(2)}) %collective-permute-start.1) | collective-permute-done | bytes 262176 | tf_op jit(solution)/shard_map/ppermute | solution.py:973
  28.4 2.3 %shard_map.95 = (bf16[128,1024]{1,0:T(8,128)(2,1)}, f32[128,128]{1,0:T(8,128)}) custom-call(bf16[256,1024]{1,0:T(8,128)(2,1)S(1)} %bitcast.27, bf16[256,1024]{1,0:T(8,128)(2,1)S(1)} %bitcast.16, bf16[256,1024]{1,0:T(8,128)(2,1)S(1)} %bitcast.20, bf16[128,1024]{1,0:T(8,128)(2,1)S(1)} %collective-permute-done.inner_ref.inner_hbm, ...), custom_call_target="tpu_custom_call" | custom-call | flops 301989888 | bytes 1048576 | tf_op jit(solution)/shard_map/pallas_call | solution.py:40
  30.7 0.0 copy-start.5
  30.7 0.7 copy-done.5
  31.4 0.0 all-to-all-done
  31.4 0.0 copy-done.4
  31.4 6.2 %shard_map.96 = (bf16[256,1024]{1,0:T(8,128)(2,1)S(1)}, f32[8,2,256]{2,1,0:T(2,128)S(1)}, f32[8,2,256]{2,1,0:T(2,128)S(1)}, f32[8,1024]{1,0:T(8,128)S(1)}, bf16[...) custom-call(bf16[8,1024]{1,0:T(8,128)(2,1)S(1)} %get-tuple-element.4, ...), custom_call_target="tpu_custom_call" | custom-call | flops 335544320 | bytes 1048576 | tf_op jit(solution)/shard_map/pallas_call | solution.py:40
  37.7 0.1 collective-permute-start.3
  37.8 0.0 collective-permute-done.4.peer_cot_ref
  37.8 1.5 %collective-permute-done.3.got_ref = bf16[256,512]{1,0:T(8,128)(2,1)S(1)} collective-permute-done((bf16[256,512]{1,0:T(8,128)(2,1)S(1)}, bf16[256,512]{1,0:T(8,128)(2,1)S(1)}, u32[]{:S(2)}, u32[]{:S(2)}) %collective-permute-start.3) | collective-permute-done | bytes 262176 | tf_op jit(solution)/shard_map/ppermute | solution.py:964
  39.3 1.9 %shard_map.97 = (bf16[640,1024]{1,0:T(8,128)(2,1)}, bf16[256,1024]{1,0:T(8,128)(2,1)}) custom-call(bf16[256,1024]{1,0:T(8,128)(2,1)S(1)} %get-tuple-element.48.att_ref, bf16[256,512]{1,0:T(8,128)(2,1)S(1)} %collective-permute-done.3.got_ref, bf16[256,1024]{1,0:T(8,128)(2,1)S(1)} %bitcast.23, bf16[256,1024]{1,0:T(8,128)(2,1)S(1)} %collective-permute-done.4.peer_cot_ref, ...), custom_call_target="tpu_custom_call" | custom-call | flops 536870912 | bytes 1048576 | tf_op jit(solution)/shard_map/pallas_call | solution.py:40
  41.3 7.0 %all-to-all-start.1 = ((bf16[16,40,1024]{2,1,0:T(8,128)(2,1)}), bf16[16,40,1024]{2,1,0:T(8,128)(2,1)S(1)}, u32[]{:S(2)}, u32[]{:S(2)}) async-start(bf16[16,40,1024]{2,1,0:T(8,128)(2,1)} %bitcast.7), calls=%async_computation.1 | async-start | bytes 2621440 | tf_op jit(solution)/shard_map/all_to_all | solution.py:984
  48.2 0.2 collective-permute-start.5
  48.4 7.0 %shard_map.98 = (bf16[256,1024]{1,0:T(8,128)(2,1)}, bf16[256,1024]{1,0:T(8,128)(2,1)}, bf16[256,1024]{1,0:T(8,128)(2,1)}, bf16[256,1024]{1,0:T(8,128)(2,1)}) custom-call(bf16[256,1024]{1,0:T(8,128)(2,1)} %bitcast.25, bf16[256,1024]{1,0:T(8,128)(2,1)} %bitcast.14, bf16[256,1024]{1,0:T(8,128)(2,1)} %bitcast.18, bf16[128,1024]{1,0:T(8,128)(2,1)} %copy-done.4, ...), custom_call_target="tpu_custom_call" | custom-call | flops 1879048192 | bytes 1048576 | tf_op jit(solution)/shard_map/pallas_call | solution.py:40
  55.4 0.0 collective-permute-done.5.near_ref
  55.4 12.5 %all-to-all-done.1 = bf16[16,40,1024]{2,1,0:T(8,128)(2,1)S(1)} async-done(((bf16[16,40,1024]{2,1,0:T(8,128)(2,1)}), bf16[16,40,1024]{2,1,0:T(8,128)(2,1)S(1)}, u32[]{:S(2)}, u32[]{:S(2)}) %all-to-all-start.1) | async-done | bytes 1310752 | tf_op jit(solution)/shard_map/all_to_all | solution.py:984
  67.9 1.5 %shard_map.99 = (f32[16,1024]{1,0:T(8,128)S(1)}, f32[8,1024]{1,0:T(8,128)S(1)}, bf16[24,1024]{1,0:T(8,128)(2,1)S(1)}, bf16[8,1024]{1,0:T(8,128)(2,1)S(1)}, bf16[...) custom-call(bf16[640,1024]{1,0:T(8,128)(2,1)S(1)} %bitcast.12, ...), custom_call_target="tpu_custom_call" | custom-call | flops 83886080 | bytes 1048576 | tf_op jit(solution)/shard_map/pallas_call | solution.py:40
  69.4 2.1 %collective-permute-start.6 = (bf16[24,1024]{1,0:T(8,128)(2,1)S(1)}, bf16[24,1024]{1,0:T(8,128)(2,1)S(1)}, u32[]{:S(2)}, u32[]{:S(2)}) collective-permute-start(bf16[24,1024]{1,0:T(8,128)(2,1)S(1)} %get-tuple-element.62), channel_id=1, source_target_pairs={{0,1},{1,0},{2,3},{3,2},{4,5},{5,4},{6,7},{7,6},{8,9},{9,8},{10,11... | collective-permute-start | bytes 147464 | tf_op jit(solution)/shard_map/ppermute | solution.py:964
  71.6 0.1 collective-permute-start.9
  71.7 4.7 %collective-permute-start.10 = (bf16[128,1024]{1,0:T(8,128)(2,1)S(1)}, bf16[128,1024]{1,0:T(8,128)(2,1)S(1)}, u32[]{:S(2)}, u32[]{:S(2)}) collective-permute-start(bf16[128,1024]{1,0:T(8,128)(2,1)S(1)} %get-tuple-element.69), channel_id=1, source_target_pairs={{1,2},{2,1},{3,4},{4,3},{5,6},{6,5},{7,8},{8,7},{9,10},{10,9},{11,... | collective-permute-start | bytes 786440 | tf_op jit(solution)/shard_map/ppermute | solution.py:973
  76.4 2.8 %collective-permute-start.7 = (bf16[8,1024]{1,0:T(8,128)(2,1)S(1)}, bf16[8,1024]{1,0:T(8,128)(2,1)S(1)}, u32[]{:S(2)}, u32[]{:S(2)}) collective-permute-start(bf16[8,1024]{1,0:T(8,128)(2,1)S(1)} %get-tuple-element.63), channel_id=1, source_target_pairs={{0,64},{32,96},{64,0},{96,32},{1,65},{33,97},{65,1},{97,33},{2,66}... | collective-permute-start | bytes 49160 | tf_op jit(solution)/shard_map/ppermute | solution.py:964
  79.2 0.0 collective-permute-start.8
  79.2 5.9 %collective-permute-done.7 = bf16[8,1024]{1,0:T(8,128)(2,1)S(1)} collective-permute-done((bf16[8,1024]{1,0:T(8,128)(2,1)S(1)}, bf16[8,1024]{1,0:T(8,128)(2,1)S(1)}, u32[]{:S(2)}, u32[]{:S(2)}) %collective-permute-start.7) | collective-permute-done | bytes 16416 | tf_op jit(solution)/shard_map/ppermute | solution.py:964
  85.1 0.0 collective-permute-done.8
  85.1 0.0 collective-permute-done.6.low_ref
  85.1 0.6 add_add_fusion
  85.8 0.0 collective-permute-done.9.inner_ref
  85.8 0.0 collective-permute-done.10.outer_ref
  85.8 1.1 %shard_map.100 = (bf16[256,1024]{1,0:T(8,128)(2,1)}, bf16[256,1024]{1,0:T(8,128)(2,1)}) custom-call(bf16[256,1024]{1,0:T(8,128)(2,1)S(1)} %get-tuple-element.66.dk_ref, bf16[256,1024]{1,0:T(8,128)(2,1)S(1)} %get-tuple-element.67.dv_ref, bf16[128,1024]{1,0:T(8,128)(2,1)S(1)} %collective-permute-done.9.inner_ref, ...), custom_call_target="tpu_custom_call" | custom-call | flops 4194304 | bytes 1048576 | tf_op jit(solution)/shard_map/pallas_call | solution.py:40
Async XLA Ops:
  0.6 18.9 %copy-start.2 = (bf16[1,256,1024]{2,1,0:T(8,128)(2,1)S(1)}, bf16[1,256,1024]{2,1,0:T(8,128)(2,1)}, u32[]{:S(2)}) copy-start(bf16[1,256,1024]{2,1,0:T(8,128)(2,1)} %param.9) | copy-start | bytes 1572868
  0.6 19.0 %copy-start = (bf16[1,256,1024]{2,1,0:T(8,128)(2,1)S(1)}, bf16[1,256,1024]{2,1,0:T(8,128)(2,1)}, u32[]{:S(2)}) copy-start(bf16[1,256,1024]{2,1,0:T(8,128)(2,1)} %param.6) | copy-start | bytes 1572868
  0.7 19.0 %copy-start.1 = (bf16[1,256,1024]{2,1,0:T(8,128)(2,1)S(1)}, bf16[1,256,1024]{2,1,0:T(8,128)(2,1)}, u32[]{:S(2)}) copy-start(bf16[1,256,1024]{2,1,0:T(8,128)(2,1)} %param.7) | copy-start | bytes 1572868
  0.7 19.0 %copy-start.3 = (bf16[1,256,1024]{2,1,0:T(8,128)(2,1)S(1)}, bf16[1,256,1024]{2,1,0:T(8,128)(2,1)}, u32[]{:S(2)}) copy-start(bf16[1,256,1024]{2,1,0:T(8,128)(2,1)} %param.5) | copy-start | bytes 1572868
  2.8 4.2 %collective-permute-start.2 = (bf16[24,1024]{1,0:T(8,128)(2,1)S(1)}, bf16[24,1024]{1,0:T(8,128)(2,1)S(1)}, u32[]{:S(2)}, u32[]{:S(2)}) collective-permute-start(bf16[24,1024]{1,0:T(8,128)(2,1)S(1)} %get-tuple-element.43.own_ref), channel_id=1, source_target_pairs={{0,1},{1,0},{2,3},{3,2},{4,5},{5,4},{6,7},{7,6},{8,9},{9,8},{10,11... | collective-permute-start | bytes 147464 | tf_op jit(solution)/shard_map/ppermute | solution.py:964
  7.9 23.6 %all-to-all-start = ((bf16[16,16,1024]{2,1,0:T(8,128)(2,1)}), bf16[16,16,1024]{2,1,0:T(8,128)(2,1)S(1)}, u32[]{:S(2)}, u32[]{:S(2)}) async-start(bf16[16,16,1024]{2,1,0:T(8,128)(2,1)} %bitcast.29), calls=%async_computation | async-start | bytes 1048576 | tf_op jit(solution)/shard_map/all_to_all | solution.py:984
  16.0 8.7 %collective-permute-start = (bf16[128,1024]{1,0:T(8,128)(2,1)}, bf16[128,1024]{1,0:T(8,128)(2,1)S(1)}, u32[]{:S(2)}, u32[]{:S(2)}) collective-permute-start(bf16[128,1024]{1,0:T(8,128)(2,1)} %get-tuple-element.39), channel_id=1, source_target_pairs={{0,1},{1,0},{2,3},{3,2},{4,5},{5,4},{6,7},{7,6},{8,9},{9,8},{10,11... | collective-permute-start | bytes 786440 | tf_op jit(solution)/shard_map/ppermute | solution.py:964
  17.4 11.0 %collective-permute-start.1 = (bf16[128,1024]{1,0:T(8,128)(2,1)}, bf16[128,1024]{1,0:T(8,128)(2,1)S(1)}, u32[]{:S(2)}, u32[]{:S(2)}) collective-permute-start(bf16[128,1024]{1,0:T(8,128)(2,1)} %get-tuple-element.40), channel_id=1, source_target_pairs={{1,2},{2,1},{3,4},{4,3},{5,6},{6,5},{7,8},{8,7},{9,10},{10,9},{11,... | collective-permute-start | bytes 786440 | tf_op jit(solution)/shard_map/ppermute | solution.py:973
  19.5 18.3 %collective-permute-start.4 = (bf16[256,1024]{1,0:T(8,128)(2,1)S(1)}, bf16[256,1024]{1,0:T(8,128)(2,1)S(1)}, u32[]{:S(2)}, u32[]{:S(2)}) collective-permute-start(bf16[256,1024]{1,0:T(8,128)(2,1)S(1)} %bitcast.21), channel_id=1, source_target_pairs={{0,32},{32,0},{64,96},{96,64},{1,33},{33,1},{65,97},{97,65},{2,34}... | collective-permute-start | bytes 1572872 | tf_op jit(solution)/shard_map/ppermute | solution.py:964
  24.6 6.8 %copy-start.4 = (bf16[128,1024]{1,0:T(8,128)(2,1)}, bf16[128,1024]{1,0:T(8,128)(2,1)S(1)}, u32[]{:S(2)}) copy-start(bf16[128,1024]{1,0:T(8,128)(2,1)S(1)} %collective-permute-done.inner_ref.inner_hbm) | copy-start | bytes 786436
  30.7 0.7 copy-start.5
  37.7 1.6 %collective-permute-start.3 = (bf16[256,512]{1,0:T(8,128)(2,1)S(1)}, bf16[256,512]{1,0:T(8,128)(2,1)S(1)}, u32[]{:S(2)}, u32[]{:S(2)}) collective-permute-start(bf16[256,512]{1,0:T(8,128)(2,1)S(1)} %get-tuple-element.49), channel_id=1, source_target_pairs={{0,32},{32,0},{64,96},{96,64},{1,33},{33,1},{65,97},{97,65},{2,34}... | collective-permute-start | bytes 786440 | tf_op jit(solution)/shard_map/ppermute | solution.py:964
  41.3 26.7 %all-to-all-start.1 = ((bf16[16,40,1024]{2,1,0:T(8,128)(2,1)}), bf16[16,40,1024]{2,1,0:T(8,128)(2,1)S(1)}, u32[]{:S(2)}, u32[]{:S(2)}) async-start(bf16[16,40,1024]{2,1,0:T(8,128)(2,1)} %bitcast.7), calls=%async_computation.1 | async-start | bytes 2621440 | tf_op jit(solution)/shard_map/all_to_all | solution.py:984
  48.2 7.2 %collective-permute-start.5 = (bf16[16,1024]{1,0:T(8,128)(2,1)S(1)}, bf16[16,1024]{1,0:T(8,128)(2,1)S(1)}, u32[]{:S(2)}, u32[]{:S(2)}) collective-permute-start(bf16[16,1024]{1,0:T(8,128)(2,1)S(1)} %get-tuple-element.57), channel_id=1, source_target_pairs={{0,2},{1,3},{2,0},{3,1},{4,6},{5,7},{6,4},{7,5},{8,10},{9,11},{10,... | collective-permute-start | bytes 98312 | tf_op jit(solution)/shard_map/ppermute | solution.py:964
  69.4 15.7 %collective-permute-start.6 = (bf16[24,1024]{1,0:T(8,128)(2,1)S(1)}, bf16[24,1024]{1,0:T(8,128)(2,1)S(1)}, u32[]{:S(2)}, u32[]{:S(2)}) collective-permute-start(bf16[24,1024]{1,0:T(8,128)(2,1)S(1)} %get-tuple-element.62), channel_id=1, source_target_pairs={{0,1},{1,0},{2,3},{3,2},{4,5},{5,4},{6,7},{7,6},{8,9},{9,8},{10,11... | collective-permute-start | bytes 147464 | tf_op jit(solution)/shard_map/ppermute | solution.py:964
  71.6 14.2 %collective-permute-start.9 = (bf16[128,1024]{1,0:T(8,128)(2,1)S(1)}, bf16[128,1024]{1,0:T(8,128)(2,1)S(1)}, u32[]{:S(2)}, u32[]{:S(2)}) collective-permute-start(bf16[128,1024]{1,0:T(8,128)(2,1)S(1)} %get-tuple-element.68), channel_id=1, source_target_pairs={{0,1},{1,0},{2,3},{3,2},{4,5},{5,4},{6,7},{7,6},{8,9},{9,8},{10,11... | collective-permute-start | bytes 786440 | tf_op jit(solution)/shard_map/ppermute | solution.py:964
  71.7 14.1 %collective-permute-start.10 = (bf16[128,1024]{1,0:T(8,128)(2,1)S(1)}, bf16[128,1024]{1,0:T(8,128)(2,1)S(1)}, u32[]{:S(2)}, u32[]{:S(2)}) collective-permute-start(bf16[128,1024]{1,0:T(8,128)(2,1)S(1)} %get-tuple-element.69), channel_id=1, source_target_pairs={{1,2},{2,1},{3,4},{4,3},{5,6},{6,5},{7,8},{8,7},{9,10},{10,9},{11,... | collective-permute-start | bytes 786440 | tf_op jit(solution)/shard_map/ppermute | solution.py:973
  76.4 8.7 %collective-permute-start.7 = (bf16[8,1024]{1,0:T(8,128)(2,1)S(1)}, bf16[8,1024]{1,0:T(8,128)(2,1)S(1)}, u32[]{:S(2)}, u32[]{:S(2)}) collective-permute-start(bf16[8,1024]{1,0:T(8,128)(2,1)S(1)} %get-tuple-element.63), channel_id=1, source_target_pairs={{0,64},{32,96},{64,0},{96,32},{1,65},{33,97},{65,1},{97,33},{2,66}... | collective-permute-start | bytes 49160 | tf_op jit(solution)/shard_map/ppermute | solution.py:964
  79.2 5.9 %collective-permute-start.8 = (bf16[8,1024]{1,0:T(8,128)(2,1)S(1)}, bf16[8,1024]{1,0:T(8,128)(2,1)S(1)}, u32[]{:S(2)}, u32[]{:S(2)}) collective-permute-start(bf16[8,1024]{1,0:T(8,128)(2,1)S(1)} %get-tuple-element.64), channel_id=1, source_target_pairs={{0,65},{1,64},{2,67},{3,66},{4,69},{5,68},{6,71},{7,70},{8,73},{9,... | collective-permute-start | bytes 49160 | tf_op jit(solution)/shard_map/ppermute | solution.py:979
